TPU v7x, 8 devices: a whole 2x2x1 slice. The times are simulated.
8 devices in a mesh: dp: 1 (over z), tp: 2 (over y), ctx: 4 (over x, core).
Axes of the slice: x: 2, y: 2, z: 1, core: 2. Of those that a mesh axis runs over, the one named last changes fastest.
Arguments:
- hidden: bfloat16 [512, 4096], P(('dp', 'ctx'))
- w_q: bfloat16 [4096, 4096], P(None, 'tp')
- w_k: bfloat16 [4096, 4096], P(None, 'tp')
- w_v: bfloat16 [4096, 4096], P(None, 'tp')
- w_o: bfloat16 [4096, 4096], P('tp')
- k_prefix: bfloat16 [4096, 32, 128], P(('dp', 'ctx'), 'tp')
- v_prefix: bfloat16 [4096, 32, 128], P(('dp', 'ctx'), 'tp')
- k_suffix: bfloat16 [512, 64, 32, 128], P(('dp', 'ctx'), None, 'tp')
- v_suffix: bfloat16 [512, 64, 32, 128], P(('dp', 'ctx'), None, 'tp')
- seq_lens: int32 [512], P(('dp', 'ctx'))
Outputs:
- output: bfloat16 [512, 4096], P(('dp', 'ctx'))
All inputs are finite; a program needn't handle non-finite values.
Results may differ from a plain program's by a relative error of at most 0.00420516.
Values are sent between devices in bfloat16 or wider.
A program may use at most 1 GiB of HBM per device.

v0:
```python
import jax
import jax.numpy as jnp
from jax import lax
from jax.sharding import PartitionSpec as P, NamedSharding


def solution(mesh):
    ctx_size = mesh.shape['ctx']
    row_axes = ('dp', 'ctx')

    def device_step(hidden, w_q, w_k, w_v, w_o, k_prefix, v_prefix, k_suffix, v_suffix, seq_lens):
        seq_count = hidden.shape[0]
        kv_local = k_prefix.shape[1]
        head_dim = k_prefix.shape[2]
        group_size = w_q.shape[1] // (kv_local * head_dim)
        score_scale = head_dim ** -0.5
        q_local = jnp.dot(hidden, w_q, preferred_element_type=jnp.float32).astype(jnp.bfloat16)
        q_local = q_local.reshape(seq_count, kv_local, group_size, head_dim)
        k_new = jnp.dot(hidden, w_k, preferred_element_type=jnp.float32).astype(jnp.bfloat16).reshape(seq_count, kv_local, head_dim)
        v_new = jnp.dot(hidden, w_v, preferred_element_type=jnp.float32).astype(jnp.bfloat16).reshape(seq_count, kv_local, head_dim)
        q_every = lax.all_gather(q_local, 'ctx', axis=0, tiled=True)
        s_pre = jnp.einsum('bkgd,pkd->bkgp', q_every, k_prefix, preferred_element_type=jnp.float32) * score_scale
        m_pre = jnp.max(s_pre, axis=-1)
        e_pre = jnp.exp(s_pre - m_pre[..., None])
        l_pre = jnp.sum(e_pre, axis=-1)
        o_pre = jnp.einsum('bkgp,pkd->bkgd', e_pre.astype(jnp.bfloat16), v_prefix, preferred_element_type=jnp.float32)
        partial_state = jnp.concatenate([o_pre / l_pre[..., None], (m_pre + jnp.log(l_pre))[..., None]], axis=-1)
        returned = lax.all_to_all(partial_state, 'ctx', 0, 0, tiled=True)
        returned = returned.reshape(ctx_size, seq_count, kv_local, group_size, head_dim + 1)
        o_parts = returned[..., :head_dim]
        lse_parts = returned[..., head_dim]
        slot_ids = jnp.arange(k_suffix.shape[1])
        in_cache = (slot_ids[None, :] < seq_lens[:, None])[:, None, None, :]
        s_cache = jnp.einsum('bkgd,bskd->bkgs', q_local, k_suffix, preferred_element_type=jnp.float32) * score_scale
        s_cache = jnp.where(in_cache, s_cache, -jnp.inf)
        s_self = jnp.einsum('clhe,cle->clh', q_local, k_new, preferred_element_type=jnp.float32) * score_scale
        m_suf = jnp.maximum(jnp.max(s_cache, axis=-1), s_self)
        e_cache = jnp.exp(s_cache - m_suf[..., None])
        e_self = jnp.exp(s_self - m_suf)
        l_suf = jnp.sum(e_cache, axis=-1) + e_self
        o_suf = jnp.einsum('bkgs,bskd->bkgd', e_cache.astype(jnp.bfloat16), v_suffix, preferred_element_type=jnp.float32)
        o_suf = (o_suf + e_self[..., None] * v_new[:, :, None, :].astype(jnp.float32)) / l_suf[..., None]
        lse_suf = m_suf + jnp.log(l_suf)
        lse_max = jnp.maximum(jnp.max(lse_parts, axis=0), lse_suf)
        w_parts = jnp.exp(lse_parts - lse_max)
        w_suf = jnp.exp(lse_suf - lse_max)
        merged = jnp.sum(w_parts[..., None] * o_parts, axis=0) + w_suf[..., None] * o_suf
        merged = merged / (jnp.sum(w_parts, axis=0) + w_suf)[..., None]
        attn_out = merged.astype(jnp.bfloat16).reshape(seq_count, kv_local * group_size * head_dim)
        proj_part = jnp.dot(attn_out, w_o, preferred_element_type=jnp.float32)
        out_hidden = hidden.astype(jnp.float32) + lax.psum(proj_part, 'tp')
        return out_hidden.astype(jnp.bfloat16)

    spec_in = (P(row_axes, None), P(None, 'tp'), P(None, 'tp'), P(None, 'tp'), P('tp', None), P(row_axes, 'tp', None), P(row_axes, 'tp', None), P(row_axes, None, 'tp', None), P(row_axes, None, 'tp', None), P(row_axes))
    return jax.shard_map(device_step, mesh=mesh, in_specs=spec_in, out_specs=P(row_axes, None), check_vma=False)
```

profile of v0, /device:TPU:0, one launch (start us, length us, event | category | flops | bytes accessed | tf_op | source)
XLA Modules:
  0.0 307.8 jit_solution(8129585404020616088)
XLA Ops:
  6.5 0.0 all-gather.2.cloned.1.call-start
  6.5 8.4 %convolution_convert_fusion.2 = bf16[128,2048]{1,0:T(8,128)(2,1)S(1)} fusion(bf16[128,4096]{1,0:T(8,128)(2,1)} %param.10, bf16[4096,2048]{1,0:T(8,128)(2,1)} %param.11), kind=kOutput, calls=%fused_computation.22 | convolution fusion | flops 2147745792 | bytes 18350080 | tf_op jit(solution)/shard_map/dot_general | solution.py:17
  15.0 0.1 copy.58
  15.1 0.9 copy.34
  16.0 0.0 all-gather.2.cloned.1.call-update
  16.1 1.1 reshape.184
  17.1 0.0 copy-start
  17.1 22.9 %fusion.1 = f32[128,16,1,64]{3,2,1,0:T(1,128)} fusion(bf16[128,16,128,1]{2,3,1,0:T(2,128)(2,1)S(1)} %reshape.184, bf16[128,64,16,128]{3,2,1,0:T(8,128)(2,1)} %param.17), kind=kOutput, calls=%fused_computation.4 | convolution fusion | flops 33554432 | bytes 34603008 | tf_op jit(solution)/shard_map/bkgd,bskd->bkgs/dot_general | solution.py:34
  40.0 0.0 copy-start.1
  40.0 2.3 copy.42
  42.3 0.0 copy-done
  42.3 8.1 %fusion.16 = bf16[16,8,16,128]{3,1,2,0:T(8,128)(2,1)S(1)} fusion(bf16[128,4096]{1,0:T(8,128)(2,1)S(1)} %copy-done, bf16[4096,2048]{1,0:T(8,128)(2,1)} %param.12), kind=kOutput, calls=%fused_computation.25 | convolution fusion | flops 2147745792 | bytes 18350080 | tf_op jit(solution)/shard_map/dot_general | solution.py:19
  50.4 0.1 copy.60
  50.5 0.4 fusion.17
  50.9 0.1 copy.46
  50.9 0.0 copy-done.1
  51.0 0.1 fusion.25
  51.1 0.1 fusion.26
  51.2 4.5 %copy.56 = f32[128,16,64]{1,2,0:T(8,128)} copy(f32[128,16,64]{0,2,1:T(8,128)S(1)} %get-tuple-element.10) | data formatting | bytes 1048576
  55.7 0.0 all-gather.2.cloned.1.call-done
  55.7 15.7 %bitcast_reduce_fusion = (f32[512,16]{0,1:T(8,128)S(1)}, f32[16,512,1024]{2,1,0:T(8,128)}) fusion(bf16[1024,16,128]{2,1,0:T(8,128)(2,1)} %param.15, bf16[512,16,1,128]{3,0,1,2:T(8,128)(2,1)} %all-gather.2.cloned.1.call-done), kind=kOutput, calls=%fused_computation.2 | convolution fusion | flops 2164252672 | bytes 39878656 | tf_op jit(solution)/shard_map/bkgd,pkd->bkgp/dot_general | solution.py:22
  71.4 0.0 copy-start.2
  71.4 14.4 %fusion.3 = f32[512,16]{0,1:T(8,128)S(1)} fusion(f32[16,512,1024]{2,1,0:T(8,128)} %get-tuple-element.13, f32[512,16]{0,1:T(8,128)S(1)} %get-tuple-element.12), kind=kLoop, calls=%fused_computation.6 | loop fusion | flops 25157632 | bytes 33619968 | tf_op jit(solution)/shard_map/reduce_sum | solution.py:25
  85.9 0.0 copy-done.2
  85.9 13.4 %bitcast_divide_fusion = f32[512,16,1,128]{0,3,1,2:T(8,128)S(1)} fusion(f32[512,16]{0,1:T(8,128)S(1)} %fusion.3, bf16[1024,16,128]{2,1,0:T(8,128)(2,1)S(1)} %copy-done.2, f32[16,512,1024]{2,1,0:T(8,128)} %get-tuple-element.13, f32[512,16]{0,1:T(8,128)S(1)} %get-tuple-element.12), kind=kOutput, calls=%fused_computation.15 | convolution fusion | flops 2173698048 | bytes 42008576 | tf_op jit(solution)/shard_map/bkgp,pkd->bkgd/dot_general | solution.py:26
  99.3 2.6 pad_maximum_fusion
  101.8 8.8 %copy.37 = f32[512,16,1,129]{3,1,2,0:T(8,128)} copy(f32[512,16,1,129]{0,3,1,2:T(8,128)} %pad_maximum_fusion) | data formatting | bytes 8454144 | tf_op jit(solution)/shard_map/concatenate | solution.py:27
  110.6 5.7 %all-to-all-start = ((f32[512,16,1,129]{3,1,2,0:T(8,128)}), f32[512,16,1,129]{3,1,2,0:T(8,128)}, u32[]{:S(2)}, u32[]{:S(2)}) async-start(f32[512,16,1,129]{3,1,2,0:T(8,128)} %copy.37), calls=%async_computation | async-start | bytes 16777216 | tf_op jit(solution)/shard_map/all_to_all | solution.py:28
  116.3 0.0 all-reduce.2.cloned.1.call-start
  116.3 22.1 %multiply_reduce_fusion = f32[128,16,128]{2,1,0:T(8,128)S(1)} fusion(f32[128,16,64]{1,2,0:T(8,128)} %copy.56, bf16[128,64,16,128]{3,2,1,0:T(8,128)(2,1)} %param.18), kind=kLoop, calls=%fused_computation | loop fusion | flops 50069504 | bytes 35127296
  138.4 0.4 copy.53
  138.8 9.1 %fusion.14 = f32[128,2048]{1,0:T(8,128)} fusion(bf16[128,4096]{1,0:T(8,128)(2,1)S(1)} %copy-done, bf16[4096,2048]{1,0:T(8,128)(2,1)} %param.13), kind=kOutput, calls=%fused_computation.20 | convolution fusion | flops 2148007936 | bytes 18874368 | tf_op jit(solution)/shard_map/dot_general | solution.py:20
  147.9 1.6 copy.55
  149.5 60.7 %all-to-all-done = f32[512,16,1,129]{3,1,2,0:T(8,128)} async-done(((f32[512,16,1,129]{3,1,2,0:T(8,128)}), f32[512,16,1,129]{3,1,2,0:T(8,128)}, u32[]{:S(2)}, u32[]{:S(2)}) %all-to-all-start) | async-done | bytes 4227104 | tf_op jit(solution)/shard_map/all_to_all | solution.py:28
  210.2 12.5 %copy.38 = f32[512,16,1,129]{0,2,3,1:T(1,128)} copy(f32[512,16,1,129]{3,1,2,0:T(8,128)} %all-to-all-done) | data formatting | bytes 8454144 | tf_op jit(solution)/shard_map/all_to_all | solution.py:28
  222.6 0.8 slice_reduce_fusion
  223.4 0.8 fusion.28
  224.2 0.8 exponential_bitcast_fusion
  225.0 5.1 %fusion.10 = f32[128,16,128]{0,2,1:T(8,128)S(1)} fusion(f32[4,128,16,1,129]{1,0,3,4,2:T(4,128)} %bitcast.82, f32[4,128,16]{1,0,2:T(4,128)S(1)} %exponential_bitcast_fusion), kind=kLoop, calls=%fused_computation.14 | loop fusion | flops 1835008 | bytes 5275648 | tf_op jit(solution)/shard_map/reduce_sum | solution.py:47
  230.2 0.4 divide_convert_fusion
  230.6 9.5 %fusion.32 = f32[128,4096]{1,0:T(8,128)} fusion(bf16[128,2048]{0,1:T(8,128)(2,1)S(1)} %bitcast.87, bf16[2048,4096]{1,0:T(8,128)(2,1)} %param.14), kind=kOutput, calls=%fused_computation.50 | convolution fusion | flops 2147483648 | bytes 19398656 | tf_op jit(solution)/shard_map/dot_general | solution.py:50
  240.0 0.0 all-reduce.2.cloned.1.call-update
  240.1 58.1 %all-reduce.2.cloned.1.call-done = f32[128,4096]{1,0:T(8,128)} async-done(((f32[128,4096]{1,0:T(8,128)}), f32[128,4096]{1,0:T(8,128)}) %all-reduce.2.cloned.1.call-update) | async-done | bytes 2097168 | tf_op jit(solution)/shard_map/psum | solution.py:51
  298.2 2.8 add_convert_fusion
  (6 shorter events, 0.1 us)
Async XLA Ops:
  6.5 49.1 %all-gather.2.cloned.1.call-start = ((), (), s32[]{:S(2)}) async-start(), calls=%async_computation.1 | async-start | bytes 2621440 | tf_op jit(solution)/shard_map/all_gather | solution.py:21
  17.1 25.2 %copy-start = (bf16[128,4096]{1,0:T(8,128)(2,1)S(1)}, bf16[128,4096]{1,0:T(8,128)(2,1)}, u32[]{:S(2)}) copy-start(bf16[128,4096]{1,0:T(8,128)(2,1)} %param.10) | copy-start | bytes 3145732
  40.0 10.9 %copy-start.1 = (s32[128]{0:T(128)S(1)}, s32[128]{0:T(128)}, u32[]{:S(2)}) copy-start(s32[128]{0:T(128)} %param.19) | copy-start | bytes 1540
  71.4 14.5 %copy-start.2 = (bf16[1024,16,128]{2,1,0:T(8,128)(2,1)S(1)}, bf16[1024,16,128]{2,1,0:T(8,128)(2,1)}, u32[]{:S(2)}) copy-start(bf16[1024,16,128]{2,1,0:T(8,128)(2,1)} %param.16) | copy-start | bytes 12582916
  110.6 99.5 %all-to-all-start = ((f32[512,16,1,129]{3,1,2,0:T(8,128)}), f32[512,16,1,129]{3,1,2,0:T(8,128)}, u32[]{:S(2)}, u32[]{:S(2)}) async-start(f32[512,16,1,129]{3,1,2,0:T(8,128)} %copy.37), calls=%async_computation | async-start | bytes 16777216 | tf_op jit(solution)/shard_map/all_to_all | solution.py:28
  116.3 181.9 %all-reduce.2.cloned.1.call-start = ((), (), s32[]{:S(2)}) async-start(), calls=%async_computation.2 | async-start | bytes 4194304 | tf_op jit(solution)/shard_map/psum | solution.py:51
Sparse Core Ops, SparseCore 0:
  16.2 22.3 all-gather.1
  240.2 57.9 all-reduce.1
where the time goes:
time: 309 us; the launch traced here: 308 us
  waiting for transfers between devices  119 us (39%)
  matrix products  87 us (28%)
  other arithmetic  50.3 us (16%)
  local copies, waits for them, and re-layouts  32.3 us (10%)
  between operations  13.6 us (4%)
  starting transfers between devices  5.7 us (2%)
    all_to_all x1, waiting for transfers between devices, device_step(): returned = lax.all_to_all(partial_state, 'ctx', 0, 0, tiled=True)  60.7 us
    psum x1, waiting for transfers between devices, device_step(): out_hidden = hidden.astype(jnp.float32) + lax.psum(proj_part, 'tp')  58.1 us
    dot_general x1, matrix products, device_step(): jnp.einsum('bkgd,bskd->bkgs', q_local, k_suffix, preferred_element_type=j...  22.9 us
    unnamed x3, other arithmetic  22.5 us
    dot_general x1, matrix products, device_step(): jnp.einsum('bkgd,pkd->bkgp', q_every, k_prefix, preferred_element_type=jn...  15.7 us
    reduce_sum x1, other arithmetic, device_step(): l_pre = jnp.sum(e_pre, axis=-1)  14.4 us
    dot_general x1, matrix products, device_step(): jnp.einsum('bkgp,pkd->bkgd', e_pre.astype(jnp.bfloat16), v_prefix, prefer...  13.4 us
    all_to_all x1, local copies, waits for them, and re-layouts, device_step(): returned = lax.all_to_all(partial_state, 'ctx', 0, 0, tiled=True)  12.5 us
  transfers between devices with their start and end apart: 3, of which 2 were waited for; matrix products, arithmetic and copies ran while one was open for 24% of the time, Pallas kernels for 0%

commit v1 on v0

v1 whole, which is shorter than its diff:
```python
import functools

import jax
import jax.numpy as jnp
from jax import lax
from jax.experimental import pallas as pl
from jax.experimental.pallas import tpu as pltpu
from jax.sharding import PartitionSpec as P

F32 = jnp.float32
BF16 = jnp.bfloat16
VM = pltpu.VMEM
LOG2E = 1.4426950408889634
BATCH = 8
SLOTS = 16
RING = 8
LIMIT = 56 * 2**20


def _cost(flops, nbytes):
    return pl.CostEstimate(flops=int(flops), bytes_accessed=int(nbytes), transcendentals=0)


def _dot(a, b, dims=(((1,), (0,)), ((), ()))):
    return lax.dot_general(a, b, dims, preferred_element_type=F32)


NT = (((1,), (1,)), ((), ()))


def _proj_kernel(x_ref, *refs):
    half = len(refs) // 2
    for w_ref, o_ref in zip(refs[:half], refs[half:]):
        y = _dot(x_ref[...], w_ref[...]).astype(BF16)
        for h in range(o_ref.shape[0]):
            o_ref[h] = y[:, h * 128:(h + 1) * 128]


def _project(x, ws, tile):
    rows, depth = x.shape
    cols = ws[0].shape[1]
    heads = cols // 128
    th = tile // 128
    n = len(ws)
    return pl.pallas_call(
        _proj_kernel,
        grid=(cols // tile,),
        in_specs=[pl.BlockSpec((rows, depth), lambda i: (0, 0))]
        + [pl.BlockSpec((depth, tile), lambda i: (0, i))] * n,
        out_specs=[pl.BlockSpec((th, rows, 128), lambda i: (i, 0, 0))] * n,
        out_shape=[jax.ShapeDtypeStruct((heads, rows, 128), BF16)] * n,
        compiler_params=pltpu.CompilerParams(vmem_limit_bytes=LIMIT),
        cost_estimate=_cost(2 * rows * depth * cols * n, 2 * depth * cols * n),
    )(x, *ws)


def _relayout_kernel(k_ref, v_ref, ko_ref, vo_ref):
    def body(i, c):
        at = pl.multiple_of(i * 16, 16)
        ko_ref[:, pl.ds(at, 16), :] = jnp.swapaxes(k_ref[pl.ds(i * 16, 16)], 0, 1)
        vo_ref[:, pl.ds(at, 16), :] = jnp.swapaxes(v_ref[pl.ds(i * 16, 16)], 0, 1)
        return c
    lax.fori_loop(0, k_ref.shape[0] // 16, body, 0, unroll=2)


def _relayout(k, v):
    n, heads, d = k.shape
    t = 128
    return pl.pallas_call(
        _relayout_kernel,
        grid=(n // t,),
        in_specs=[pl.BlockSpec((t, heads, d), lambda i: (i, 0, 0))] * 2,
        out_specs=[pl.BlockSpec((heads, t, d), lambda i: (0, i, 0))] * 2,
        out_shape=[jax.ShapeDtypeStruct((heads, n, d), BF16)] * 2,
        compiler_params=pltpu.CompilerParams(vmem_limit_bytes=LIMIT),
        cost_estimate=_cost(2e9, 8 * n * heads * d),
    )(k, v)


def _prefix_kernel(scale, q0_ref, q1_ref, k_ref, v_ref, o0_ref, o1_ref, l0_ref, l1_ref):
    h = pl.program_id(0)
    lane = lax.broadcasted_iota(jnp.int32, (128, 128), 1)

    @pl.when(h == 0)
    def _():
        l0_ref[...] = jnp.zeros_like(l0_ref)
        l1_ref[...] = jnp.zeros_like(l1_ref)

    k = k_ref[0]
    v = v_ref[0]
    for q_ref, o_ref, l_ref in ((q0_ref, o0_ref, l0_ref), (q1_ref, o1_ref, l1_ref)):
        s = _dot(q_ref[0], k, NT)
        m = jnp.max(s, axis=1, keepdims=True) * scale
        e = jnp.exp2(s * scale - m)
        l = jnp.sum(e, axis=1, keepdims=True)
        o = _dot(e.astype(BF16), v)
        o_ref[0] = o / l
        l_ref[...] = jnp.where(lane == h, m + jnp.log2(l), l_ref[...])


def _prefix(q0, q1, k, v, scale):
    heads, rows, d = q0.shape
    n = k.shape[1]
    head = lambda i: (i, 0, 0)
    return pl.pallas_call(
        functools.partial(_prefix_kernel, scale),
        grid=(heads,),
        in_specs=[pl.BlockSpec((1, rows, d), head)] * 2 + [pl.BlockSpec((1, n, d), head)] * 2,
        out_specs=[pl.BlockSpec((1, rows, d), head)] * 2 + [pl.BlockSpec((rows, 128), lambda i: (0, 0))] * 2,
        out_shape=[jax.ShapeDtypeStruct((heads, rows, d), F32)] * 2
        + [jax.ShapeDtypeStruct((rows, 128), F32)] * 2,
        compiler_params=pltpu.CompilerParams(vmem_limit_bytes=LIMIT),
        cost_estimate=_cost(8 * heads * rows * n * d, 4 * heads * n * d),
    )(q0, q1, k, v)


def _merge_kernel(o0_ref, l0_ref, o1_ref, l1_ref, o_ref, l_ref):
    l0, l1 = l0_ref[...], l1_ref[...]
    m = jnp.maximum(l0, l1)
    w0, w1 = jnp.exp2(l0 - m), jnp.exp2(l1 - m)
    t = w0 + w1
    l_ref[...] = m + jnp.log2(t)
    w0, w1 = w0 / t, w1 / t
    for h in range(o0_ref.shape[0]):
        o_ref[h] = (w0[:, h:h + 1] * o0_ref[h] + w1[:, h:h + 1] * o1_ref[h]).astype(BF16)


def _merge(o0, l0, o1, l1):
    return pl.pallas_call(
        _merge_kernel,
        in_specs=[pl.BlockSpec(memory_space=VM)] * 4,
        out_specs=[pl.BlockSpec(memory_space=VM)] * 2,
        out_shape=[jax.ShapeDtypeStruct(o0.shape, BF16), jax.ShapeDtypeStruct(l0.shape, F32)],
        compiler_params=pltpu.CompilerParams(vmem_limit_bytes=LIMIT),
        cost_estimate=_cost(1e9, 10 * o0.size),
    )(o0, l0, o1, l1)


def _suffix_kernel(scale, lens, q_ref, kn_ref, vn_ref, k_hbm, v_hbm, o_ref, lse_ref,
                   items, qb, acc, m_s, l_s, kbuf, vbuf, sbuf, ksem, vsem):
    heads, rows, d = q_ref.shape
    per = k_hbm.shape[0] // rows
    wide = SLOTS * heads
    dummy = rows * per

    for g in range(BATCH):
        items[g] = dummy

    def listing(b, t):
        for j in range(per):
            items[BATCH + t + j] = b * per + j
        return t + (lens[b] + SLOTS - 1) // SLOTS
    total = lax.fori_loop(0, rows, listing, 0)
    for g in range(2 * BATCH):
        items[BATCH + total + g] = dummy
    batches = (total + BATCH - 1) // BATCH

    def fetch(i):
        slot = lax.rem(i, RING)
        for g in range(BATCH):
            it = jnp.minimum(items[BATCH + i * BATCH + g], dummy - 1)
            pltpu.make_async_copy(k_hbm.at[it], kbuf.at[slot, g], ksem.at[slot]).start()
            pltpu.make_async_copy(v_hbm.at[it], vbuf.at[slot, g], vsem.at[slot]).start()

    def prime(i, c):
        fetch(i)
        return c
    lax.fori_loop(0, jnp.minimum(batches, RING - 1), prime, 0)

    for c in range(rows // 16):
        q = jnp.swapaxes(q_ref[:, c * 16:c * 16 + 16, :], 0, 1)
        kn = jnp.swapaxes(kn_ref[:, c * 16:c * 16 + 16, :], 0, 1)
        vn = jnp.swapaxes(vn_ref[:, c * 16:c * 16 + 16, :], 0, 1)
        qb[c * 16:c * 16 + 16] = q
        s = jnp.sum(q.astype(F32) * kn.astype(F32), axis=-1, keepdims=True) * scale
        m_s[c * 16:c * 16 + 16] = jnp.broadcast_to(s, (16, heads, 128))
        l_s[c * 16:c * 16 + 16] = jnp.ones((16, heads, 128), F32)
        acc[c * 16:c * 16 + 16] = vn.astype(F32)

    row = lax.broadcasted_iota(jnp.int32, (heads, wide), 0)
    col = lax.broadcasted_iota(jnp.int32, (heads, wide), 1)
    slot_of = jnp.where(lax.rem(col, heads) == row, col // heads, 1 << 20)

    def step(i, c):
        slot = lax.rem(i, RING)
        last = lax.rem(i + RING - 1, RING)
        par = lax.rem(i, 2)

        @pl.when(i < batches)
        def _():
            pltpu.make_async_copy(k_hbm.at[pl.ds(0, BATCH)], kbuf.at[slot], ksem.at[slot]).wait()

        @pl.when(i > 0)
        def _():
            pltpu.make_async_copy(v_hbm.at[pl.ds(0, BATCH)], vbuf.at[last], vsem.at[last]).wait()

        for g in range(BATCH):
            it = items[BATCH + i * BATCH + g]
            b = it // per
            left = lens[jnp.minimum(b, rows - 1)] - lax.rem(it, per) * SLOTS
            s = _dot(qb[b], kbuf[slot, g], NT) * scale
            sbuf[par, g] = jnp.where(slot_of < left, s, -jnp.inf)

        parts = []
        for g in range(0, BATCH, 2):
            ps = []
            for u in range(2):
                s = sbuf[1 - par, g + u]
                m = jnp.max(s, axis=1, keepdims=True)
                p = jnp.exp2(s - m)
                parts.append([m, jnp.sum(p, axis=1, keepdims=True), None])
                ps.append(p.astype(BF16))
            o = _dot(jnp.concatenate(ps, axis=0),
                     jnp.concatenate([vbuf[last, g], vbuf[last, g + 1]], axis=1))
            parts[g][2] = o[:heads, :d]
            parts[g + 1][2] = o[heads:, d:]
        for g in range(BATCH):
            b = items[i * BATCH + g] // per
            m, l, o = parts[g]
            m_old = m_s[b]
            m_new = jnp.maximum(m_old, m)
            w_old = jnp.exp2(m_old - m_new)
            w = jnp.exp2(m - m_new)
            m_s[b] = m_new
            l_s[b] = l_s[b] * w_old + l * w
            acc[b] = acc[b] * w_old + o * w

        @pl.when(i + RING - 1 < batches)
        def _():
            fetch(i + RING - 1)
        return c

    lax.fori_loop(0, batches + 1, step, 0)

    lane = lax.broadcasted_iota(jnp.int32, (16, 128), 1)
    for c in range(rows // 16):
        l = l_s[c * 16:c * 16 + 16]
        o = acc[c * 16:c * 16 + 16] / l
        lse = m_s[c * 16:c * 16 + 16] + jnp.log2(l)
        o_ref[:, c * 16:c * 16 + 16, :] = jnp.swapaxes(o, 0, 1)
        lse = jnp.swapaxes(lse, 0, 1)
        out = jnp.zeros((16, 128), F32)
        for h in range(heads):
            out = jnp.where(lane == h, lse[h], out)
        lse_ref[c * 16:c * 16 + 16, :] = out


def _suffix(lens, q, kn, vn, k, v, scale):
    heads, rows, d = q.shape
    slots = k.shape[1]
    per = slots // SLOTS
    wide = SLOTS * heads
    k = k.reshape(rows * per, wide, d)
    v = v.reshape(rows * per, wide, d)
    return pl.pallas_call(
        functools.partial(_suffix_kernel, scale),
        in_specs=[pl.BlockSpec(memory_space=pltpu.SMEM)] + [pl.BlockSpec(memory_space=VM)] * 3
        + [pl.BlockSpec(memory_space=pl.ANY)] * 2,
        out_specs=[pl.BlockSpec(memory_space=VM)] * 2,
        out_shape=[jax.ShapeDtypeStruct((heads, rows, d), F32), jax.ShapeDtypeStruct((rows, 128), F32)],
        scratch_shapes=[
            pltpu.SMEM((rows * per + 4 * BATCH,), jnp.int32),
            VM((rows + 1, heads, d), BF16),
            VM((rows + 1, heads, d), F32),
            VM((rows + 1, heads, 128), F32),
            VM((rows + 1, heads, 128), F32),
            VM((RING, BATCH, wide, d), BF16),
            VM((RING, BATCH, wide, d), BF16),
            VM((2, BATCH, heads, wide), F32),
            pltpu.SemaphoreType.DMA((RING,)),
            pltpu.SemaphoreType.DMA((RING,)),
        ],
        compiler_params=pltpu.CompilerParams(vmem_limit_bytes=LIMIT),
        cost_estimate=_cost(2e10, 4 * k.size),
    )(lens, q, kn, vn, k, v)


def _merge4_kernel(*refs):
    o_refs, l_refs, att_ref = refs[0:8:2], refs[1:8:2], refs[8]
    ls = [r[...] for r in l_refs]
    m = functools.reduce(jnp.maximum, ls)
    ws = [jnp.exp2(l - m) for l in ls]
    t = functools.reduce(jnp.add, ws)
    ws = [w / t for w in ws]
    for h in range(o_refs[0].shape[0]):
        a = ws[0][:, h:h + 1] * o_refs[0][h].astype(F32)
        for w, r in zip(ws[1:], o_refs[1:]):
            a += w[:, h:h + 1] * r[h].astype(F32)
        att_ref[:, h * 128:(h + 1) * 128] = a.astype(BF16)


def _merge4(parts):
    heads, rows, d = parts[0][0].shape
    flat = [a for p in parts for a in p]
    return pl.pallas_call(
        _merge4_kernel,
        in_specs=[pl.BlockSpec(memory_space=VM)] * 8,
        out_specs=pl.BlockSpec(memory_space=VM),
        out_shape=jax.ShapeDtypeStruct((rows, heads * d), BF16),
        compiler_params=pltpu.CompilerParams(vmem_limit_bytes=LIMIT),
        cost_estimate=_cost(1e9, 20 * heads * rows * d),
    )(*flat)


def _send_kernel(at, a_ref, w_ref, o_ref):
    o_ref[...] = _dot(a_ref[...], w_ref[...]).astype(BF16)


def _keep_kernel(at, a_ref, w_ref, x_ref, o_ref):
    o_ref[...] = _dot(a_ref[...], w_ref[...]) + x_ref[...].astype(F32)


def _out_proj(att, w_o, x, first, cols, tile):
    rows, depth = att.shape
    in_specs = [pl.BlockSpec((rows, depth), lambda i, at: (0, 0)),
                pl.BlockSpec((depth, tile), lambda i, at: (0, at[0] + i))]
    args = [att, w_o]
    if x is not None:
        in_specs.append(pl.BlockSpec((rows, tile), lambda i, at: (0, at[0] + i)))
        args.append(x)
    return pl.pallas_call(
        _send_kernel if x is None else _keep_kernel,
        grid_spec=pltpu.PrefetchScalarGridSpec(
            num_scalar_prefetch=1, grid=(cols // tile,), in_specs=in_specs,
            out_specs=pl.BlockSpec((rows, tile), lambda i, at: (0, i))),
        out_shape=jax.ShapeDtypeStruct((rows, cols), BF16 if x is None else F32),
        compiler_params=pltpu.CompilerParams(vmem_limit_bytes=LIMIT),
        cost_estimate=_cost(2 * rows * depth * cols, 2 * depth * cols),
    )(first, *args)


def solution(mesh):
    n_ctx = mesh.shape['ctx']
    row_axes = ('dp', 'ctx')
    chip_swap = [(i, i ^ 2) for i in range(n_ctx)]
    core_swap = [(i, i ^ 1) for i in range(n_ctx)]
    tp_swap = [(0, 1), (1, 0)]

    def device_step(hidden, w_q, w_k, w_v, w_o, k_prefix, v_prefix, k_suffix, v_suffix, seq_lens):
        scale = LOG2E * k_prefix.shape[2] ** -0.5
        far = lambda a: lax.ppermute(a, 'ctx', chip_swap)
        near = lambda a: lax.ppermute(a, 'ctx', core_swap)
        (q,) = _project(hidden, [w_q], 512)
        q_far = far(q)
        q_near = near(q)
        kn, vn = _project(hidden, [w_k, w_v], 256)
        kt, vt = _relayout(k_prefix, v_prefix)
        q_diag = near(q_far)
        o_diag, o_far, l_diag, l_far = _prefix(q_diag, q_far, kt, vt, scale)
        o_x, l_x = _merge(o_far, l_far, near(o_diag), near(l_diag))
        o_x, l_x = far(o_x), far(l_x)
        o_near, o_own, l_near, l_own = _prefix(q_near, q, kt, vt, scale)
        o_near, l_near = near(o_near), near(l_near)
        o_suf, l_suf = _suffix(seq_lens, q, kn, vn, k_suffix, v_suffix, scale)
        att = _merge4([(o_own, l_own), (o_near, l_near), (o_x, l_x), (o_suf, l_suf)])

        me = lax.axis_index('tp')
        half = w_o.shape[1] // 2
        parts = 2
        cols = half // parts
        tile = 512
        sent = [lax.ppermute(_out_proj(att, w_o, None, ((1 - me) * half + p * cols)[None] // tile, cols, tile), 'tp', tp_swap)
                for p in range(parts)]
        kept = [_out_proj(att, w_o, hidden, (me * half + p * cols)[None] // tile, cols, tile) for p in range(parts)]
        mine = [(a + b.astype(F32)).astype(BF16) for a, b in zip(kept, sent)]
        other = [lax.ppermute(a, 'tp', tp_swap) for a in mine]
        mine, other = jnp.concatenate(mine, axis=1), jnp.concatenate(other, axis=1)
        return jnp.where(me == 0, jnp.concatenate([mine, other], axis=1), jnp.concatenate([other, mine], axis=1))

    spec_in = (P(row_axes, None), P(None, 'tp'), P(None, 'tp'), P(None, 'tp'), P('tp', None),
               P(row_axes, 'tp', None), P(row_axes, 'tp', None), P(row_axes, None, 'tp', None),
               P(row_axes, None, 'tp', None), P(row_axes))
    return jax.shard_map(device_step, mesh=mesh, in_specs=spec_in, out_specs=P(row_axes, None), check_vma=False)
```

time: 309 us -> 155 us (0.50)
  Pallas kernels: 0 us -> 116 us
  waiting for transfers between devices: 119 us -> 19.8 us
  matrix products: 87 us -> 0 us
  other arithmetic: 50.3 us -> 2.36 us
  local copies, waits for them, and re-layouts: 32.3 us -> 3.71 us
  between operations: 13.6 us -> 0.16 us
  starting transfers between devices: 5.7 us -> 10.8 us
    pallas_call x0 -> x12, Pallas kernels: none -> 116 us  [the longest x2 35.3 us: _prefix(): pl.pallas_call(functools.partial(_prefix_kernel, scale), grid=(heads,), i...]
    dot_general x7 -> x0, matrix products: 87 us -> none  [the longest x1 22.9 us: device_step(): jnp.einsum('bkgd,bskd->bkgs', q_local, k_suffix, preferred_element_type=j...]
    all_to_all x1 -> x0, waiting for transfers between devices: 60.7 us -> none  [device_step(): returned = lax.all_to_all(partial_state, 'ctx', 0, 0, tiled=True)]
    psum x1 -> x0, waiting for transfers between devices: 58.1 us -> none  [device_step(): out_hidden = hidden.astype(jnp.float32) + lax.psum(proj_part, 'tp')]
    unnamed x3 -> x0, other arithmetic: 22.5 us -> none
    reduce_sum x3 -> x0, other arithmetic: 20.4 us -> none  [the longest x1 14.4 us: device_step(): l_pre = jnp.sum(e_pre, axis=-1)]
    ppermute x0 -> x13, waiting for transfers between devices: none -> 19.8 us  [the longest x3 11.9 us: device_step(): far = lambda a: lax.ppermute(a, 'ctx', chip_swap)]
    all_to_all x1 -> x0, local copies, waits for them, and re-layouts: 12.5 us -> none  [device_step(): returned = lax.all_to_all(partial_state, 'ctx', 0, 0, tiled=True)]
  transfers between devices with their start and end apart: 3 -> 13, of which waited for: 2 -> 3; matrix products, arithmetic and copies ran while one was open for 24% -> 1% of each run, Pallas kernels for 0% -> 54%
where the time goes in v1:
time: 155 us; the launch traced here: 153 us
  Pallas kernels  116 us (75%)
  waiting for transfers between devices  19.8 us (13%)
  starting transfers between devices  10.8 us (7%)
  local copies, waits for them, and re-layouts  3.71 us (2%)
  other arithmetic  2.36 us (2%)
    pallas_call x2, Pallas kernels, _prefix(): pl.pallas_call(functools.partial(_prefix_kernel, scale), grid=(heads,), i...  35.3 us
    pallas_call x1, Pallas kernels, _suffix(): pl.pallas_call(functools.partial(_suffix_kernel, scale), in_specs=[pl.Blo...  26.3 us
    pallas_call x2, Pallas kernels, _project(): pl.pallas_call(_proj_kernel, grid=(cols // tile,), in_specs=[pl.BlockSpec...  23.3 us
    pallas_call x4, Pallas kernels, _out_proj(): pl.pallas_call(_send_kernel if x is None else _keep_kernel, grid_spec=plt...  14.3 us
    ppermute x3, waiting for transfers between devices, device_step(): far = lambda a: lax.ppermute(a, 'ctx', chip_swap)  11.9 us
    pallas_call x1, Pallas kernels, _relayout(): pl.pallas_call(_relayout_kernel, grid=(n // t,), in_specs=[pl.BlockSpec((...  10 us
    ppermute x2, waiting for transfers between devices, device_step(): other = [lax.ppermute(a, 'tp', tp_swap) for a in mine]  7.9 us
    ppermute x3, starting transfers between devices, device_step(): far = lambda a: lax.ppermute(a, 'ctx', chip_swap)  5.37 us
  transfers between devices with their start and end apart: 13, of which 3 were waited for; matrix products, arithmetic and copies ran while one was open for 1% of the time, Pallas kernels for 54%

profile of v1, /device:TPU:0, one launch (start us, length us, event | category | flops | bytes accessed | tf_op | source)
XLA Modules:
  0.0 153.3 jit_solution(14966883579618899688)
XLA Ops:
  0.0 8.4 %shard_map.100.q1_ref.q_ref = bf16[16,128,128]{2,1,0:T(8,128)(2,1)} custom-call(bf16[128,4096]{1,0:T(8,128)(2,1)} %x_ref.7, bf16[4096,2048]{1,0:T(8,128)(2,1)} %refs_0_.2), custom_call_target="tpu_custom_call" | custom-call | flops 2147483648 | bytes 16777216 | tf_op jit(solution)/shard_map/pallas_call | solution.py:45
  8.4 3.3 %collective-permute-start.3 = (bf16[16,128,128]{2,1,0:T(8,128)(2,1)}, bf16[16,128,128]{2,1,0:T(8,128)(2,1)S(1)}, u32[]{:S(2)}, u32[]{:S(2)}) collective-permute-start(bf16[16,128,128]{2,1,0:T(8,128)(2,1)} %shard_map.100.q1_ref.q_ref), channel_id=1, source_target_pairs={{0,2},{1,3},{2,0},{3,1},{4,6},{5,7},{6,4},{7,5}} | collective-permute-start | bytes 1572872 | tf_op jit(solution)/shard_map/ppermute | solution.py:341
  11.7 11.9 %collective-permute-done.3.q1_ref = bf16[16,128,128]{2,1,0:T(8,128)(2,1)S(1)} collective-permute-done((bf16[16,128,128]{2,1,0:T(8,128)(2,1)}, bf16[16,128,128]{2,1,0:T(8,128)(2,1)S(1)}, u32[]{:S(2)}, u32[]{:S(2)}) %collective-permute-start.3) | collective-permute-done | bytes 524320 | tf_op jit(solution)/shard_map/ppermute | solution.py:341
  23.7 0.0 copy-start.4
  23.7 0.0 collective-permute-start.4
  23.7 10.0 %shard_map.101 = (bf16[16,1024,128]{2,1,0:T(8,128)(2,1)}, bf16[16,1024,128]{2,1,0:T(8,128)(2,1)}) custom-call(bf16[1024,16,128]{2,1,0:T(8,128)(2,1)} %k_ref.1, bf16[1024,16,128]{2,1,0:T(8,128)(2,1)} %v_ref.1), custom_call_target="tpu_custom_call" | custom-call | flops 2000000000 | bytes 16777216 | tf_op jit(solution)/shard_map/pallas_call | solution.py:69
  33.7 0.0 copy-done.4
  33.7 0.0 collective-permute-done.4.q0_ref
  33.7 0.0 copy-start.6
  33.7 0.8 copy-done.6
  34.5 0.0 copy-start
  34.5 17.7 %shard_map.103 = (f32[16,128,128]{2,1,0:T(8,128)}, f32[16,128,128]{2,1,0:T(8,128)}, f32[128,128]{1,0:T(8,128)}, f32[128,128]{1,0:T(8,128)}) custom-call(bf16[16,128,128]{2,1,0:T(8,128)(2,1)} %copy-done.6, bf16[16,128,128]{2,1,0:T(8,128)(2,1)} %copy-done.4, bf16[16,1024,128]{2,1,0:T(8,128)(2,1)} %get-tuple-element.21.k_ref, ...), custom_call_target="tpu_custom_call" | custom-call | flops 2147483648 | bytes 8388608 | tf_op jit(solution)/shard_map/pallas_call | solution.py:105
  52.2 0.0 copy-start.10
  52.2 0.3 collective-permute-start.5
  52.5 0.0 copy-done
  52.5 0.2 collective-permute-start
  52.7 14.9 %shard_map.105 = (bf16[16,128,128]{2,1,0:T(8,128)(2,1)}, bf16[16,128,128]{2,1,0:T(8,128)(2,1)}) custom-call(bf16[128,4096]{1,0:T(8,128)(2,1)} %x_ref.7, bf16[4096,2048]{1,0:T(8,128)(2,1)} %refs_0_.3, bf16[4096,2048]{1,0:T(8,128)(2,1)} %refs_1_.1), custom_call_target="tpu_custom_call" | custom-call | flops 4294967296 | bytes 33554432 | tf_op jit(solution)/shard_map/pallas_call | solution.py:45
  67.6 0.0 copy-done.10
  67.6 0.3 collective-permute-start.6
  67.9 0.0 collective-permute-done.q0_ref
  67.9 0.0 copy-start.5
  67.9 0.8 copy-done.5
  68.7 17.6 %shard_map.102 = (f32[16,128,128]{2,1,0:T(8,128)}, f32[16,128,128]{2,1,0:T(8,128)}, f32[128,128]{1,0:T(8,128)}, f32[128,128]{1,0:T(8,128)}) custom-call(bf16[16,128,128]{2,1,0:T(8,128)(2,1)} %copy-done.5, bf16[16,128,128]{2,1,0:T(8,128)(2,1)} %shard_map.100.q1_ref.q_ref, bf16[16,1024,128]{2,1,0:T(8,128)(2,1)} %get-tuple-element.21.k_ref, ...), custom_call_target="tpu_custom_call" | custom-call | flops 2147483648 | bytes 8388608 | tf_op jit(solution)/shard_map/pallas_call | solution.py:105
  86.4 0.2 collective-permute-start.1
  86.6 0.3 collective-permute-start.2
  86.9 0.0 collective-permute-done.6.l1_ref
  86.9 0.0 copy-start.11
  86.9 0.0 collective-permute-done.5.o1_ref
  86.9 0.0 copy-start.9
  86.9 0.6 copy-done.11
  87.5 0.4 copy-done.9
  87.9 3.1 %shard_map.104 = (bf16[16,128,128]{2,1,0:T(8,128)(2,1)}, f32[128,128]{1,0:T(8,128)}) custom-call(f32[16,128,128]{2,1,0:T(8,128)} %get-tuple-element.27.o0_ref, f32[128,128]{1,0:T(8,128)} %get-tuple-element.28.l0_ref, f32[16,128,128]{2,1,0:T(8,128)} %copy-done.9, f32[128,128]{1,0:T(8,128)} %copy-done.11), custom_call_target="tpu_custom_call" | custom-call | flops 1000000000 | bytes 2621440 | tf_op jit(solution)/shard_map/pallas_call | solution.py:129
  90.9 1.7 %collective-permute-start.7 = (bf16[16,128,128]{2,1,0:T(8,128)(2,1)}, bf16[16,128,128]{2,1,0:T(8,128)(2,1)S(1)}, u32[]{:S(2)}, u32[]{:S(2)}) collective-permute-start(bf16[16,128,128]{2,1,0:T(8,128)(2,1)} %get-tuple-element.31), channel_id=1, source_target_pairs={{0,2},{1,3},{2,0},{3,1},{4,6},{5,7},{6,4},{7,5}} | collective-permute-start | bytes 1572872 | tf_op jit(solution)/shard_map/ppermute | solution.py:341
  92.7 0.3 collective-permute-start.8
  93.0 26.3 %shard_map.106 = (f32[16,128,128]{2,1,0:T(8,128)}, f32[128,128]{1,0:T(8,128)}) custom-call(s32[128]{0:T(128)} %lens.1, bf16[16,128,128]{2,1,0:T(8,128)(2,1)} %shard_map.100.q1_ref.q_ref, bf16[16,128,128]{2,1,0:T(8,128)(2,1)} %get-tuple-element.33.kn_ref, bf16[16,128,128]{2,1,0:T(8,128)(2,1)} %get-tuple-element.34.vn_ref, bf16[512,256,128]{2,1,0:T(8,128)(2,1)} %bitcast.6, ...), custom_call_target="tpu_custom_call" | custom-call | flops 20000000000 | bytes 67108864 | tf_op jit(solution)/shard_map/pallas_call | solution.py:255
  119.3 0.0 collective-permute-done.2.refs_3_
  119.3 0.0 copy-start.7
  119.3 0.0 collective-permute-done.1.refs_2_
  119.3 0.0 copy-start.2
  119.3 0.0 collective-permute-done.8.refs_5_
  119.3 0.0 copy-start.8
  119.3 0.0 collective-permute-done.7.refs_4_
  119.3 0.0 copy-start.3
  119.4 0.5 copy-done.7
  119.9 0.4 copy-done.2
  120.3 0.0 copy-done.8
  120.3 0.2 copy-done.3
  120.5 4.2 %shard_map.107.a_ref = bf16[128,2048]{1,0:T(8,128)(2,1)} custom-call(f32[16,128,128]{2,1,0:T(8,128)} %get-tuple-element.23.refs_0_, f32[128,128]{1,0:T(8,128)} %get-tuple-element.24.refs_1_, f32[16,128,128]{2,1,0:T(8,128)} %copy-done.2, f32[128,128]{1,0:T(8,128)} %copy-done.7, bf16[16,128,128]{2,1,0:T(8,128)(2,1)} %copy-done.3, f32[128,128]{1,0:T(8,128)} %copy-done.8, ...), custom_call_target="tpu_custom_call" | custom-call | flops 1000000000 | bytes 5242880 | tf_op jit(solution)/shard_map/pallas_call | solution.py:295
  124.6 3.5 %shard_map.109 = bf16[128,1024]{1,0:T(8,128)(2,1)} custom-call(s32[1]{0:T(128)S(6)} %select_n.24.at, bf16[128,2048]{1,0:T(8,128)(2,1)} %shard_map.107.a_ref, bf16[2048,4096]{1,0:T(8,128)(2,1)} %w_ref.7), custom_call_target="tpu_custom_call" | custom-call | flops 536870912 | bytes 4194304 | tf_op jit(solution)/shard_map/pallas_call | solution.py:321
  128.2 1.8 %collective-permute-start.9 = (bf16[128,1024]{1,0:T(8,128)(2,1)}, bf16[128,1024]{1,0:T(8,128)(2,1)S(1)}, u32[]{:S(2)}, u32[]{:S(2)}) collective-permute-start(bf16[128,1024]{1,0:T(8,128)(2,1)} %shard_map.109), channel_id=1, source_target_pairs={{0,4},{4,0},{1,5},{5,1},{2,6},{6,2},{3,7},{7,3}} | collective-permute-start | bytes 786440 | tf_op jit(solution)/shard_map/ppermute | solution.py:362
  129.9 3.5 %shard_map.111 = bf16[128,1024]{1,0:T(8,128)(2,1)} custom-call(s32[1]{0:T(128)S(6)} %select_n.26.at, bf16[128,2048]{1,0:T(8,128)(2,1)} %shard_map.107.a_ref, bf16[2048,4096]{1,0:T(8,128)(2,1)} %w_ref.7), custom_call_target="tpu_custom_call" | custom-call | flops 536870912 | bytes 4194304 | tf_op jit(solution)/shard_map/pallas_call | solution.py:321
  133.4 0.3 collective-permute-start.10
  133.7 3.6 %shard_map.108 = f32[128,1024]{1,0:T(8,128)} custom-call(s32[1]{0:T(128)S(6)} %select_n.23.at, bf16[128,2048]{1,0:T(8,128)(2,1)} %shard_map.107.a_ref, bf16[2048,4096]{1,0:T(8,128)(2,1)} %w_ref.7, bf16[128,4096]{1,0:T(8,128)(2,1)} %x_ref.7), custom_call_target="tpu_custom_call" | custom-call | flops 536870912 | bytes 4194304 | tf_op jit(solution)/shard_map/pallas_call | solution.py:321
  137.3 3.7 %shard_map.110 = f32[128,1024]{1,0:T(8,128)} custom-call(s32[1]{0:T(128)S(6)} %select_n.25.at, bf16[128,2048]{1,0:T(8,128)(2,1)} %shard_map.107.a_ref, bf16[2048,4096]{1,0:T(8,128)(2,1)} %w_ref.7, bf16[128,4096]{1,0:T(8,128)(2,1)} %x_ref.7), custom_call_target="tpu_custom_call" | custom-call | flops 536870912 | bytes 4194304 | tf_op jit(solution)/shard_map/pallas_call | solution.py:321
  140.9 0.0 collective-permute-done.9
  141.0 0.0 copy-done.1
  141.0 0.1 add_convert_fusion.1
  141.0 1.8 %collective-permute-start.11 = (bf16[128,1024]{1,0:T(8,128)(2,1)S(1)}, bf16[128,1024]{1,0:T(8,128)(2,1)S(1)}, u32[]{:S(2)}, u32[]{:S(2)}) collective-permute-start(bf16[128,1024]{1,0:T(8,128)(2,1)S(1)} %add_convert_fusion.1), channel_id=1, source_target_pairs={{0,4},{4,0},{1,5},{5,1},{2,6},{6,2},{3,7},{7,3}} | collective-permute-start | bytes 786440 | tf_op jit(solution)/shard_map/ppermute | solution.py:366
  142.8 0.0 collective-permute-done.10
  142.8 1.1 add_convert_fusion
  143.9 0.3 collective-permute-start.12
  144.2 5.1 %collective-permute-done.11 = bf16[128,1024]{1,0:T(8,128)(2,1)S(1)} collective-permute-done((bf16[128,1024]{1,0:T(8,128)(2,1)S(1)}, bf16[128,1024]{1,0:T(8,128)(2,1)S(1)}, u32[]{:S(2)}, u32[]{:S(2)}) %collective-permute-start.11) | collective-permute-done | bytes 262176 | tf_op jit(solution)/shard_map/ppermute | solution.py:366
  149.3 2.8 %collective-permute-done.12 = bf16[128,1024]{1,0:T(8,128)(2,1)S(1)} collective-permute-done((bf16[128,1024]{1,0:T(8,128)(2,1)S(1)}, bf16[128,1024]{1,0:T(8,128)(2,1)S(1)}, u32[]{:S(2)}, u32[]{:S(2)}) %collective-permute-start.12) | collective-permute-done | bytes 262176 | tf_op jit(solution)/shard_map/ppermute | solution.py:366
  152.1 1.2 maximum_select_fusion
  (1 shorter events, 0.0 us)
Async XLA Ops:
  8.4 15.3 %collective-permute-start.3 = (bf16[16,128,128]{2,1,0:T(8,128)(2,1)}, bf16[16,128,128]{2,1,0:T(8,128)(2,1)S(1)}, u32[]{:S(2)}, u32[]{:S(2)}) collective-permute-start(bf16[16,128,128]{2,1,0:T(8,128)(2,1)} %shard_map.100.q1_ref.q_ref), channel_id=1, source_target_pairs={{0,2},{1,3},{2,0},{3,1},{4,6},{5,7},{6,4},{7,5}} | collective-permute-start | bytes 1572872 | tf_op jit(solution)/shard_map/ppermute | solution.py:341
  23.7 10.0 %copy-start.4 = (bf16[16,128,128]{2,1,0:T(8,128)(2,1)}, bf16[16,128,128]{2,1,0:T(8,128)(2,1)S(1)}, u32[]{:S(2)}) copy-start(bf16[16,128,128]{2,1,0:T(8,128)(2,1)S(1)} %collective-permute-done.3.q1_ref) | copy-start | bytes 1572868
  23.7 10.0 %collective-permute-start.4 = (bf16[16,128,128]{2,1,0:T(8,128)(2,1)S(1)}, bf16[16,128,128]{2,1,0:T(8,128)(2,1)S(1)}, u32[]{:S(2)}, u32[]{:S(2)}) collective-permute-start(bf16[16,128,128]{2,1,0:T(8,128)(2,1)S(1)} %collective-permute-done.3.q1_ref), channel_id=1, source_target_pairs={{0,1},{1,0},{2,3},{3,2},{4,5},{5,4},{6,7},{7,6}} | collective-permute-start | bytes 1572872 | tf_op jit(solution)/shard_map/ppermute | solution.py:342
  33.7 0.8 copy-start.6
  34.5 18.0 %copy-start = (bf16[16,128,128]{2,1,0:T(8,128)(2,1)S(1)}, bf16[16,128,128]{2,1,0:T(8,128)(2,1)}, u32[]{:S(2)}) copy-start(bf16[16,128,128]{2,1,0:T(8,128)(2,1)} %shard_map.100.q1_ref.q_ref) | copy-start | bytes 1572868
  52.2 15.4 %copy-start.10 = (f32[128,128]{1,0:T(8,128)S(1)}, f32[128,128]{1,0:T(8,128)}, u32[]{:S(2)}) copy-start(f32[128,128]{1,0:T(8,128)} %get-tuple-element.30) | copy-start | bytes 196612
  52.2 34.7 %collective-permute-start.5 = (f32[16,128,128]{2,1,0:T(8,128)}, f32[16,128,128]{2,1,0:T(8,128)S(1)}, u32[]{:S(2)}, u32[]{:S(2)}) collective-permute-start(f32[16,128,128]{2,1,0:T(8,128)} %get-tuple-element.29), channel_id=1, source_target_pairs={{0,1},{1,0},{2,3},{3,2},{4,5},{5,4},{6,7},{7,6}} | collective-permute-start | bytes 3145736 | tf_op jit(solution)/shard_map/ppermute | solution.py:342
  52.5 15.4 %collective-permute-start = (bf16[16,128,128]{2,1,0:T(8,128)(2,1)S(1)}, bf16[16,128,128]{2,1,0:T(8,128)(2,1)S(1)}, u32[]{:S(2)}, u32[]{:S(2)}) collective-permute-start(bf16[16,128,128]{2,1,0:T(8,128)(2,1)S(1)} %copy-done), channel_id=1, source_target_pairs={{0,1},{1,0},{2,3},{3,2},{4,5},{5,4},{6,7},{7,6}} | collective-permute-start | bytes 1572872 | tf_op jit(solution)/shard_map/ppermute | solution.py:342
  67.6 19.3 %collective-permute-start.6 = (f32[128,128]{1,0:T(8,128)S(1)}, f32[128,128]{1,0:T(8,128)S(1)}, u32[]{:S(2)}, u32[]{:S(2)}) collective-permute-start(f32[128,128]{1,0:T(8,128)S(1)} %copy-done.10), channel_id=1, source_target_pairs={{0,1},{1,0},{2,3},{3,2},{4,5},{5,4},{6,7},{7,6}} | collective-permute-start | bytes 196616 | tf_op jit(solution)/shard_map/ppermute | solution.py:342
  67.9 0.8 copy-start.5
  86.4 32.9 %collective-permute-start.1 = (f32[16,128,128]{2,1,0:T(8,128)}, f32[16,128,128]{2,1,0:T(8,128)S(1)}, u32[]{:S(2)}, u32[]{:S(2)}) collective-permute-start(f32[16,128,128]{2,1,0:T(8,128)} %get-tuple-element.25), channel_id=1, source_target_pairs={{0,1},{1,0},{2,3},{3,2},{4,5},{5,4},{6,7},{7,6}} | collective-permute-start | bytes 3145736 | tf_op jit(solution)/shard_map/ppermute | solution.py:342
  86.6 32.7 %collective-permute-start.2 = (f32[128,128]{1,0:T(8,128)}, f32[128,128]{1,0:T(8,128)S(1)}, u32[]{:S(2)}, u32[]{:S(2)}) collective-permute-start(f32[128,128]{1,0:T(8,128)} %get-tuple-element.26), channel_id=1, source_target_pairs={{0,1},{1,0},{2,3},{3,2},{4,5},{5,4},{6,7},{7,6}} | collective-permute-start | bytes 196616 | tf_op jit(solution)/shard_map/ppermute | solution.py:342
  86.9 0.6 copy-start.11
  86.9 1.0 copy-start.9
  90.9 28.4 %collective-permute-start.7 = (bf16[16,128,128]{2,1,0:T(8,128)(2,1)}, bf16[16,128,128]{2,1,0:T(8,128)(2,1)S(1)}, u32[]{:S(2)}, u32[]{:S(2)}) collective-permute-start(bf16[16,128,128]{2,1,0:T(8,128)(2,1)} %get-tuple-element.31), channel_id=1, source_target_pairs={{0,2},{1,3},{2,0},{3,1},{4,6},{5,7},{6,4},{7,5}} | collective-permute-start | bytes 1572872 | tf_op jit(solution)/shard_map/ppermute | solution.py:341
  92.7 26.6 %collective-permute-start.8 = (f32[128,128]{1,0:T(8,128)}, f32[128,128]{1,0:T(8,128)S(1)}, u32[]{:S(2)}, u32[]{:S(2)}) collective-permute-start(f32[128,128]{1,0:T(8,128)} %get-tuple-element.32), channel_id=1, source_target_pairs={{0,2},{1,3},{2,0},{3,1},{4,6},{5,7},{6,4},{7,5}} | collective-permute-start | bytes 196616 | tf_op jit(solution)/shard_map/ppermute | solution.py:341
  119.3 0.6 copy-start.7
  119.3 1.0 copy-start.2
  119.3 1.0 copy-start.8
  119.3 1.1 copy-start.3
  128.2 12.8 %collective-permute-start.9 = (bf16[128,1024]{1,0:T(8,128)(2,1)}, bf16[128,1024]{1,0:T(8,128)(2,1)S(1)}, u32[]{:S(2)}, u32[]{:S(2)}) collective-permute-start(bf16[128,1024]{1,0:T(8,128)(2,1)} %shard_map.109), channel_id=1, source_target_pairs={{0,4},{4,0},{1,5},{5,1},{2,6},{6,2},{3,7},{7,3}} | collective-permute-start | bytes 786440 | tf_op jit(solution)/shard_map/ppermute | solution.py:362
  133.4 9.4 %collective-permute-start.10 = (bf16[128,1024]{1,0:T(8,128)(2,1)}, bf16[128,1024]{1,0:T(8,128)(2,1)S(1)}, u32[]{:S(2)}, u32[]{:S(2)}) collective-permute-start(bf16[128,1024]{1,0:T(8,128)(2,1)} %shard_map.111), channel_id=1, source_target_pairs={{0,4},{4,0},{1,5},{5,1},{2,6},{6,2},{3,7},{7,3}} | collective-permute-start | bytes 786440 | tf_op jit(solution)/shard_map/ppermute | solution.py:362
  137.3 3.7 %copy-start.1 = (f32[128,1024]{1,0:T(8,128)S(1)}, f32[128,1024]{1,0:T(8,128)}, u32[]{:S(2)}) copy-start(f32[128,1024]{1,0:T(8,128)} %shard_map.108) | copy-start | bytes 1572868
  141.0 8.3 %collective-permute-start.11 = (bf16[128,1024]{1,0:T(8,128)(2,1)S(1)}, bf16[128,1024]{1,0:T(8,128)(2,1)S(1)}, u32[]{:S(2)}, u32[]{:S(2)}) collective-permute-start(bf16[128,1024]{1,0:T(8,128)(2,1)S(1)} %add_convert_fusion.1), channel_id=1, source_target_pairs={{0,4},{4,0},{1,5},{5,1},{2,6},{6,2},{3,7},{7,3}} | collective-permute-start | bytes 786440 | tf_op jit(solution)/shard_map/ppermute | solution.py:366
  143.9 8.2 %collective-permute-start.12 = (bf16[128,1024]{1,0:T(8,128)(2,1)S(1)}, bf16[128,1024]{1,0:T(8,128)(2,1)S(1)}, u32[]{:S(2)}, u32[]{:S(2)}) collective-permute-start(bf16[128,1024]{1,0:T(8,128)(2,1)S(1)} %add_convert_fusion), channel_id=1, source_target_pairs={{0,4},{4,0},{1,5},{5,1},{2,6},{6,2},{3,7},{7,3}} | collective-permute-start | bytes 786440 | tf_op jit(solution)/shard_map/ppermute | solution.py:366

commit v2 on v1

v2 whole, which is shorter than its diff:
```python
import functools

import jax
import jax.numpy as jnp
from jax import lax
from jax.experimental import pallas as pl
from jax.experimental.pallas import tpu as pltpu
from jax.sharding import PartitionSpec as P

F32 = jnp.float32
BF16 = jnp.bfloat16
VM = pltpu.VMEM
LOG2E = 1.4426950408889634
BATCH = 16
SLOTS = 16
RING = 5
CHUNK = 256
RINGW = 10
LIMIT = 56 * 2**20


def _cost(flops, nbytes):
    return pl.CostEstimate(flops=int(flops), bytes_accessed=int(nbytes), transcendentals=0)


def _dot(a, b, dims=(((1,), (0,)), ((), ()))):
    return lax.dot_general(a, b, dims, preferred_element_type=F32)


NT = (((1,), (1,)), ((), ()))


def _stream(x_ref, ws, bufs, sem, acc, chunk, emit, extra_start=None, extra_body=None):
    depth = ws[0].shape[0]
    n = depth // chunk
    total = n * len(ws)

    def start(g):
        for i, w in enumerate(ws):
            @pl.when((g >= i * n) & (g < (i + 1) * n))
            def _():
                at = pl.multiple_of((g - i * n) * chunk, chunk)
                pltpu.make_async_copy(w.at[pl.ds(at, chunk)], bufs.at[lax.rem(g, RINGW)],
                                      sem.at[lax.rem(g, RINGW)]).start()
        if extra_start is not None:
            @pl.when(g < total)
            def _():
                extra_start(g)

    def run():
        for i, w in enumerate(ws):
            def body(c, carry):
                g = i * n + c
                slot = lax.rem(g, RINGW)
                pltpu.make_async_copy(w.at[pl.ds(0, chunk)], bufs.at[slot], sem.at[slot]).wait()
                at = pl.multiple_of(c * chunk, chunk)
                y = _dot(x_ref[:, pl.ds(at, chunk)], bufs[slot])

                @pl.when(c == 0)
                def _():
                    acc[...] = y

                @pl.when(c > 0)
                def _():
                    acc[...] += y
                if extra_body is not None:
                    extra_body(g)
                start(g + RINGW)
                return carry
            lax.fori_loop(0, n, body, 0)
            emit(i)
    return start, run


def _prime(start, count):
    def body(g, c):
        start(g)
        return c
    lax.fori_loop(0, count, body, 0)


def _heads_out(acc, o_ref):
    for h in range(o_ref.shape[0]):
        o_ref[h] = acc[:, h * 128:(h + 1) * 128].astype(BF16)


def _q_kernel(x_hbm, w_hbm, o_ref, x_ref, bufs, acc, xsem, sem):
    cp = pltpu.make_async_copy(x_hbm, x_ref, xsem)
    cp.start()
    start, run = _stream(x_ref, [w_hbm], bufs, sem, acc, bufs.shape[1], lambda i: _heads_out(acc, o_ref))
    _prime(start, RINGW)
    cp.wait()
    run()


def _project_q(x, w):
    rows, depth = x.shape
    cols = w.shape[1]
    return pl.pallas_call(
        _q_kernel,
        in_specs=[pl.BlockSpec(memory_space=pl.ANY)] * 2,
        out_specs=pl.BlockSpec(memory_space=VM),
        out_shape=jax.ShapeDtypeStruct((cols // 128, rows, 128), BF16),
        scratch_shapes=[VM((rows, depth), BF16), VM((RINGW, CHUNK, cols), BF16), VM((rows, cols), F32),
                        pltpu.SemaphoreType.DMA, pltpu.SemaphoreType.DMA((RINGW,))],
        compiler_params=pltpu.CompilerParams(vmem_limit_bytes=LIMIT),
        cost_estimate=_cost(2 * rows * depth * cols, 2 * depth * cols),
    )(x, w)


def _kv_kernel(x_hbm, wk_hbm, wv_hbm, kp_hbm, vp_hbm, kn_ref, vn_ref, kt_hbm, vt_hbm,
               x_ref, bufs, acc, raw, out, xsem, sem, psem, osem):
    cp = pltpu.make_async_copy(x_hbm, x_ref, xsem)
    cp.start()
    chunk = bufs.shape[1]
    total = 2 * x_hbm.shape[1] // chunk
    pos = kp_hbm.shape[0] // total
    stage = total // 4

    def pieces(g):
        at = pl.ds(g * pos, pos)
        return [pltpu.make_async_copy(src.at[at], raw.at[j, at], psem.at[lax.rem(g, RINGW)])
                for j, src in enumerate((kp_hbm, vp_hbm))]

    def stores(s):
        at = pl.ds(pl.multiple_of(s * stage * pos, stage * pos), stage * pos)
        return [pltpu.make_async_copy(out.at[j, :, at], dst.at[:, at], osem)
                for j, dst in enumerate((kt_hbm, vt_hbm))]

    def extra_start(g):
        for c in pieces(g):
            c.start()

    def extra_body(g):
        for c in pieces(g):
            c.wait()
        for j in range(2):
            for u in range(pos // 16):
                at = pl.multiple_of(g * pos + u * 16, 16)
                out[j, :, pl.ds(at, 16), :] = jnp.swapaxes(raw[j, pl.ds(g * pos + u * 16, 16)], 0, 1)

        @pl.when(lax.rem(g + 1, stage) == 0)
        def _():
            for c in stores(g // stage):
                c.start()

    start, run = _stream(x_ref, [wk_hbm, wv_hbm], bufs, sem, acc, chunk,
                         lambda i: _heads_out(acc, (kn_ref, vn_ref)[i]), extra_start, extra_body)
    _prime(start, RINGW)
    cp.wait()
    run()
    for s in range(4):
        for c in stores(s):
            c.wait()


def _project_kv(x, wk, wv, kp, vp):
    rows, depth = x.shape
    cols = wk.shape[1]
    n, heads, d = kp.shape
    return pl.pallas_call(
        _kv_kernel,
        in_specs=[pl.BlockSpec(memory_space=pl.ANY)] * 5,
        out_specs=[pl.BlockSpec(memory_space=VM)] * 2 + [pl.BlockSpec(memory_space=pl.ANY)] * 2,
        out_shape=[jax.ShapeDtypeStruct((cols // 128, rows, 128), BF16)] * 2
        + [jax.ShapeDtypeStruct((heads, n, d), BF16)] * 2,
        scratch_shapes=[VM((rows, depth), BF16), VM((RINGW, CHUNK, cols), BF16), VM((rows, cols), F32),
                        VM((2, n, heads, d), BF16), VM((2, heads, n, d), BF16),
                        pltpu.SemaphoreType.DMA, pltpu.SemaphoreType.DMA((RINGW,)),
                        pltpu.SemaphoreType.DMA((RINGW,)), pltpu.SemaphoreType.DMA],
        compiler_params=pltpu.CompilerParams(vmem_limit_bytes=LIMIT),
        cost_estimate=_cost(2e10, 4 * depth * cols),
    )(x, wk, wv, kp, vp)


def _prefix_kernel(scale, q0_ref, q1_ref, k_ref, v_ref, o0_ref, o1_ref):
    group = k_ref.shape[0]
    heads = o0_ref.shape[0] - 1
    i = pl.program_id(0)
    rows = q0_ref.shape[1]
    lane = lax.broadcasted_iota(jnp.int32, (rows, 128), 1)

    @pl.when(i == 0)
    def _():
        o0_ref[heads] = jnp.zeros_like(o0_ref[heads])
        o1_ref[heads] = jnp.zeros_like(o1_ref[heads])

    units = [(u, q, o) for u in range(group) for q, o in ((q0_ref, o0_ref), (q1_ref, o1_ref))]
    lses = {id(o0_ref): [], id(o1_ref): []}
    for u, q_ref, o_ref in units:
        s = _dot(q_ref[u], k_ref[u], NT)
        m = jnp.max(s, axis=1, keepdims=True) * scale
        e = jnp.exp2(s * scale - m)
        l = jnp.sum(e, axis=1, keepdims=True)
        o = _dot(e.astype(BF16), v_ref[u])
        o_ref[i * group + u] = o / l
        lses[id(o_ref)].append(m + jnp.log2(l))
    for o_ref in (o0_ref, o1_ref):
        x = o_ref[heads]
        for u, lse in enumerate(lses[id(o_ref)]):
            x = jnp.where(lane == i * group + u, lse, x)
        o_ref[heads] = x


def _prefix(q0, q1, k, v, scale):
    heads, rows, d = q0.shape
    n = k.shape[1]
    group = 2
    head = lambda i: (i, 0, 0)
    return pl.pallas_call(
        functools.partial(_prefix_kernel, scale),
        grid=(heads // group,),
        in_specs=[pl.BlockSpec((group, rows, d), head)] * 2 + [pl.BlockSpec((group, n, d), head)] * 2,
        out_specs=[pl.BlockSpec((heads + 1, rows, d), lambda i: (0, 0, 0))] * 2,
        out_shape=[jax.ShapeDtypeStruct((heads + 1, rows, d), F32)] * 2,
        compiler_params=pltpu.CompilerParams(vmem_limit_bytes=LIMIT),
        cost_estimate=_cost(8 * heads * rows * n * d, 4 * heads * n * d),
    )(q0, q1, k, v)


def _merge_kernel(a_ref, b_ref, o_ref):
    heads = a_ref.shape[0] - 1
    l0, l1 = a_ref[heads], b_ref[heads]
    m = jnp.maximum(l0, l1)
    w0, w1 = jnp.exp2(l0 - m), jnp.exp2(l1 - m)
    t = w0 + w1
    w0, w1 = w0 / t, w1 / t
    for h in range(heads):
        o_ref[h] = (w0[:, h:h + 1] * a_ref[h] + w1[:, h:h + 1] * b_ref[h]).astype(BF16)
    lse = m + jnp.log2(t)
    for j in range(3):
        term = lse.astype(BF16)
        o_ref[heads + j] = term
        lse = lse - term.astype(F32)


def _merge(a, b):
    heads = a.shape[0] - 1
    return pl.pallas_call(
        _merge_kernel,
        in_specs=[pl.BlockSpec(memory_space=VM)] * 2,
        out_specs=pl.BlockSpec(memory_space=VM),
        out_shape=jax.ShapeDtypeStruct((heads + 3,) + a.shape[1:], BF16),
        compiler_params=pltpu.CompilerParams(vmem_limit_bytes=LIMIT),
        cost_estimate=_cost(1e9, 10 * a.size),
    )(a, b)


def _suffix_kernel(scale, lens, q_ref, kn_ref, vn_ref, k_hbm, v_hbm, o_ref,
                   items, qb, acc, m_s, l_s, kbuf, vbuf, sbuf, ksem, vsem):
    heads, rows, d = q_ref.shape
    per = k_hbm.shape[0] // rows
    wide = SLOTS * heads
    dummy = rows * per

    for g in range(BATCH):
        items[g] = dummy

    def listing(b, t):
        for j in range(per):
            items[BATCH + t + j] = b * per + j
        return t + (lens[b] + SLOTS - 1) // SLOTS
    total = lax.fori_loop(0, rows, listing, 0)
    for g in range(2 * BATCH):
        items[BATCH + total + g] = dummy
    batches = (total + BATCH - 1) // BATCH

    def fetch(i):
        slot = lax.rem(i, RING)
        for g in range(BATCH):
            it = jnp.minimum(items[BATCH + i * BATCH + g], dummy - 1)
            pltpu.make_async_copy(k_hbm.at[it], kbuf.at[slot, g], ksem.at[slot]).start()
            pltpu.make_async_copy(v_hbm.at[it], vbuf.at[slot, g], vsem.at[slot]).start()

    def prime(i, c):
        fetch(i)
        return c
    lax.fori_loop(0, jnp.minimum(batches, RING - 1), prime, 0)

    for c in range(rows // 16):
        q = jnp.swapaxes(q_ref[:, c * 16:c * 16 + 16, :], 0, 1)
        kn = jnp.swapaxes(kn_ref[:, c * 16:c * 16 + 16, :], 0, 1)
        vn = jnp.swapaxes(vn_ref[:, c * 16:c * 16 + 16, :], 0, 1)
        qb[c * 16:c * 16 + 16] = q
        s = jnp.sum(q.astype(F32) * kn.astype(F32), axis=-1, keepdims=True) * scale
        m_s[c * 16:c * 16 + 16] = jnp.broadcast_to(s, (16, heads, 128))
        l_s[c * 16:c * 16 + 16] = jnp.ones((16, heads, 128), F32)
        acc[c * 16:c * 16 + 16] = vn.astype(F32)

    row = lax.broadcasted_iota(jnp.int32, (heads, wide), 0)
    col = lax.broadcasted_iota(jnp.int32, (heads, wide), 1)
    slot_of = jnp.where(lax.rem(col, heads) == row, col // heads, 1 << 20)

    def step(i, c):
        slot = lax.rem(i, RING)
        last = lax.rem(i + RING - 1, RING)
        par = lax.rem(i, 2)

        @pl.when(i < batches)
        def _():
            pltpu.make_async_copy(k_hbm.at[pl.ds(0, BATCH)], kbuf.at[slot], ksem.at[slot]).wait()

        @pl.when(i > 0)
        def _():
            pltpu.make_async_copy(v_hbm.at[pl.ds(0, BATCH)], vbuf.at[last], vsem.at[last]).wait()

        for g in range(BATCH):
            it = items[BATCH + i * BATCH + g]
            b = it // per
            left = lens[jnp.minimum(b, rows - 1)] - lax.rem(it, per) * SLOTS
            s = _dot(qb[b], kbuf[slot, g], NT) * scale
            sbuf[par, g] = jnp.where(slot_of < left, s, -jnp.inf)

        parts = []
        for g in range(0, BATCH, 2):
            ps = []
            for u in range(2):
                s = sbuf[1 - par, g + u]
                m = jnp.max(s, axis=1, keepdims=True)
                p = jnp.exp2(s - m)
                parts.append([m, jnp.sum(p, axis=1, keepdims=True), None])
                ps.append(p.astype(BF16))
            o = _dot(jnp.concatenate(ps, axis=0),
                     jnp.concatenate([vbuf[last, g], vbuf[last, g + 1]], axis=1))
            parts[g][2] = o[:heads, :d]
            parts[g + 1][2] = o[heads:, d:]
        for g in range(BATCH):
            b = items[i * BATCH + g] // per
            m, l, o = parts[g]
            m_old = m_s[b]
            m_new = jnp.maximum(m_old, m)
            w_old = jnp.exp2(m_old - m_new)
            w = jnp.exp2(m - m_new)
            m_s[b] = m_new
            l_s[b] = l_s[b] * w_old + l * w
            acc[b] = acc[b] * w_old + o * w

        @pl.when(i + RING - 1 < batches)
        def _():
            fetch(i + RING - 1)
        return c

    lax.fori_loop(0, batches + 1, step, 0)

    lane = lax.broadcasted_iota(jnp.int32, (16, 128), 1)
    for c in range(rows // 16):
        l = l_s[c * 16:c * 16 + 16]
        o = acc[c * 16:c * 16 + 16] / l
        lse = m_s[c * 16:c * 16 + 16] + jnp.log2(l)
        o_ref[:heads, c * 16:c * 16 + 16, :] = jnp.swapaxes(o, 0, 1)
        lse = jnp.swapaxes(lse, 0, 1)
        out = jnp.zeros((16, 128), F32)
        for h in range(heads):
            out = jnp.where(lane == h, lse[h], out)
        o_ref[heads, c * 16:c * 16 + 16, :] = out


def _suffix(lens, q, kn, vn, k, v, scale):
    heads, rows, d = q.shape
    slots = k.shape[1]
    per = slots // SLOTS
    wide = SLOTS * heads
    k = k.reshape(rows * per, wide, d)
    v = v.reshape(rows * per, wide, d)
    return pl.pallas_call(
        functools.partial(_suffix_kernel, scale),
        in_specs=[pl.BlockSpec(memory_space=pltpu.SMEM)] + [pl.BlockSpec(memory_space=VM)] * 3
        + [pl.BlockSpec(memory_space=pl.ANY)] * 2,
        out_specs=pl.BlockSpec(memory_space=VM),
        out_shape=jax.ShapeDtypeStruct((heads + 1, rows, d), F32),
        scratch_shapes=[
            pltpu.SMEM((rows * per + 4 * BATCH,), jnp.int32),
            VM((rows + 1, heads, d), BF16),
            VM((rows + 1, heads, d), F32),
            VM((rows + 1, heads, 128), F32),
            VM((rows + 1, heads, 128), F32),
            VM((RING, BATCH, wide, d), BF16),
            VM((RING, BATCH, wide, d), BF16),
            VM((2, BATCH, heads, wide), F32),
            pltpu.SemaphoreType.DMA((RING,)),
            pltpu.SemaphoreType.DMA((RING,)),
        ],
        compiler_params=pltpu.CompilerParams(vmem_limit_bytes=LIMIT),
        cost_estimate=_cost(2e10, 4 * k.size),
    )(lens, q, kn, vn, k, v)


def _weights(ls):
    m = functools.reduce(jnp.maximum, ls)
    ws = [jnp.exp2(l - m) for l in ls]
    t = functools.reduce(jnp.add, ws)
    return [w / t for w in ws]


def _half(w_hbm, other):
    half = w_hbm.shape[1] // 2
    me = lax.axis_index('tp')
    return w_hbm.at[:, pl.ds(pl.multiple_of((1 - me if other else me) * half, half), half)]


def _send_kernel(own_ref, near_ref, far_ref, suf_ref, w_hbm, att_ref, o0_ref, o1_ref, bufs, acc, sem):
    heads = own_ref.shape[0] - 1
    cols = o0_ref.shape[1]

    def emit(i):
        o0_ref[...] = acc[:, :cols].astype(BF16)
        o1_ref[...] = acc[:, cols:].astype(BF16)
    start, run = _stream(att_ref, [_half(w_hbm, True)], bufs, sem, acc, bufs.shape[1], emit)
    _prime(start, 8)
    far_lse = far_ref[heads].astype(F32) + far_ref[heads + 1].astype(F32) + far_ref[heads + 2].astype(F32)
    ws = _weights([own_ref[heads], near_ref[heads], far_lse, suf_ref[heads]])
    for h in range(heads):
        a = ws[0][:, h:h + 1] * own_ref[h]
        for w, r in zip(ws[1:], (near_ref, far_ref, suf_ref)):
            a += w[:, h:h + 1] * r[h].astype(F32)
        att_ref[:, h * 128:(h + 1) * 128] = a.astype(BF16)
    run()


def _keep_kernel(att_hbm, x_hbm, w_hbm, o0_ref, o1_ref, att_ref, x_ref, bufs, acc, xsem, sem):
    cols = o0_ref.shape[1]
    half = 2 * cols
    at = pl.multiple_of(lax.axis_index('tp') * half, half)
    cps = [pltpu.make_async_copy(att_hbm, att_ref, xsem.at[0]),
           pltpu.make_async_copy(x_hbm.at[:, pl.ds(at, half)], x_ref, xsem.at[1])]

    def emit(i):
        cps[1].wait()
        y = acc[...] + x_ref[...].astype(F32)
        o0_ref[...] = y[:, :cols]
        o1_ref[...] = y[:, cols:]
    start, run = _stream(att_ref, [_half(w_hbm, False)], bufs, sem, acc, bufs.shape[1], emit)
    for c in cps:
        c.start()
    _prime(start, 8)
    cps[0].wait()
    run()


def _out_send(own, near, far, suf, w_o):
    rows = own.shape[1]
    depth, cols = w_o.shape
    cols //= 2
    return pl.pallas_call(
        _send_kernel,
        in_specs=[pl.BlockSpec(memory_space=VM)] * 4 + [pl.BlockSpec(memory_space=pl.ANY)],
        out_specs=[pl.BlockSpec(memory_space=VM)] * 3,
        out_shape=[jax.ShapeDtypeStruct((rows, depth), BF16)] + [jax.ShapeDtypeStruct((rows, cols // 2), BF16)] * 2,
        scratch_shapes=[VM((RINGW, CHUNK, cols), BF16), VM((rows, cols), F32), pltpu.SemaphoreType.DMA((RINGW,))],
        compiler_params=pltpu.CompilerParams(vmem_limit_bytes=LIMIT),
        cost_estimate=_cost(2 * rows * depth * cols, 2 * depth * cols),
    )(own, near, far, suf, w_o)


def _out_keep(att, x, w_o):
    rows, depth = att.shape
    cols = w_o.shape[1] // 2
    return pl.pallas_call(
        _keep_kernel,
        in_specs=[pl.BlockSpec(memory_space=pl.ANY)] * 3,
        out_specs=[pl.BlockSpec(memory_space=VM)] * 2,
        out_shape=[jax.ShapeDtypeStruct((rows, cols // 2), F32)] * 2,
        scratch_shapes=[VM((rows, depth), BF16), VM((rows, cols), BF16), VM((RINGW, CHUNK, cols), BF16),
                        VM((rows, cols), F32), pltpu.SemaphoreType.DMA((2,)), pltpu.SemaphoreType.DMA((RINGW,))],
        compiler_params=pltpu.CompilerParams(vmem_limit_bytes=LIMIT),
        cost_estimate=_cost(2 * rows * depth * cols, 2 * depth * cols),
    )(att, x, w_o)


def solution(mesh):
    n_ctx = mesh.shape['ctx']
    row_axes = ('dp', 'ctx')
    chip_swap = [(i, i ^ 2) for i in range(n_ctx)]
    core_swap = [(i, i ^ 1) for i in range(n_ctx)]
    tp_swap = [(0, 1), (1, 0)]

    def device_step(hidden, w_q, w_k, w_v, w_o, k_prefix, v_prefix, k_suffix, v_suffix, seq_lens):
        scale = LOG2E * k_prefix.shape[2] ** -0.5
        far = lambda a: lax.ppermute(a, 'ctx', chip_swap)
        near = lambda a: lax.ppermute(a, 'ctx', core_swap)
        q = _project_q(hidden, w_q)
        q_far = far(q)
        q_near = near(q)
        kn, vn, kt, vt = _project_kv(hidden, w_k, w_v, k_prefix, v_prefix)
        q_far, kt = lax.optimization_barrier((q_far, kt))
        o_diag, o_far = _prefix(near(q_far), q_far, kt, vt, scale)
        o_diag, q_near = lax.optimization_barrier((o_diag, q_near))
        o_diag = near(o_diag)
        o_near, o_own = _prefix(q_near, q, kt, vt, scale)
        o_x = far(_merge(o_far, o_diag))
        o_near = near(o_near)
        o_suf = _suffix(seq_lens, q, kn, vn, k_suffix, v_suffix, scale)
        att, s0, s1 = _out_send(o_own, o_near, o_x, o_suf, w_o)
        swap = lambda a: lax.ppermute(a, 'tp', tp_swap)
        sent = [swap(s0), swap(s1)]
        kept = _out_keep(att, hidden, w_o)
        mine = [(a + b.astype(F32)).astype(BF16) for a, b in zip(kept, sent)]
        other = [swap(a) for a in mine]
        mine, other = jnp.concatenate(mine, axis=1), jnp.concatenate(other, axis=1)
        me = lax.axis_index('tp')
        return jnp.where(me == 0, jnp.concatenate([mine, other], axis=1), jnp.concatenate([other, mine], axis=1))

    spec_in = (P(row_axes, None), P(None, 'tp'), P(None, 'tp'), P(None, 'tp'), P('tp', None),
               P(row_axes, 'tp', None), P(row_axes, 'tp', None), P(row_axes, None, 'tp', None),
               P(row_axes, None, 'tp', None), P(row_axes))
    return jax.shard_map(device_step, mesh=mesh, in_specs=spec_in, out_specs=P(row_axes, None), check_vma=False)
```

time: 155 us -> 128 us (0.83)
  Pallas kernels: 116 us -> 97.6 us
  waiting for transfers between devices: 19.8 us -> 11.9 us
    pallas_call x10 -> x6, Pallas kernels: 87.1 us -> 73.8 us  [the longest x2 30.7 us: _prefix(): pl.pallas_call(functools.partial(_prefix_kernel, scale), grid=(heads // g...]
    ppermute x3 -> x2, waiting for transfers between devices: 11.9 us -> 0.01 us  [device_step(): far = lambda a: lax.ppermute(a, 'ctx', chip_swap)]
    pallas_call x1, Pallas kernels: 26.3 us -> 20.7 us  [_suffix(): pl.pallas_call(functools.partial(_suffix_kernel, scale), in_specs=[pl.Blo...]
    ppermute x4, waiting for transfers between devices: 7.9 us -> 10.5 us  [device_step(): swap = lambda a: lax.ppermute(a, 'tp', tp_swap)]
    ppermute x4, starting transfers between devices: 4.09 us -> 6.05 us  [device_step(): swap = lambda a: lax.ppermute(a, 'tp', tp_swap)]
    ppermute x3 -> x2, starting transfers between devices: 5.37 us -> 3.42 us  [device_step(): far = lambda a: lax.ppermute(a, 'ctx', chip_swap)]
    unnamed x24 -> x14, local copies, waits for them, and re-layouts: 3.71 us -> 3.62 us
  transfers between devices with their start and end apart: 13 -> 10, of which waited for: 3 -> 5; matrix products, arithmetic and copies ran while one was open for 1% -> 2% of each run, Pallas kernels for 54% -> 64%
where the time goes in v2:
time: 128 us; the launch traced here: 127 us
  Pallas kernels  97.6 us (76%)
  waiting for transfers between devices  11.9 us (9%)
  starting transfers between devices  10.3 us (8%)
  local copies, waits for them, and re-layouts  3.62 us (3%)
  other arithmetic  3.4 us (3%)
    pallas_call x2, Pallas kernels, _prefix(): pl.pallas_call(functools.partial(_prefix_kernel, scale), grid=(heads // g...  30.7 us
    pallas_call x1, Pallas kernels, _suffix(): pl.pallas_call(functools.partial(_suffix_kernel, scale), in_specs=[pl.Blo...  20.7 us
    pallas_call x1, Pallas kernels, _project_kv(): pl.pallas_call(_kv_kernel, in_specs=[pl.BlockSpec(memory_space=pl.ANY)] *...  20.2 us
    ppermute x4, waiting for transfers between devices, device_step(): swap = lambda a: lax.ppermute(a, 'tp', tp_swap)  10.5 us
    pallas_call x1, Pallas kernels, _project_q(): pl.pallas_call(_q_kernel, in_specs=[pl.BlockSpec(memory_space=pl.ANY)] *...  9.22 us
    pallas_call x1, Pallas kernels, _out_send(): pl.pallas_call(_send_kernel, in_specs=[pl.BlockSpec(memory_space=VM)] * 4...  7.72 us
    ppermute x4, starting transfers between devices, device_step(): swap = lambda a: lax.ppermute(a, 'tp', tp_swap)  6.05 us
    pallas_call x1, Pallas kernels, _out_keep(): pl.pallas_call(_keep_kernel, in_specs=[pl.BlockSpec(memory_space=pl.ANY)]...  5.98 us
  transfers between devices with their start and end apart: 10, of which 5 were waited for; matrix products, arithmetic and copies ran while one was open for 2% of the time, Pallas kernels for 64%

profile of v2, /device:TPU:0, one launch (start us, length us, event | category | flops | bytes accessed | tf_op | source)
XLA Modules:
  0.0 126.9 jit_solution(315631051476731541)
XLA Ops:
  0.0 9.2 %shard_map.100.q1_ref.q_ref = bf16[16,128,128]{2,1,0:T(8,128)(2,1)} custom-call(bf16[128,4096]{1,0:T(8,128)(2,1)} %x_hbm.5, bf16[4096,2048]{1,0:T(8,128)(2,1)} %w_hbm.3), custom_call_target="tpu_custom_call" | custom-call | flops 2147483648 | bytes 16777216 | tf_op jit(solution)/shard_map/pallas_call | solution.py:99
  9.2 0.0 copy-start
  9.2 3.4 %collective-permute-start = (bf16[16,128,128]{2,1,0:T(8,128)(2,1)}, bf16[16,128,128]{2,1,0:T(8,128)(2,1)S(1)}, u32[]{:S(2)}, u32[]{:S(2)}) collective-permute-start(bf16[16,128,128]{2,1,0:T(8,128)(2,1)} %shard_map.100.q1_ref.q_ref), channel_id=1, source_target_pairs={{0,2},{1,3},{2,0},{3,1},{4,6},{5,7},{6,4},{7,5}} | collective-permute-start | bytes 1572872 | tf_op jit(solution)/shard_map/ppermute | solution.py:479
  12.6 20.2 %shard_map.101 = (bf16[16,128,128]{2,1,0:T(8,128)(2,1)}, bf16[16,128,128]{2,1,0:T(8,128)(2,1)}, bf16[16,1024,128]{2,1,0:T(8,128)(2,1)}, bf16[16,1024,128]{2,1,0:T(8,128)(2,1)}) custom-call(bf16[128,4096]{1,0:T(8,128)(2,1)} %x_hbm.5, bf16[4096,2048]{1,0:T(8,128)(2,1)} %wk_hbm.1, bf16[4096,2048]{1,0:T(8,128)(2,1)} %wv_hbm.1, bf16[1024,16,128]{2,1,0:T(8,128)(2,1)} %kp_hbm.1, ...), custom_call_target="tpu_custom_call" | custom-call | flops 20000000000 | bytes 33554432 | tf_op jit(solution)/shard_map/pallas_call | solution.py:161
  32.8 0.0 collective-permute-done.q1_ref
  32.8 0.0 copy-start.3
  32.8 0.0 collective-permute-start.1
  32.8 0.0 copy-done
  32.8 0.5 collective-permute-start.2
  33.3 1.4 %collective-permute-done.1.q0_ref = bf16[16,128,128]{2,1,0:T(8,128)(2,1)S(1)} collective-permute-done((bf16[16,128,128]{2,1,0:T(8,128)(2,1)S(1)}, bf16[16,128,128]{2,1,0:T(8,128)(2,1)S(1)}, u32[]{:S(2)}, u32[]{:S(2)}) %collective-permute-start.1) | collective-permute-done | bytes 524320 | tf_op jit(solution)/shard_map/ppermute | solution.py:480
  34.7 0.0 copy-start.5
  34.7 0.0 copy-done.3
  34.7 0.8 copy-done.5
  35.5 15.3 %shard_map.102 = (f32[17,128,128]{2,1,0:T(8,128)}, f32[17,128,128]{2,1,0:T(8,128)}) custom-call(bf16[16,128,128]{2,1,0:T(8,128)(2,1)} %copy-done.5, bf16[16,128,128]{2,1,0:T(8,128)(2,1)} %copy-done.3, bf16[16,1024,128]{2,1,0:T(8,128)(2,1)} %get-tuple-element.24.k_ref, bf16[16,1024,128]{2,1,0:T(8,128)(2,1)} %get-tuple-element.25.v_ref), custom_call_target="tpu_custom_call" | custom-call | flops 2147483648 | bytes 8388608 | tf_op jit(solution)/shard_map/pallas_call | solution.py:210
  50.8 0.0 collective-permute-done.2.q0_ref
  50.8 0.0 copy-start.4
  50.8 0.2 collective-permute-start.4
  51.0 0.6 copy-done.4
  51.6 15.4 %shard_map.103 = (f32[17,128,128]{2,1,0:T(8,128)}, f32[17,128,128]{2,1,0:T(8,128)}) custom-call(bf16[16,128,128]{2,1,0:T(8,128)(2,1)} %copy-done.4, bf16[16,128,128]{2,1,0:T(8,128)(2,1)} %shard_map.100.q1_ref.q_ref, bf16[16,1024,128]{2,1,0:T(8,128)(2,1)} %get-tuple-element.24.k_ref, bf16[16,1024,128]{2,1,0:T(8,128)(2,1)} %get-tuple-element.25.v_ref), custom_call_target="tpu_custom_call" | custom-call | flops 2147483648 | bytes 8388608 | tf_op jit(solution)/shard_map/pallas_call | solution.py:210
  67.0 0.1 collective-permute-start.3
  67.1 0.0 collective-permute-done.4.b_ref
  67.1 0.0 copy-start.6
  67.1 1.0 copy-done.6
  68.2 3.1 %shard_map.104 = bf16[19,128,128]{2,1,0:T(8,128)(2,1)} custom-call(f32[17,128,128]{2,1,0:T(8,128)} %get-tuple-element.30.a_ref, f32[17,128,128]{2,1,0:T(8,128)} %copy-done.6), custom_call_target="tpu_custom_call" | custom-call | flops 1000000000 | bytes 2785280 | tf_op jit(solution)/shard_map/pallas_call | solution.py:239
  71.2 0.1 collective-permute-start.5
  71.3 20.7 %shard_map.105.suf_ref = f32[17,128,128]{2,1,0:T(8,128)} custom-call(s32[128]{0:T(128)} %lens.1, bf16[16,128,128]{2,1,0:T(8,128)(2,1)} %shard_map.100.q1_ref.q_ref, bf16[16,128,128]{2,1,0:T(8,128)(2,1)} %get-tuple-element.32.kn_ref, bf16[16,128,128]{2,1,0:T(8,128)(2,1)} %get-tuple-element.33.vn_ref, bf16[512,256,128]{2,1,0:T(8,128)(2,1)} %bitcast.2, ...), custom_call_target="tpu_custom_call" | custom-call | flops 20000000000 | bytes 67108864 | tf_op jit(solution)/shard_map/pallas_call | solution.py:365
  92.0 0.0 collective-permute-done.3.near_ref
  92.1 0.0 copy-start.1
  92.1 0.0 collective-permute-done.5.far_ref
  92.1 0.0 copy-start.2
  92.1 1.0 copy-done.1
  93.0 0.2 copy-done.2
  93.2 7.7 %shard_map.106 = (bf16[128,2048]{1,0:T(8,128)(2,1)}, bf16[128,1024]{1,0:T(8,128)(2,1)}, bf16[128,1024]{1,0:T(8,128)(2,1)}) custom-call(f32[17,128,128]{2,1,0:T(8,128)} %get-tuple-element.28.own_ref, f32[17,128,128]{2,1,0:T(8,128)} %copy-done.1, bf16[19,128,128]{2,1,0:T(8,128)(2,1)} %copy-done.2, f32[17,128,128]{2,1,0:T(8,128)} %shard_map.105.suf_ref, ...), custom_call_target="tpu_custom_call" | custom-call | flops 1073741824 | bytes 8388608 | tf_op jit(solution)/shard_map/pallas_call | solution.py:444
  101.0 2.0 %collective-permute-start.6 = (bf16[128,1024]{1,0:T(8,128)(2,1)}, bf16[128,1024]{1,0:T(8,128)(2,1)S(1)}, u32[]{:S(2)}, u32[]{:S(2)}) collective-permute-start(bf16[128,1024]{1,0:T(8,128)(2,1)} %get-tuple-element.36), channel_id=1, source_target_pairs={{0,4},{4,0},{1,5},{5,1},{2,6},{6,2},{3,7},{7,3}} | collective-permute-start | bytes 786440 | tf_op jit(solution)/shard_map/ppermute | solution.py:494
  103.0 0.0 collective-permute-start.7
  103.0 6.0 %shard_map.107 = (f32[128,1024]{1,0:T(8,128)}, f32[128,1024]{1,0:T(8,128)}) custom-call(bf16[128,2048]{1,0:T(8,128)(2,1)} %get-tuple-element.34.att_hbm, bf16[128,4096]{1,0:T(8,128)(2,1)} %x_hbm.5, bf16[2048,4096]{1,0:T(8,128)(2,1)} %w_hbm.5), custom_call_target="tpu_custom_call" | custom-call | flops 1073741824 | bytes 8388608 | tf_op jit(solution)/shard_map/pallas_call | solution.py:458
  109.0 1.2 collective-permute-done.6
  110.2 1.1 add_convert_fusion.1
  111.3 2.0 %collective-permute-start.8 = (bf16[128,1024]{1,0:T(8,128)(2,1)S(1)}, bf16[128,1024]{1,0:T(8,128)(2,1)S(1)}, u32[]{:S(2)}, u32[]{:S(2)}) collective-permute-start(bf16[128,1024]{1,0:T(8,128)(2,1)S(1)} %add_convert_fusion.1), channel_id=1, source_target_pairs={{0,4},{4,0},{1,5},{5,1},{2,6},{6,2},{3,7},{7,3}} | collective-permute-start | bytes 786440 | tf_op jit(solution)/shard_map/ppermute | solution.py:494
  113.3 2.5 %collective-permute-done.7 = bf16[128,1024]{1,0:T(8,128)(2,1)S(1)} collective-permute-done((bf16[128,1024]{1,0:T(8,128)(2,1)}, bf16[128,1024]{1,0:T(8,128)(2,1)S(1)}, u32[]{:S(2)}, u32[]{:S(2)}) %collective-permute-start.7) | collective-permute-done | bytes 262176 | tf_op jit(solution)/shard_map/ppermute | solution.py:494
  115.8 1.1 add_convert_fusion
  116.9 2.0 %collective-permute-start.9 = (bf16[128,1024]{1,0:T(8,128)(2,1)S(1)}, bf16[128,1024]{1,0:T(8,128)(2,1)S(1)}, u32[]{:S(2)}, u32[]{:S(2)}) collective-permute-start(bf16[128,1024]{1,0:T(8,128)(2,1)S(1)} %add_convert_fusion), channel_id=1, source_target_pairs={{0,4},{4,0},{1,5},{5,1},{2,6},{6,2},{3,7},{7,3}} | collective-permute-start | bytes 786440 | tf_op jit(solution)/shard_map/ppermute | solution.py:494
  118.9 2.5 %collective-permute-done.8 = bf16[128,1024]{1,0:T(8,128)(2,1)S(1)} collective-permute-done((bf16[128,1024]{1,0:T(8,128)(2,1)S(1)}, bf16[128,1024]{1,0:T(8,128)(2,1)S(1)}, u32[]{:S(2)}, u32[]{:S(2)}) %collective-permute-start.8) | collective-permute-done | bytes 262176 | tf_op jit(solution)/shard_map/ppermute | solution.py:494
  121.4 4.3 %collective-permute-done.9 = bf16[128,1024]{1,0:T(8,128)(2,1)S(1)} collective-permute-done((bf16[128,1024]{1,0:T(8,128)(2,1)S(1)}, bf16[128,1024]{1,0:T(8,128)(2,1)S(1)}, u32[]{:S(2)}, u32[]{:S(2)}) %collective-permute-start.9) | collective-permute-done | bytes 262176 | tf_op jit(solution)/shard_map/ppermute | solution.py:494
  125.7 1.2 maximum_select_fusion
Async XLA Ops:
  9.2 23.6 %copy-start = (bf16[16,128,128]{2,1,0:T(8,128)(2,1)S(1)}, bf16[16,128,128]{2,1,0:T(8,128)(2,1)}, u32[]{:S(2)}) copy-start(bf16[16,128,128]{2,1,0:T(8,128)(2,1)} %shard_map.100.q1_ref.q_ref) | copy-start | bytes 1572868
  9.2 23.5 %collective-permute-start = (bf16[16,128,128]{2,1,0:T(8,128)(2,1)}, bf16[16,128,128]{2,1,0:T(8,128)(2,1)S(1)}, u32[]{:S(2)}, u32[]{:S(2)}) collective-permute-start(bf16[16,128,128]{2,1,0:T(8,128)(2,1)} %shard_map.100.q1_ref.q_ref), channel_id=1, source_target_pairs={{0,2},{1,3},{2,0},{3,1},{4,6},{5,7},{6,4},{7,5}} | collective-permute-start | bytes 1572872 | tf_op jit(solution)/shard_map/ppermute | solution.py:479
  32.8 1.9 %copy-start.3 = (bf16[16,128,128]{2,1,0:T(8,128)(2,1)}, bf16[16,128,128]{2,1,0:T(8,128)(2,1)S(1)}, u32[]{:S(2)}) copy-start(bf16[16,128,128]{2,1,0:T(8,128)(2,1)S(1)} %collective-permute-done.q1_ref) | copy-start | bytes 1572868
  32.8 1.9 %collective-permute-start.1 = (bf16[16,128,128]{2,1,0:T(8,128)(2,1)S(1)}, bf16[16,128,128]{2,1,0:T(8,128)(2,1)S(1)}, u32[]{:S(2)}, u32[]{:S(2)}) collective-permute-start(bf16[16,128,128]{2,1,0:T(8,128)(2,1)S(1)} %collective-permute-done.q1_ref), channel_id=1, source_target_pairs={{0,1},{1,0},{2,3},{3,2},{4,5},{5,4},{6,7},{7,6}} | collective-permute-start | bytes 1572872 | tf_op jit(solution)/shard_map/ppermute | solution.py:480
  32.8 18.0 %collective-permute-start.2 = (bf16[16,128,128]{2,1,0:T(8,128)(2,1)S(1)}, bf16[16,128,128]{2,1,0:T(8,128)(2,1)S(1)}, u32[]{:S(2)}, u32[]{:S(2)}) collective-permute-start(bf16[16,128,128]{2,1,0:T(8,128)(2,1)S(1)} %copy-done), channel_id=1, source_target_pairs={{0,1},{1,0},{2,3},{3,2},{4,5},{5,4},{6,7},{7,6}} | collective-permute-start | bytes 1572872 | tf_op jit(solution)/shard_map/ppermute | solution.py:480
  34.7 0.8 copy-start.5
  50.8 0.8 copy-start.4
  50.8 16.3 %collective-permute-start.4 = (f32[17,128,128]{2,1,0:T(8,128)}, f32[17,128,128]{2,1,0:T(8,128)S(1)}, u32[]{:S(2)}, u32[]{:S(2)}) collective-permute-start(f32[17,128,128]{2,1,0:T(8,128)} %get-tuple-element.31), channel_id=1, source_target_pairs={{0,1},{1,0},{2,3},{3,2},{4,5},{5,4},{6,7},{7,6}} | collective-permute-start | bytes 3342344 | tf_op jit(solution)/shard_map/ppermute | solution.py:480
  67.0 25.0 %collective-permute-start.3 = (f32[17,128,128]{2,1,0:T(8,128)}, f32[17,128,128]{2,1,0:T(8,128)S(1)}, u32[]{:S(2)}, u32[]{:S(2)}) collective-permute-start(f32[17,128,128]{2,1,0:T(8,128)} %get-tuple-element.29), channel_id=1, source_target_pairs={{0,1},{1,0},{2,3},{3,2},{4,5},{5,4},{6,7},{7,6}} | collective-permute-start | bytes 3342344 | tf_op jit(solution)/shard_map/ppermute | solution.py:480
  67.1 1.0 copy-start.6
  71.2 20.8 %collective-permute-start.5 = (bf16[19,128,128]{2,1,0:T(8,128)(2,1)}, bf16[19,128,128]{2,1,0:T(8,128)(2,1)S(1)}, u32[]{:S(2)}, u32[]{:S(2)}) collective-permute-start(bf16[19,128,128]{2,1,0:T(8,128)(2,1)} %shard_map.104), channel_id=1, source_target_pairs={{0,2},{1,3},{2,0},{3,1},{4,6},{5,7},{6,4},{7,5}} | collective-permute-start | bytes 1867784 | tf_op jit(solution)/shard_map/ppermute | solution.py:479
  92.1 1.0 copy-start.1
  92.1 1.2 copy-start.2
  101.0 9.2 %collective-permute-start.6 = (bf16[128,1024]{1,0:T(8,128)(2,1)}, bf16[128,1024]{1,0:T(8,128)(2,1)S(1)}, u32[]{:S(2)}, u32[]{:S(2)}) collective-permute-start(bf16[128,1024]{1,0:T(8,128)(2,1)} %get-tuple-element.36), channel_id=1, source_target_pairs={{0,4},{4,0},{1,5},{5,1},{2,6},{6,2},{3,7},{7,3}} | collective-permute-start | bytes 786440 | tf_op jit(solution)/shard_map/ppermute | solution.py:494
  103.0 12.8 %collective-permute-start.7 = (bf16[128,1024]{1,0:T(8,128)(2,1)}, bf16[128,1024]{1,0:T(8,128)(2,1)S(1)}, u32[]{:S(2)}, u32[]{:S(2)}) collective-permute-start(bf16[128,1024]{1,0:T(8,128)(2,1)} %get-tuple-element.38), channel_id=1, source_target_pairs={{0,4},{4,0},{1,5},{5,1},{2,6},{6,2},{3,7},{7,3}} | collective-permute-start | bytes 786440 | tf_op jit(solution)/shard_map/ppermute | solution.py:494
  111.3 10.1 %collective-permute-start.8 = (bf16[128,1024]{1,0:T(8,128)(2,1)S(1)}, bf16[128,1024]{1,0:T(8,128)(2,1)S(1)}, u32[]{:S(2)}, u32[]{:S(2)}) collective-permute-start(bf16[128,1024]{1,0:T(8,128)(2,1)S(1)} %add_convert_fusion.1), channel_id=1, source_target_pairs={{0,4},{4,0},{1,5},{5,1},{2,6},{6,2},{3,7},{7,3}} | collective-permute-start | bytes 786440 | tf_op jit(solution)/shard_map/ppermute | solution.py:494
  116.9 8.8 %collective-permute-start.9 = (bf16[128,1024]{1,0:T(8,128)(2,1)S(1)}, bf16[128,1024]{1,0:T(8,128)(2,1)S(1)}, u32[]{:S(2)}, u32[]{:S(2)}) collective-permute-start(bf16[128,1024]{1,0:T(8,128)(2,1)S(1)} %add_convert_fusion), channel_id=1, source_target_pairs={{0,4},{4,0},{1,5},{5,1},{2,6},{6,2},{3,7},{7,3}} | collective-permute-start | bytes 786440 | tf_op jit(solution)/shard_map/ppermute | solution.py:494

commit v3 on v2

v3 whole, which is shorter than its diff:
```python
import functools

import jax
import jax.numpy as jnp
from jax import lax
from jax.experimental import pallas as pl
from jax.experimental.pallas import tpu as pltpu
from jax.sharding import PartitionSpec as P

F32 = jnp.float32
BF16 = jnp.bfloat16
VM = pltpu.VMEM
LOG2E = 1.4426950408889634
BATCH = 16
SLOTS = 16
RING = 5
CHUNK = 512
RINGW = 5
LIMIT = 56 * 2**20


def _cost(flops, nbytes):
    return pl.CostEstimate(flops=int(flops), bytes_accessed=int(nbytes), transcendentals=0)


def _dot(a, b, dims=(((1,), (0,)), ((), ()))):
    return lax.dot_general(a, b, dims, preferred_element_type=F32)


NT = (((1,), (1,)), ((), ()))


MESH = pl.DeviceIdType.MESH


def _stream(x_ref, ws, bufs, sem, acc, emit, extra_start=None, extra_body=None):
    ring, chunk, cols = bufs.shape
    n = ws[0].shape[0] // chunk
    total = n * len(ws)
    part = 512

    def start(g):
        slot = lax.rem(g, ring)
        for i, w in enumerate(ws):
            @pl.when((g >= i * n) & (g < (i + 1) * n))
            def _():
                at = pl.multiple_of((g - i * n) * chunk, chunk)
                pltpu.make_async_copy(w.at[pl.ds(at, chunk)], bufs.at[slot], sem.at[slot]).start()
        if extra_start is not None:
            extra_start(g)

    def prime():
        def body(g, c):
            start(g)
            return c
        lax.fori_loop(0, min(ring, total), body, 0)

    def run():
        for i, w in enumerate(ws):
            acc[...] = jnp.zeros_like(acc)

            def body(c, carry):
                g = i * n + c
                slot = lax.rem(g, ring)
                pltpu.make_async_copy(w.at[pl.ds(0, chunk)], bufs.at[slot], sem.at[slot]).wait()
                x = x_ref[:, pl.ds(pl.multiple_of(c * chunk, chunk), chunk)]
                for j in range(0, cols, part):
                    acc[:, j:j + part] += _dot(x, bufs[slot, :, j:j + part])
                if extra_body is not None:
                    extra_body(i, g)
                start(g + ring)
                return carry
            lax.fori_loop(0, n, body, 0)
            emit(i)
    return prime, run


def _front_kernel(scale, x_hbm, wq_hbm, wk_hbm, wv_hbm, kp_hbm, vp_hbm, q_hbm, kn_hbm, vn_hbm, out_ref,
                  x_ref, bufs, acc, raw, kt, vt, qs, kvn, ds, dr, ns, nr, fo, wo, xs, xr, xl, xlr,
                  xsem, sem, psem, osem, q_s, q_r, d_s, d_r, n_s, n_r, x_s, x_r):
    heads, n_pos, d = kt.shape
    rows = x_ref.shape[0]
    ring, chunk, _ = bufs.shape
    me = lax.axis_index('ctx')
    near = me + 1 - 2 * lax.rem(me, 2)
    far = me + 2 - 4 * (me // 2)
    n = x_hbm.shape[1] // chunk
    pos = n_pos // (2 * n)

    cp = pltpu.make_async_copy(x_hbm, x_ref, xsem)
    cp.start()

    def remote(src, dst, s, r, to):
        return pltpu.make_async_remote_copy(src_ref=src, dst_ref=dst, send_sem=s, recv_sem=r,
                                            device_id={'ctx': to}, device_id_type=MESH)

    hh = heads // 2
    q_near = remote(qs.at[0], qs.at[1], q_s.at[0], q_r.at[0], near)
    q_far = [remote(qs.at[0, pl.ds(j * hh, hh)], qs.at[2, pl.ds(j * hh, hh)], q_s.at[1 + j], q_r.at[1 + j], far)
             for j in range(2)]
    q_diag = [remote(qs.at[2, pl.ds(j * hh, hh)], qs.at[3, pl.ds(j * hh, hh)], q_s.at[3 + j], q_r.at[3 + j], near)
              for j in range(2)]
    outs = [pltpu.make_async_copy(qs.at[0], q_hbm, osem.at[0]),
            pltpu.make_async_copy(kvn.at[0], kn_hbm, osem.at[1]),
            pltpu.make_async_copy(kvn.at[1], vn_hbm, osem.at[2])]

    def pieces(g):
        at = pl.ds((g - n) * pos, pos)
        slot = lax.rem(g, ring)
        return [pltpu.make_async_copy(src.at[at], raw.at[slot, j], psem.at[slot, j])
                for j, src in enumerate((kp_hbm, vp_hbm))]

    def extra_start(g):
        @pl.when((g >= n) & (g < 3 * n))
        def _():
            for c in pieces(g):
                c.start()

    def extra_body(i, g):
        if i == 0:
            return
        slot = lax.rem(g, ring)
        for c in pieces(g):
            c.wait()
        for j, dst in enumerate((kt, vt)):
            for u in range(pos // 16):
                at = pl.multiple_of((g - n) * pos + u * 16, 16)
                dst[:, pl.ds(at, 16), :] = jnp.swapaxes(raw[slot, j, u * 16:u * 16 + 16], 0, 1)

    def emit(i):
        dst = qs.at[0] if i == 0 else kvn.at[i - 1]
        for h in range(heads):
            dst[h] = acc[:, h * d:(h + 1) * d].astype(BF16)
        if i == 0:
            pl.semaphore_wait(barrier, 2)
            for c in (q_far[0], q_far[1], q_near):
                c.start()
        outs[i].start()

    prime, run = _stream(x_ref, [wq_hbm, wk_hbm, wv_hbm], bufs, sem, acc, emit, extra_start, extra_body)
    prime()
    barrier = pltpu.get_barrier_semaphore()
    for to in (near, far):
        pl.semaphore_signal(barrier, inc=1, device_id={'ctx': to}, device_id_type=MESH)
    cp.wait()
    run()

    for j in range(2):
        q_far[j].wait_recv()
        q_diag[j].start()

    lane = lax.broadcasted_iota(jnp.int32, (rows, d), 1)
    group = 2
    steps = heads // group

    def attend(units):
        for qi, h, dst in units:
            s = _dot(qs[qi, h], kt[h], NT)
            m = jnp.max(s, axis=1, keepdims=True) * scale
            e = jnp.exp2(s * scale - m)
            l = jnp.sum(e, axis=1, keepdims=True)
            o = _dot(e.astype(BF16), vt[h])
            dst[h, 0] = o / l
            dst[h, 1] = jnp.broadcast_to(m + jnp.log2(l), (rows, d))

    def d_copy(i):
        at = pl.ds(i * group, group)
        return remote(ds.at[at], dr.at[at], d_s.at[i], d_r.at[i], near)

    def n_copy(i):
        at = pl.ds(i * group, group)
        return remote(ns.at[at], nr.at[at], n_s.at[i], n_r.at[i], near)

    def x_copy(i):
        at = pl.ds(i * group, group)
        return remote(xs.at[at], xr.at[at], x_s.at[i], x_r.at[i], far)

    xl_copy = remote(xl, xlr, x_s.at[steps], x_r.at[steps], far)

    def merge_far(i):
        d_copy(i).wait_recv()
        for u in range(group):
            h = i * group + u
            l0, l1 = fo[h, 1], dr[h, 1]
            m = jnp.maximum(l0, l1)
            w0, w1 = jnp.exp2(l0 - m), jnp.exp2(l1 - m)
            t = w0 + w1
            xs[h] = ((w0 * fo[h, 0] + w1 * dr[h, 0]) / t).astype(BF16)
            xl[...] = jnp.where(lane == h, m + jnp.log2(t), xl[...])
        x_copy(i).start()

    q_diag[0].wait_recv()
    q_diag[1].wait_recv()
    xl[...] = jnp.zeros_like(xl)

    def far_step(i, c):
        attend([(qi, i * group + u, dst) for u in range(group) for qi, dst in ((3, ds), (2, fo))])
        d_copy(i).start()

        @pl.when(i > 0)
        def _():
            merge_far(i - 1)
        return c
    lax.fori_loop(0, steps, far_step, 0)

    q_near.wait_recv()

    def near_step(i, c):
        attend([(qi, i * group + u, dst) for u in range(group) for qi, dst in ((1, ns), (0, wo))])
        n_copy(i).start()

        @pl.when(i == 0)
        def _():
            merge_far(steps - 1)
            xl_copy.start()
        return c
    lax.fori_loop(0, steps, near_step, 0)

    xl_copy.wait_recv()
    far_lse = xlr[...]
    lse_out = jnp.zeros((rows, d), F32)
    for h in range(heads):
        if h % group == 0:
            n_copy(h // group).wait_recv()
            x_copy(h // group).wait_recv()
        l0, l1, l2 = wo[h, 1], nr[h, 1], jnp.broadcast_to(far_lse[:, h:h + 1], (rows, d))
        m = jnp.maximum(jnp.maximum(l0, l1), l2)
        w0, w1, w2 = jnp.exp2(l0 - m), jnp.exp2(l1 - m), jnp.exp2(l2 - m)
        t = w0 + w1 + w2
        out_ref[h] = (w0 * wo[h, 0] + w1 * nr[h, 0] + w2 * xr[h].astype(F32)) / t
        lse_out = jnp.where(lane == h, m + jnp.log2(t), lse_out)
    out_ref[heads] = lse_out

    for c in outs:
        c.wait()
    for c in [q_near] + q_far + q_diag + [xl_copy]:
        c.wait_send()

    def drain(i, c):
        d_copy(i).wait_send()
        n_copy(i).wait_send()
        x_copy(i).wait_send()
        return c
    lax.fori_loop(0, steps, drain, 0)


def _front(x, wq, wk, wv, kp, vp, scale):
    rows, depth = x.shape
    cols = wq.shape[1]
    n, heads, d = kp.shape
    pos = n // (2 * depth // CHUNK)
    dma = pltpu.SemaphoreType.DMA
    blk = (heads, rows, d)
    pair = (heads, 2, rows, d)
    return pl.pallas_call(
        functools.partial(_front_kernel, scale),
        in_specs=[pl.BlockSpec(memory_space=pl.ANY)] * 6,
        out_specs=[pl.BlockSpec(memory_space=pl.ANY)] * 3 + [pl.BlockSpec(memory_space=VM)],
        out_shape=[jax.ShapeDtypeStruct(blk, BF16)] * 3 + [jax.ShapeDtypeStruct((heads + 1, rows, d), F32)],
        scratch_shapes=[
            VM((rows, depth), BF16), VM((RINGW, CHUNK, cols), BF16), VM((rows, cols), F32),
            VM((RINGW, 2, pos, heads, d), BF16), VM((heads, n, d), BF16), VM((heads, n, d), BF16),
            VM((4,) + blk, BF16), VM((2,) + blk, BF16),
            VM(pair, F32), VM(pair, F32), VM(pair, F32), VM(pair, F32), VM(pair, F32), VM(pair, F32),
            VM(blk, BF16), VM(blk, BF16), VM((rows, d), F32), VM((rows, d), F32),
            dma, dma((RINGW,)), dma((RINGW, 2)), dma((3,)), dma((5,)), dma((5,)),
            dma((heads // 2,)), dma((heads // 2,)), dma((heads // 2,)), dma((heads // 2,)),
            dma((heads // 2 + 1,)), dma((heads // 2 + 1,))],
        compiler_params=pltpu.CompilerParams(vmem_limit_bytes=LIMIT, collective_id=0, has_side_effects=True),
        cost_estimate=_cost(5e10, 6 * depth * cols),
    )(x, wq, wk, wv, kp, vp)


def _suffix_kernel(scale, lens, q_ref, kn_ref, vn_ref, k_hbm, v_hbm, o_ref,
                   items, qb, acc, m_s, l_s, kbuf, vbuf, sbuf, ksem, vsem):
    heads, rows, d = q_ref.shape
    per = k_hbm.shape[0] // rows
    wide = SLOTS * heads
    dummy = rows * per

    for g in range(BATCH):
        items[g] = dummy

    def listing(b, t):
        for j in range(per):
            items[BATCH + t + j] = b * per + j
        return t + (lens[b] + SLOTS - 1) // SLOTS
    total = lax.fori_loop(0, rows, listing, 0)
    for g in range(2 * BATCH):
        items[BATCH + total + g] = dummy
    batches = (total + BATCH - 1) // BATCH

    def fetch(i):
        slot = lax.rem(i, RING)
        for g in range(BATCH):
            it = jnp.minimum(items[BATCH + i * BATCH + g], dummy - 1)
            pltpu.make_async_copy(k_hbm.at[it], kbuf.at[slot, g], ksem.at[slot]).start()
            pltpu.make_async_copy(v_hbm.at[it], vbuf.at[slot, g], vsem.at[slot]).start()

    def prime(i, c):
        fetch(i)
        return c
    lax.fori_loop(0, jnp.minimum(batches, RING - 1), prime, 0)

    for c in range(rows // 16):
        q = jnp.swapaxes(q_ref[:, c * 16:c * 16 + 16, :], 0, 1)
        kn = jnp.swapaxes(kn_ref[:, c * 16:c * 16 + 16, :], 0, 1)
        vn = jnp.swapaxes(vn_ref[:, c * 16:c * 16 + 16, :], 0, 1)
        qb[c * 16:c * 16 + 16] = q
        s = jnp.sum(q.astype(F32) * kn.astype(F32), axis=-1, keepdims=True) * scale
        m_s[c * 16:c * 16 + 16] = jnp.broadcast_to(s, (16, heads, 128))
        l_s[c * 16:c * 16 + 16] = jnp.ones((16, heads, 128), F32)
        acc[c * 16:c * 16 + 16] = vn.astype(F32)

    row = lax.broadcasted_iota(jnp.int32, (heads, wide), 0)
    col = lax.broadcasted_iota(jnp.int32, (heads, wide), 1)
    slot_of = jnp.where(lax.rem(col, heads) == row, col // heads, 1 << 20)

    def step(i, c):
        slot = lax.rem(i, RING)
        last = lax.rem(i + RING - 1, RING)
        par = lax.rem(i, 2)

        @pl.when(i < batches)
        def _():
            pltpu.make_async_copy(k_hbm.at[pl.ds(0, BATCH)], kbuf.at[slot], ksem.at[slot]).wait()

        @pl.when(i > 0)
        def _():
            pltpu.make_async_copy(v_hbm.at[pl.ds(0, BATCH)], vbuf.at[last], vsem.at[last]).wait()

        for g in range(BATCH):
            it = items[BATCH + i * BATCH + g]
            b = it // per
            left = lens[jnp.minimum(b, rows - 1)] - lax.rem(it, per) * SLOTS
            s = _dot(qb[b], kbuf[slot, g], NT) * scale
            sbuf[par, g] = jnp.where(slot_of < left, s, -jnp.inf)

        parts = []
        for g in range(0, BATCH, 2):
            ps = []
            for u in range(2):
                s = sbuf[1 - par, g + u]
                m = jnp.max(s, axis=1, keepdims=True)
                p = jnp.exp2(s - m)
                parts.append([m, jnp.sum(p, axis=1, keepdims=True), None])
                ps.append(p.astype(BF16))
            o = _dot(jnp.concatenate(ps, axis=0),
                     jnp.concatenate([vbuf[last, g], vbuf[last, g + 1]], axis=1))
            parts[g][2] = o[:heads, :d]
            parts[g + 1][2] = o[heads:, d:]
        for g in range(BATCH):
            b = items[i * BATCH + g] // per
            m, l, o = parts[g]
            m_old = m_s[b]
            m_new = jnp.maximum(m_old, m)
            w_old = jnp.exp2(m_old - m_new)
            w = jnp.exp2(m - m_new)
            m_s[b] = m_new
            l_s[b] = l_s[b] * w_old + l * w
            acc[b] = acc[b] * w_old + o * w

        @pl.when(i + RING - 1 < batches)
        def _():
            fetch(i + RING - 1)
        return c

    lax.fori_loop(0, batches + 1, step, 0)

    lane = lax.broadcasted_iota(jnp.int32, (16, 128), 1)
    for c in range(rows // 16):
        l = l_s[c * 16:c * 16 + 16]
        o = acc[c * 16:c * 16 + 16] / l
        lse = m_s[c * 16:c * 16 + 16] + jnp.log2(l)
        o_ref[:heads, c * 16:c * 16 + 16, :] = jnp.swapaxes(o, 0, 1)
        lse = jnp.swapaxes(lse, 0, 1)
        out = jnp.zeros((16, 128), F32)
        for h in range(heads):
            out = jnp.where(lane == h, lse[h], out)
        o_ref[heads, c * 16:c * 16 + 16, :] = out


def _suffix(lens, q, kn, vn, k, v, scale):
    heads, rows, d = q.shape
    slots = k.shape[1]
    per = slots // SLOTS
    wide = SLOTS * heads
    k = k.reshape(rows * per, wide, d)
    v = v.reshape(rows * per, wide, d)
    return pl.pallas_call(
        functools.partial(_suffix_kernel, scale),
        in_specs=[pl.BlockSpec(memory_space=pltpu.SMEM)] + [pl.BlockSpec(memory_space=VM)] * 3
        + [pl.BlockSpec(memory_space=pl.ANY)] * 2,
        out_specs=pl.BlockSpec(memory_space=VM),
        out_shape=jax.ShapeDtypeStruct((heads + 1, rows, d), F32),
        scratch_shapes=[
            pltpu.SMEM((rows * per + 4 * BATCH,), jnp.int32),
            VM((rows + 1, heads, d), BF16),
            VM((rows + 1, heads, d), F32),
            VM((rows + 1, heads, 128), F32),
            VM((rows + 1, heads, 128), F32),
            VM((RING, BATCH, wide, d), BF16),
            VM((RING, BATCH, wide, d), BF16),
            VM((2, BATCH, heads, wide), F32),
            pltpu.SemaphoreType.DMA((RING,)),
            pltpu.SemaphoreType.DMA((RING,)),
        ],
        compiler_params=pltpu.CompilerParams(vmem_limit_bytes=LIMIT),
        cost_estimate=_cost(2e10, 4 * k.size),
    )(lens, q, kn, vn, k, v)


def _weights(ls):
    m = functools.reduce(jnp.maximum, ls)
    ws = [jnp.exp2(l - m) for l in ls]
    t = functools.reduce(jnp.add, ws)
    return [w / t for w in ws]


def _half(w_hbm, other):
    half = w_hbm.shape[1] // 2
    me = lax.axis_index('tp')
    return w_hbm.at[:, pl.ds(pl.multiple_of((1 - me if other else me) * half, half), half)]


def _send_kernel(pre_ref, suf_ref, w_hbm, att_ref, o0_ref, o1_ref, bufs, acc, sem):
    heads = pre_ref.shape[0] - 1
    cols = o0_ref.shape[1]

    def emit(i):
        o0_ref[...] = acc[:, :cols].astype(BF16)
        o1_ref[...] = acc[:, cols:].astype(BF16)
    prime, run = _stream(att_ref, [_half(w_hbm, True)], bufs, sem, acc, emit)
    prime()
    ws = _weights([pre_ref[heads], suf_ref[heads]])
    for h in range(heads):
        a = ws[0][:, h:h + 1] * pre_ref[h] + ws[1][:, h:h + 1] * suf_ref[h]
        att_ref[:, h * 128:(h + 1) * 128] = a.astype(BF16)
    run()


def _keep_kernel(att_hbm, x_hbm, w_hbm, o0_ref, o1_ref, att_ref, x_ref, bufs, acc, xsem, sem):
    cols = o0_ref.shape[1]
    half = 2 * cols
    at = pl.multiple_of(lax.axis_index('tp') * half, half)
    cps = [pltpu.make_async_copy(att_hbm, att_ref, xsem.at[0]),
           pltpu.make_async_copy(x_hbm.at[:, pl.ds(at, half)], x_ref, xsem.at[1])]

    def emit(i):
        cps[1].wait()
        y = acc[...] + x_ref[...].astype(F32)
        o0_ref[...] = y[:, :cols]
        o1_ref[...] = y[:, cols:]
    prime, run = _stream(att_ref, [_half(w_hbm, False)], bufs, sem, acc, emit)
    for c in cps:
        c.start()
    prime()
    cps[0].wait()
    run()


def _out_send(pre, suf, w_o):
    rows = pre.shape[1]
    depth, cols = w_o.shape
    cols //= 2
    return pl.pallas_call(
        _send_kernel,
        in_specs=[pl.BlockSpec(memory_space=VM)] * 2 + [pl.BlockSpec(memory_space=pl.ANY)],
        out_specs=[pl.BlockSpec(memory_space=VM)] * 3,
        out_shape=[jax.ShapeDtypeStruct((rows, depth), BF16)] + [jax.ShapeDtypeStruct((rows, cols // 2), BF16)] * 2,
        scratch_shapes=[VM((RINGW, CHUNK, cols), BF16), VM((rows, cols), F32), pltpu.SemaphoreType.DMA((RINGW,))],
        compiler_params=pltpu.CompilerParams(vmem_limit_bytes=LIMIT),
        cost_estimate=_cost(2 * rows * depth * cols, 2 * depth * cols),
    )(pre, suf, w_o)


def _out_keep(att, x, w_o):
    rows, depth = att.shape
    cols = w_o.shape[1] // 2
    return pl.pallas_call(
        _keep_kernel,
        in_specs=[pl.BlockSpec(memory_space=pl.ANY)] * 3,
        out_specs=[pl.BlockSpec(memory_space=VM)] * 2,
        out_shape=[jax.ShapeDtypeStruct((rows, cols // 2), F32)] * 2,
        scratch_shapes=[VM((rows, depth), BF16), VM((rows, cols), BF16), VM((RINGW, CHUNK, cols), BF16),
                        VM((rows, cols), F32), pltpu.SemaphoreType.DMA((2,)), pltpu.SemaphoreType.DMA((RINGW,))],
        compiler_params=pltpu.CompilerParams(vmem_limit_bytes=LIMIT),
        cost_estimate=_cost(2 * rows * depth * cols, 2 * depth * cols),
    )(att, x, w_o)


def solution(mesh):
    row_axes = ('dp', 'ctx')
    tp_swap = [(0, 1), (1, 0)]

    def device_step(hidden, w_q, w_k, w_v, w_o, k_prefix, v_prefix, k_suffix, v_suffix, seq_lens):
        scale = LOG2E * k_prefix.shape[2] ** -0.5
        q, kn, vn, pre = _front(hidden, w_q, w_k, w_v, k_prefix, v_prefix, scale)
        suf = _suffix(seq_lens, q, kn, vn, k_suffix, v_suffix, scale)
        att, s0, s1 = _out_send(pre, suf, w_o)
        swap = lambda a: lax.ppermute(a, 'tp', tp_swap)
        sent = [swap(s0), swap(s1)]
        kept = _out_keep(att, hidden, w_o)
        mine = [(a + b.astype(F32)).astype(BF16) for a, b in zip(kept, sent)]
        other = [swap(a) for a in mine]
        mine, other = jnp.concatenate(mine, axis=1), jnp.concatenate(other, axis=1)
        me = lax.axis_index('tp')
        return jnp.where(me == 0, jnp.concatenate([mine, other], axis=1), jnp.concatenate([other, mine], axis=1))

    spec_in = (P(row_axes, None), P(None, 'tp'), P(None, 'tp'), P(None, 'tp'), P('tp', None),
               P(row_axes, 'tp', None), P(row_axes, 'tp', None), P(row_axes, None, 'tp', None),
               P(row_axes, None, 'tp', None), P(row_axes))
    return jax.shard_map(device_step, mesh=mesh, in_specs=spec_in, out_specs=P(row_axes, None), check_vma=False)
```

time: 128 us -> 106 us (0.83)
  Pallas kernels: 97.6 us -> 84 us
  starting transfers between devices: 10.3 us -> 5.17 us
  local copies, waits for them, and re-layouts: 3.62 us -> 0 us
  waiting for transfers between devices: 11.9 us -> 13.3 us
    pallas_call x6 -> x2, Pallas kernels: 70.9 us -> 58.6 us  [the longest x1 52.3 us: _front(): pl.pallas_call(functools.partial(_front_kernel, scale), in_specs=[pl.Bloc...]
    ppermute x6 -> x0, starting transfers between devices: 4.23 us -> none  [the longest x2 3.42 us: device_step(): far = lambda a: lax.ppermute(a, 'ctx', chip_swap)]
    unnamed x14 -> x0, local copies, waits for them, and re-layouts: 3.62 us -> none
    ppermute x4, waiting for transfers between devices: 10.5 us -> 13.3 us  [device_step(): swap = lambda a: lax.ppermute(a, 'tp', tp_swap)]
    ppermute x6 -> x0, waiting for transfers between devices: 1.41 us -> none  [the longest x4 1.4 us: device_step(): near = lambda a: lax.ppermute(a, 'ctx', core_swap)]
  transfers between devices with their start and end apart: 10 -> 4, of which waited for: 5 -> 4; matrix products, arithmetic and copies ran while one was open for 2% -> 2% of each run, Pallas kernels for 64% -> 5%
where the time goes in v3:
time: 106 us
  Pallas kernels  84 us (79%)
  waiting for transfers between devices  13.3 us (13%)
  starting transfers between devices  5.17 us (5%)
  other arithmetic  3.4 us (3%)
    pallas_call x1, Pallas kernels, _front(): pl.pallas_call(functools.partial(_front_kernel, scale), in_specs=[pl.Bloc...  52.3 us
    pallas_call x1, Pallas kernels, _suffix(): pl.pallas_call(functools.partial(_suffix_kernel, scale), in_specs=[pl.Blo...  20 us
    ppermute x4, waiting for transfers between devices, device_step(): swap = lambda a: lax.ppermute(a, 'tp', tp_swap)  13.3 us
    pallas_call x1, Pallas kernels, _out_send(): pl.pallas_call(_send_kernel, in_specs=[pl.BlockSpec(memory_space=VM)] * 2...  6.36 us
    pallas_call x1, Pallas kernels, _out_keep(): pl.pallas_call(_keep_kernel, in_specs=[pl.BlockSpec(memory_space=pl.ANY)]...  5.31 us
    ppermute x4, starting transfers between devices, device_step(): swap = lambda a: lax.ppermute(a, 'tp', tp_swap)  5.17 us
    convert_element_type x2, other arithmetic, device_step(): mine = [(a + b.astype(F32)).astype(BF16) for a, b in zip(kept, sent)]  2.19 us
  transfers between devices with their start and end apart: 4, of which 4 were waited for; matrix products, arithmetic and copies ran while one was open for 2% of the time, Pallas kernels for 5%

profile of v3, /device:TPU:0, one launch (start us, length us, event | category | flops | bytes accessed | tf_op | source)
XLA Modules:
  0.0 105.9 jit_solution(16888442165875492569)
XLA Ops:
  0.0 52.3 %shard_map.100 = (bf16[16,128,128]{2,1,0:T(8,128)(2,1)}, bf16[16,128,128]{2,1,0:T(8,128)(2,1)}, bf16[16,128,128]{2,1,0:T(8,128)(2,1)}, f32[17,128,128]{2,1,0:T(8,128)}) custom-call(bf16[128,4096]{1,0:T(8,128)(2,1)} %x_hbm.3, bf16[4096,2048]{1,0:T(8,128)(2,1)} %wq_hbm.1, bf16[4096,2048]{1,0:T(8,128)(2,1)} %wk_hbm.1, bf16[4096,2048]{1,0:T(8,128)(2,1)} %wv_hbm.1, ...), custom_call_target="tpu_custom_call" | custom-call | flops 49999998976 | bytes 50331648 | tf_op jit(solution)/shard_map/pallas_call | solution.py:255
  52.3 20.0 %shard_map.101.suf_ref = f32[17,128,128]{2,1,0:T(8,128)} custom-call(s32[128]{0:T(128)} %lens.1, bf16[16,128,128]{2,1,0:T(8,128)(2,1)} %get-tuple-element.15.q_ref, bf16[16,128,128]{2,1,0:T(8,128)(2,1)} %get-tuple-element.16.kn_ref, bf16[16,128,128]{2,1,0:T(8,128)(2,1)} %get-tuple-element.17.vn_ref, bf16[512,256,128]{2,1,0:T(8,128)(2,1)} %bitcast.2, ...), custom_call_target="tpu_custom_call" | custom-call | flops 20000000000 | bytes 67108864 | tf_op jit(solution)/shard_map/pallas_call | solution.py:390
  72.3 6.4 %shard_map.102 = (bf16[128,2048]{1,0:T(8,128)(2,1)}, bf16[128,1024]{1,0:T(8,128)(2,1)}, bf16[128,1024]{1,0:T(8,128)(2,1)}) custom-call(f32[17,128,128]{2,1,0:T(8,128)} %get-tuple-element.14.pre_ref, f32[17,128,128]{2,1,0:T(8,128)} %shard_map.101.suf_ref, bf16[2048,4096]{1,0:T(8,128)(2,1)} %w_hbm.3), custom_call_target="tpu_custom_call" | custom-call | flops 1073741824 | bytes 8388608 | tf_op jit(solution)/shard_map/pallas_call | solution.py:466
  78.7 1.6 %collective-permute-start.1 = (bf16[128,1024]{1,0:T(8,128)(2,1)}, bf16[128,1024]{1,0:T(8,128)(2,1)S(1)}, u32[]{:S(2)}, u32[]{:S(2)}) collective-permute-start(bf16[128,1024]{1,0:T(8,128)(2,1)} %get-tuple-element.22), channel_id=1, source_target_pairs={{0,4},{4,0},{1,5},{5,1},{2,6},{6,2},{3,7},{7,3}} | collective-permute-start | bytes 786440 | tf_op jit(solution)/shard_map/ppermute | solution.py:501
  80.3 0.5 collective-permute-start
  80.8 5.3 %shard_map.103 = (f32[128,1024]{1,0:T(8,128)}, f32[128,1024]{1,0:T(8,128)}) custom-call(bf16[128,2048]{1,0:T(8,128)(2,1)} %get-tuple-element.18.att_hbm, bf16[128,4096]{1,0:T(8,128)(2,1)} %x_hbm.3, bf16[2048,4096]{1,0:T(8,128)(2,1)} %w_hbm.3), custom_call_target="tpu_custom_call" | custom-call | flops 1073741824 | bytes 8388608 | tf_op jit(solution)/shard_map/pallas_call | solution.py:480
  86.1 1.8 %collective-permute-done.1 = bf16[128,1024]{1,0:T(8,128)(2,1)S(1)} collective-permute-done((bf16[128,1024]{1,0:T(8,128)(2,1)}, bf16[128,1024]{1,0:T(8,128)(2,1)S(1)}, u32[]{:S(2)}, u32[]{:S(2)}) %collective-permute-start.1) | collective-permute-done | bytes 262176 | tf_op jit(solution)/shard_map/ppermute | solution.py:501
  87.9 1.1 %add_convert_fusion = bf16[128,1024]{1,0:T(8,128)(2,1)S(1)} fusion(f32[128,1024]{1,0:T(8,128)} %get-tuple-element.21, bf16[128,1024]{1,0:T(8,128)(2,1)S(1)} %collective-permute-done.1), kind=kLoop, calls=%fused_computation.1 | loop fusion | flops 393216 | bytes 1048576 | tf_op jit(solution)/shard_map/convert_element_type | solution.py:504
  89.0 1.6 %collective-permute-start.3 = (bf16[128,1024]{1,0:T(8,128)(2,1)S(1)}, bf16[128,1024]{1,0:T(8,128)(2,1)S(1)}, u32[]{:S(2)}, u32[]{:S(2)}) collective-permute-start(bf16[128,1024]{1,0:T(8,128)(2,1)S(1)} %add_convert_fusion), channel_id=1, source_target_pairs={{0,4},{4,0},{1,5},{5,1},{2,6},{6,2},{3,7},{7,3}} | collective-permute-start | bytes 786440 | tf_op jit(solution)/shard_map/ppermute | solution.py:501
  90.6 3.0 %collective-permute-done = bf16[128,1024]{1,0:T(8,128)(2,1)S(1)} collective-permute-done((bf16[128,1024]{1,0:T(8,128)(2,1)}, bf16[128,1024]{1,0:T(8,128)(2,1)S(1)}, u32[]{:S(2)}, u32[]{:S(2)}) %collective-permute-start) | collective-permute-done | bytes 262176 | tf_op jit(solution)/shard_map/ppermute | solution.py:501
  93.5 1.1 %add_convert_fusion.1 = bf16[128,1024]{1,0:T(8,128)(2,1)S(1)} fusion(f32[128,1024]{1,0:T(8,128)} %get-tuple-element.19, bf16[128,1024]{1,0:T(8,128)(2,1)S(1)} %collective-permute-done), kind=kLoop, calls=%fused_computation.2 | loop fusion | flops 393216 | bytes 1048576 | tf_op jit(solution)/shard_map/convert_element_type | solution.py:504
  94.6 1.6 %collective-permute-start.2 = (bf16[128,1024]{1,0:T(8,128)(2,1)S(1)}, bf16[128,1024]{1,0:T(8,128)(2,1)S(1)}, u32[]{:S(2)}, u32[]{:S(2)}) collective-permute-start(bf16[128,1024]{1,0:T(8,128)(2,1)S(1)} %add_convert_fusion.1), channel_id=1, source_target_pairs={{0,4},{4,0},{1,5},{5,1},{2,6},{6,2},{3,7},{7,3}} | collective-permute-start | bytes 786440 | tf_op jit(solution)/shard_map/ppermute | solution.py:501
  96.2 3.0 %collective-permute-done.3 = bf16[128,1024]{1,0:T(8,128)(2,1)S(1)} collective-permute-done((bf16[128,1024]{1,0:T(8,128)(2,1)S(1)}, bf16[128,1024]{1,0:T(8,128)(2,1)S(1)}, u32[]{:S(2)}, u32[]{:S(2)}) %collective-permute-start.3) | collective-permute-done | bytes 262176 | tf_op jit(solution)/shard_map/ppermute | solution.py:501
  99.1 5.5 %collective-permute-done.2 = bf16[128,1024]{1,0:T(8,128)(2,1)S(1)} collective-permute-done((bf16[128,1024]{1,0:T(8,128)(2,1)S(1)}, bf16[128,1024]{1,0:T(8,128)(2,1)S(1)}, u32[]{:S(2)}, u32[]{:S(2)}) %collective-permute-start.2) | collective-permute-done | bytes 262176 | tf_op jit(solution)/shard_map/ppermute | solution.py:501
  104.7 1.2 %maximum_select_fusion = bf16[128,4096]{1,0:T(8,128)(2,1)} fusion(bf16[128,1024]{1,0:T(8,128)(2,1)S(1)} %collective-permute-done.3, bf16[128,1024]{1,0:T(8,128)(2,1)S(1)} %collective-permute-done.2, bf16[128,1024]{1,0:T(8,128)(2,1)S(1)} %add_convert_fusion, bf16[128,1024]{1,0:T(8,128)(2,1)S(1)} %add_convert_fusion.1, pred[]{:T(512)S(6)} %eq.3), kind=kLoop, calls=%fused_computation | loop fusion | flops 8912896 | bytes 2097153 | tf_op jit(solution)/shard_map/jit(_where)/select_n | solution.py:508
Async XLA Ops:
  78.7 9.2 %collective-permute-start.1 = (bf16[128,1024]{1,0:T(8,128)(2,1)}, bf16[128,1024]{1,0:T(8,128)(2,1)S(1)}, u32[]{:S(2)}, u32[]{:S(2)}) collective-permute-start(bf16[128,1024]{1,0:T(8,128)(2,1)} %get-tuple-element.22), channel_id=1, source_target_pairs={{0,4},{4,0},{1,5},{5,1},{2,6},{6,2},{3,7},{7,3}} | collective-permute-start | bytes 786440 | tf_op jit(solution)/shard_map/ppermute | solution.py:501
  80.3 13.3 %collective-permute-start = (bf16[128,1024]{1,0:T(8,128)(2,1)}, bf16[128,1024]{1,0:T(8,128)(2,1)S(1)}, u32[]{:S(2)}, u32[]{:S(2)}) collective-permute-start(bf16[128,1024]{1,0:T(8,128)(2,1)} %get-tuple-element.20), channel_id=1, source_target_pairs={{0,4},{4,0},{1,5},{5,1},{2,6},{6,2},{3,7},{7,3}} | collective-permute-start | bytes 786440 | tf_op jit(solution)/shard_map/ppermute | solution.py:501
  89.0 10.1 %collective-permute-start.3 = (bf16[128,1024]{1,0:T(8,128)(2,1)S(1)}, bf16[128,1024]{1,0:T(8,128)(2,1)S(1)}, u32[]{:S(2)}, u32[]{:S(2)}) collective-permute-start(bf16[128,1024]{1,0:T(8,128)(2,1)S(1)} %add_convert_fusion), channel_id=1, source_target_pairs={{0,4},{4,0},{1,5},{5,1},{2,6},{6,2},{3,7},{7,3}} | collective-permute-start | bytes 786440 | tf_op jit(solution)/shard_map/ppermute | solution.py:501
  94.6 10.0 %collective-permute-start.2 = (bf16[128,1024]{1,0:T(8,128)(2,1)S(1)}, bf16[128,1024]{1,0:T(8,128)(2,1)S(1)}, u32[]{:S(2)}, u32[]{:S(2)}) collective-permute-start(bf16[128,1024]{1,0:T(8,128)(2,1)S(1)} %add_convert_fusion.1), channel_id=1, source_target_pairs={{0,4},{4,0},{1,5},{5,1},{2,6},{6,2},{3,7},{7,3}} | collective-permute-start | bytes 786440 | tf_op jit(solution)/shard_map/ppermute | solution.py:501

commit v4 on v3

v4 whole, which is shorter than its diff:
```python
import functools

import jax
import jax.numpy as jnp
from jax import lax
from jax.experimental import pallas as pl
from jax.experimental.pallas import tpu as pltpu
from jax.sharding import PartitionSpec as P

F32 = jnp.float32
BF16 = jnp.bfloat16
VM = pltpu.VMEM
LOG2E = 1.4426950408889634
BATCH = 16
SLOTS = 16
RING = 5
CHUNK = 512
RINGW = 5
LIMIT = 56 * 2**20


def _cost(flops, nbytes):
    return pl.CostEstimate(flops=int(flops), bytes_accessed=int(nbytes), transcendentals=0)


def _dot(a, b, dims=(((1,), (0,)), ((), ()))):
    return lax.dot_general(a, b, dims, preferred_element_type=F32)


NT = (((1,), (1,)), ((), ()))


MESH = pl.DeviceIdType.MESH


def _stream(x_ref, ws, bufs, sem, acc, emit, extra_start=None, extra_body=None):
    ring, chunk, cols = bufs.shape
    n = ws[0].shape[0] // chunk
    total = n * len(ws)
    part = 512

    def start(g):
        slot = lax.rem(g, ring)
        for i, w in enumerate(ws):
            @pl.when((g >= i * n) & (g < (i + 1) * n))
            def _():
                at = pl.multiple_of((g - i * n) * chunk, chunk)
                pltpu.make_async_copy(w.at[pl.ds(at, chunk)], bufs.at[slot], sem.at[slot]).start()
        if extra_start is not None:
            extra_start(g)

    def prime():
        def body(g, c):
            start(g)
            return c
        lax.fori_loop(0, min(ring, total), body, 0)

    def run():
        for i, w in enumerate(ws):
            acc[...] = jnp.zeros_like(acc)

            def body(c, carry):
                g = i * n + c
                slot = lax.rem(g, ring)
                pltpu.make_async_copy(w.at[pl.ds(0, chunk)], bufs.at[slot], sem.at[slot]).wait()
                x = x_ref[:, pl.ds(pl.multiple_of(c * chunk, chunk), chunk)]
                for j in range(0, cols, part):
                    acc[:, j:j + part] += _dot(x, bufs[slot, :, j:j + part])
                if extra_body is not None:
                    extra_body(i, g)
                start(g + ring)
                return carry
            lax.fori_loop(0, n, body, 0)
            emit(i)
    return prime, run


def _peers():
    me = lax.axis_index('ctx')
    return me + 1 - 2 * lax.rem(me, 2), me + 2 - 4 * (me // 2)


def _remote(src, dst, s, r, **to):
    return pltpu.make_async_remote_copy(src_ref=src, dst_ref=dst, send_sem=s, recv_sem=r,
                                        device_id=to, device_id_type=MESH)


def _front_kernel(x_hbm, wq_hbm, wk_hbm, wv_hbm, kp_hbm, vp_hbm, q_hbm, kn_hbm, vn_hbm, kt_hbm, vt_hbm,
                  x_ref, bufs, acc, raw, kt, vt, qs, kvn,
                  xsem, sem, psem, osem, tsem, q_s, q_r):
    heads, n_pos, d = kt.shape
    ring, chunk, _ = bufs.shape
    near, far = _peers()
    n = x_hbm.shape[1] // chunk
    pos = n_pos // (2 * n)
    stages = 4
    span = n_pos // stages

    cp = pltpu.make_async_copy(x_hbm, x_ref, xsem)
    cp.start()

    hh = heads // 2
    half = [pl.ds(j * hh, hh) for j in range(2)]
    q_near = _remote(qs.at[0], qs.at[1], q_s.at[0], q_r.at[0], ctx=near)
    q_far = [_remote(qs.at[0, at], qs.at[2, at], q_s.at[1 + j], q_r.at[1 + j], ctx=far) for j, at in enumerate(half)]
    q_diag = [_remote(qs.at[2, at], qs.at[3, at], q_s.at[3 + j], q_r.at[3 + j], ctx=near) for j, at in enumerate(half)]
    outs = [pltpu.make_async_copy(qs.at[0], q_hbm.at[0], osem.at[0]),
            pltpu.make_async_copy(kvn.at[0], kn_hbm, osem.at[1]),
            pltpu.make_async_copy(kvn.at[1], vn_hbm, osem.at[2])]

    def pieces(g):
        at = pl.ds((g - n) * pos, pos)
        slot = lax.rem(g, ring)
        return [pltpu.make_async_copy(src.at[at], raw.at[slot, j], psem.at[slot, j])
                for j, src in enumerate((kp_hbm, vp_hbm))]

    def stores(t):
        at = pl.ds(pl.multiple_of(t * span, span), span)
        return [pltpu.make_async_copy(src.at[:, at], dst.at[:, at], tsem.at[j, t])
                for j, (src, dst) in enumerate(((kt, kt_hbm), (vt, vt_hbm)))]

    def extra_start(g):
        @pl.when((g >= n) & (g < 3 * n))
        def _():
            for c in pieces(g):
                c.start()

    def extra_body(i, g):
        if i == 0:
            return
        slot = lax.rem(g, ring)
        for c in pieces(g):
            c.wait()
        for j, dst in enumerate((kt, vt)):
            for u in range(pos // 16):
                at = pl.multiple_of((g - n) * pos + u * 16, 16)
                dst[:, pl.ds(at, 16), :] = jnp.swapaxes(raw[slot, j, u * 16:u * 16 + 16], 0, 1)
        done = (g - n + 1) * pos

        @pl.when(lax.rem(done, span) == 0)
        def _():
            for c in stores(done // span - 1):
                c.start()

    def emit(i):
        dst = qs.at[0] if i == 0 else kvn.at[i - 1]
        for h in range(heads):
            dst[h] = acc[:, h * d:(h + 1) * d].astype(BF16)
        if i == 0:
            pl.semaphore_wait(barrier, 2)
            for c in (q_far[0], q_far[1], q_near):
                c.start()
        outs[i].start()

    prime, run = _stream(x_ref, [wq_hbm, wk_hbm, wv_hbm], bufs, sem, acc, emit, extra_start, extra_body)
    prime()
    barrier = pltpu.get_barrier_semaphore()
    for to in (near, far):
        pl.semaphore_signal(barrier, inc=1, device_id={'ctx': to}, device_id_type=MESH)
    cp.wait()
    run()

    for j in range(2):
        q_far[j].wait_recv()
        q_diag[j].start()
    q_near.wait_recv()
    for c in q_diag:
        c.wait_recv()
    rest = pltpu.make_async_copy(qs.at[pl.ds(1, 3)], q_hbm.at[pl.ds(1, 3)], xsem)
    rest.start()
    for c in outs + [rest]:
        c.wait()
    for t in range(stages):
        for c in stores(t):
            c.wait()
    for c in [q_near] + q_far + q_diag:
        c.wait_send()


def _front(x, wq, wk, wv, kp, vp):
    rows, depth = x.shape
    cols = wq.shape[1]
    n, heads, d = kp.shape
    pos = n // (2 * depth // CHUNK)
    dma = pltpu.SemaphoreType.DMA
    blk = (heads, rows, d)
    return pl.pallas_call(
        _front_kernel,
        in_specs=[pl.BlockSpec(memory_space=pl.ANY)] * 6,
        out_specs=[pl.BlockSpec(memory_space=pl.ANY)] * 5,
        out_shape=[jax.ShapeDtypeStruct((4,) + blk, BF16)] + [jax.ShapeDtypeStruct(blk, BF16)] * 2
        + [jax.ShapeDtypeStruct((heads, n, d), BF16)] * 2,
        scratch_shapes=[
            VM((rows, depth), BF16), VM((RINGW, CHUNK, cols), BF16), VM((rows, cols), F32),
            VM((RINGW, 2, pos, heads, d), BF16), VM((heads, n, d), BF16), VM((heads, n, d), BF16),
            VM((4,) + blk, BF16), VM((2,) + blk, BF16),
            dma, dma((RINGW,)), dma((RINGW, 2)), dma((3,)), dma((2, 4)), dma((5,)), dma((5,))],
        compiler_params=pltpu.CompilerParams(vmem_limit_bytes=LIMIT, collective_id=0, has_side_effects=True),
        cost_estimate=_cost(2e10, 6 * depth * cols),
    )(x, wq, wk, wv, kp, vp)


def _back_kernel(scale, q_hbm, kt_hbm, vt_hbm, suf_hbm, x_hbm, w_hbm, y_ref,
                 qs, kt, vt, suf, x_ref, wo, ds, dr, ns, nr, fo, mo, xs, xr, xl, xlr, att, keep, ps, pr,
                 qsem, ksem, wsem, d_s, d_r, n_s, n_r, x_s, x_r, p_s, p_r, y_s, y_r):
    heads, n_pos, d = kt.shape
    rows = x_ref.shape[0]
    rh = rows // 2
    cols = x_ref.shape[1]
    half = cols // 2
    near, far = _peers()
    tp = lax.axis_index('tp')
    steps = 4
    group = heads // steps
    wide = ps.shape[-1]
    blocks = half // wide

    barrier = pltpu.get_barrier_semaphore()
    for to in ({'ctx': near}, {'ctx': far}, {'tp': 1 - tp}):
        pl.semaphore_signal(barrier, inc=1, device_id=to, device_id_type=MESH)
    q_cp = pltpu.make_async_copy(q_hbm, qs, qsem.at[0])
    q_cp.start()
    kv_cp = [[pltpu.make_async_copy(src.at[pl.ds(i * group, group)], dst.at[pl.ds(i * group, group)], ksem.at[j, i])
              for j, (src, dst) in enumerate(((kt_hbm, kt), (vt_hbm, vt)))] for i in range(steps)]
    for cs in kv_cp:
        for c in cs:
            c.start()
    suf_cp = pltpu.make_async_copy(suf_hbm, suf, qsem.at[1])
    x_cp = pltpu.make_async_copy(x_hbm, x_ref, qsem.at[2])
    wr = w_hbm.shape[0] // 4
    w_cp = [pltpu.make_async_copy(w_hbm.at[pl.ds(i * wr, wr)], wo.at[pl.ds(i * wr, wr)], wsem.at[i]) for i in range(4)]
    for c in [suf_cp, x_cp] + w_cp:
        c.start()

    lane = lax.broadcasted_iota(jnp.int32, (rh, d), 1)

    def d_copy(a, i):
        at = pl.ds(i * group, group)
        return _remote(ds.at[a, at], dr.at[a, at], d_s.at[a, i], d_r.at[a, i], ctx=near)

    def n_copy(a, i):
        at = pl.ds(i * group, group)
        return _remote(ns.at[a, at], nr.at[a, at], n_s.at[a, i], n_r.at[a, i], ctx=near)

    def x_copy(a, i):
        at = pl.ds(i * group, group)
        return _remote(xs.at[a, at], xr.at[a, at], x_s.at[a, i], x_r.at[a, i], ctx=far)

    def l_copy(a):
        return _remote(xl.at[a], xlr.at[a], x_s.at[a, steps], x_r.at[a, steps], ctx=far)

    def p_copy(a, j):
        return _remote(ps.at[a, j], pr.at[a, j], p_s.at[a, j], p_r.at[a, j], tp=1 - tp)

    def y_copy(a, j):
        at = (pl.ds(a * rh, rh), pl.ds(pl.multiple_of(tp * half + j * wide, wide), wide))
        return _remote(y_ref.at[at], y_ref.at[at], y_s.at[a, j], y_r.at[a, j], tp=1 - tp)

    def attend(a, h, q0, q1, dst0, dst1):
        at = slice(a * rh, (a + 1) * rh)
        q = jnp.concatenate([qs[q0, h, at], qs[q1, h, at]], axis=0)
        s = _dot(q, kt[h], NT)
        m = jnp.max(s, axis=1, keepdims=True) * scale
        e = jnp.exp2(s * scale - m)
        l = jnp.sum(e, axis=1, keepdims=True)
        o = _dot(e.astype(BF16), vt[h]) / l
        lse = jnp.broadcast_to(m + jnp.log2(l), (rows, d))
        dst0[h, 0], dst0[h, 1] = o[:rh], lse[:rh]
        dst1[h, 0], dst1[h, 1] = o[rh:], lse[rh:]

    def merge_far(a, i):
        d_copy(a, i).wait_recv()
        for u in range(group):
            h = i * group + u
            l0, l1 = fo[h, 1], dr[a, h, 1]
            m = jnp.maximum(l0, l1)
            w0, w1 = jnp.exp2(l0 - m), jnp.exp2(l1 - m)
            t = w0 + w1
            xs[a, h] = ((w0 * fo[h, 0] + w1 * dr[a, h, 0]) / t).astype(BF16)
            xl[a] = jnp.where(lane == h, m + jnp.log2(t), xl[a])
        x_copy(a, i).start()

    def add_peer(a):
        for j in range(blocks):
            p_copy(a, j).wait_recv()
            y = (keep[a, j] + pr[a, j].astype(F32)).astype(BF16)
            y_ref[a * rh:(a + 1) * rh, pl.ds(pl.multiple_of(tp * half + j * wide, wide), wide)] = y
            y_copy(a, j).start()

    xl[...] = jnp.zeros_like(xl)
    q_cp.wait()
    for a in range(2):
        def far_step(i, c):
            if a == 0:
                for k in range(steps):
                    @pl.when(i == k)
                    def _():
                        for cp in kv_cp[k]:
                            cp.wait()
            for u in range(group):
                attend(a, i * group + u, 3, 2, ds.at[a], fo)
            if a == 0:
                @pl.when(i == 0)
                def _():
                    pl.semaphore_wait(barrier, 3)
            d_copy(a, i).start()

            @pl.when(i > 0)
            def _():
                merge_far(a, i - 1)
            return c
        lax.fori_loop(0, steps, far_step, 0)

        def near_step(i, c):
            for u in range(group):
                attend(a, i * group + u, 1, 0, ns.at[a], mo)
            n_copy(a, i).start()

            @pl.when(i == 0)
            def _():
                merge_far(a, steps - 1)
                l_copy(a).start()
                if a == 1:
                    add_peer(0)
            return c
        lax.fori_loop(0, steps, near_step, 0)

        if a == 0:
            suf_cp.wait()
            x_cp.wait()
        at = slice(a * rh, (a + 1) * rh)
        l_copy(a).wait_recv()
        far_lse, suf_lse = xlr[a], suf[heads, at]
        for h in range(heads):
            if h % group == 0:
                n_copy(a, h // group).wait_recv()
                x_copy(a, h // group).wait_recv()
            ls = [mo[h, 1], nr[a, h, 1], jnp.broadcast_to(far_lse[:, h:h + 1], (rh, d)),
                  jnp.broadcast_to(suf_lse[:, h:h + 1], (rh, d))]
            m = functools.reduce(jnp.maximum, ls)
            ws = [jnp.exp2(l - m) for l in ls]
            o = ws[0] * mo[h, 0] + ws[1] * nr[a, h, 0] + ws[2] * xr[a, h].astype(F32) + ws[3] * suf[h, at]
            att[:, h * d:(h + 1) * d] = (o / functools.reduce(jnp.add, ws)).astype(BF16)
        if a == 0:
            for c in w_cp:
                c.wait()

        def send_block(j, c):
            cols_at = pl.ds(pl.multiple_of((1 - tp) * half + j * wide, wide), wide)
            ps[a, j] = _dot(att[...], wo[:, cols_at]).astype(BF16)
            p_copy(a, j).start()
            return c
        lax.fori_loop(0, blocks, send_block, 0)

        def keep_block(j, c):
            cols_at = pl.ds(pl.multiple_of(tp * half + j * wide, wide), wide)
            keep[a, j] = _dot(att[...], wo[:, cols_at]) + x_ref[at, cols_at].astype(F32)
            return c
        lax.fori_loop(0, blocks, keep_block, 0)

    add_peer(1)
    for a in range(2):
        for j in range(blocks):
            y_copy(a, j).wait_recv()
            y_copy(a, j).wait_send()
            p_copy(a, j).wait_send()
        for i in range(steps):
            d_copy(a, i).wait_send()
            n_copy(a, i).wait_send()
            x_copy(a, i).wait_send()
        l_copy(a).wait_send()


def _back(q, kt, vt, suf, x, w_o, scale):
    _, heads, rows, d = q.shape
    n = kt.shape[1]
    depth, cols = w_o.shape
    dma = pltpu.SemaphoreType.DMA
    rh, wide, steps = rows // 2, 512, 4
    blocks = cols // 2 // wide
    return pl.pallas_call(
        functools.partial(_back_kernel, scale),
        in_specs=[pl.BlockSpec(memory_space=pl.ANY)] * 6,
        out_specs=pl.BlockSpec(memory_space=VM),
        out_shape=jax.ShapeDtypeStruct((rows, cols), BF16),
        scratch_shapes=[
            VM(q.shape, BF16), VM(kt.shape, BF16), VM(vt.shape, BF16), VM(suf.shape, F32), VM((rows, cols), BF16),
            VM(w_o.shape, BF16)]
        + [VM((2, heads, 2, rh, d), F32)] * 4 + [VM((heads, 2, rh, d), F32)] * 2
        + [VM((2, heads, rh, d), BF16)] * 2 + [VM((2, rh, d), F32)] * 2
        + [VM((rh, depth), BF16), VM((2, blocks, rh, wide), F32)] + [VM((2, blocks, rh, wide), BF16)] * 2
        + [dma((3,)), dma((2, steps)), dma((4,))]
        + [dma((2, steps))] * 4 + [dma((2, steps + 1))] * 2 + [dma((2, blocks))] * 4,
        compiler_params=pltpu.CompilerParams(vmem_limit_bytes=62 * 2**20, collective_id=1, has_side_effects=True),
        cost_estimate=_cost(5e10, 2 * depth * cols),
    )(q, kt, vt, suf, x, w_o)


def _suffix_kernel(scale, lens, q_hbm, kn_hbm, vn_hbm, k_hbm, v_hbm, o_ref,
                   new, newsem, items, qb, acc, m_s, l_s, kbuf, vbuf, sbuf, ksem, vsem):
    _, heads, rows, d = new.shape
    news = [pltpu.make_async_copy(src, new.at[j], newsem.at[j])
            for j, src in enumerate((q_hbm.at[0], kn_hbm, vn_hbm))]
    for c in news:
        c.start()
    per = k_hbm.shape[0] // rows
    wide = SLOTS * heads
    dummy = rows * per

    for g in range(BATCH):
        items[g] = dummy

    def listing(b, t):
        for j in range(per):
            items[BATCH + t + j] = b * per + j
        return t + (lens[b] + SLOTS - 1) // SLOTS
    total = lax.fori_loop(0, rows, listing, 0)
    for g in range(2 * BATCH):
        items[BATCH + total + g] = dummy
    batches = (total + BATCH - 1) // BATCH

    def fetch(i):
        slot = lax.rem(i, RING)
        for g in range(BATCH):
            it = jnp.minimum(items[BATCH + i * BATCH + g], dummy - 1)
            pltpu.make_async_copy(k_hbm.at[it], kbuf.at[slot, g], ksem.at[slot]).start()
            pltpu.make_async_copy(v_hbm.at[it], vbuf.at[slot, g], vsem.at[slot]).start()

    def prime(i, c):
        fetch(i)
        return c
    lax.fori_loop(0, jnp.minimum(batches, RING - 1), prime, 0)

    for c in news:
        c.wait()
    for c in range(rows // 16):
        q, kn, vn = [jnp.swapaxes(new[j, :, c * 16:c * 16 + 16, :], 0, 1) for j in range(3)]
        qb[c * 16:c * 16 + 16] = q
        s = jnp.sum(q.astype(F32) * kn.astype(F32), axis=-1, keepdims=True) * scale
        m_s[c * 16:c * 16 + 16] = jnp.broadcast_to(s, (16, heads, 128))
        l_s[c * 16:c * 16 + 16] = jnp.ones((16, heads, 128), F32)
        acc[c * 16:c * 16 + 16] = vn.astype(F32)

    row = lax.broadcasted_iota(jnp.int32, (heads, wide), 0)
    col = lax.broadcasted_iota(jnp.int32, (heads, wide), 1)
    slot_of = jnp.where(lax.rem(col, heads) == row, col // heads, 1 << 20)

    def step(i, c):
        slot = lax.rem(i, RING)
        last = lax.rem(i + RING - 1, RING)
        par = lax.rem(i, 2)

        @pl.when(i < batches)
        def _():
            pltpu.make_async_copy(k_hbm.at[pl.ds(0, BATCH)], kbuf.at[slot], ksem.at[slot]).wait()

        @pl.when(i > 0)
        def _():
            pltpu.make_async_copy(v_hbm.at[pl.ds(0, BATCH)], vbuf.at[last], vsem.at[last]).wait()

        for g in range(BATCH):
            it = items[BATCH + i * BATCH + g]
            b = it // per
            left = lens[jnp.minimum(b, rows - 1)] - lax.rem(it, per) * SLOTS
            s = _dot(qb[b], kbuf[slot, g], NT) * scale
            sbuf[par, g] = jnp.where(slot_of < left, s, -jnp.inf)

        parts = []
        for g in range(0, BATCH, 2):
            ps = []
            for u in range(2):
                s = sbuf[1 - par, g + u]
                m = jnp.max(s, axis=1, keepdims=True)
                p = jnp.exp2(s - m)
                parts.append([m, jnp.sum(p, axis=1, keepdims=True), None])
                ps.append(p.astype(BF16))
            o = _dot(jnp.concatenate(ps, axis=0),
                     jnp.concatenate([vbuf[last, g], vbuf[last, g + 1]], axis=1))
            parts[g][2] = o[:heads, :d]
            parts[g + 1][2] = o[heads:, d:]
        for g in range(BATCH):
            b = items[i * BATCH + g] // per
            m, l, o = parts[g]
            m_old = m_s[b]
            m_new = jnp.maximum(m_old, m)
            w_old = jnp.exp2(m_old - m_new)
            w = jnp.exp2(m - m_new)
            m_s[b] = m_new
            l_s[b] = l_s[b] * w_old + l * w
            acc[b] = acc[b] * w_old + o * w

        @pl.when(i + RING - 1 < batches)
        def _():
            fetch(i + RING - 1)
        return c

    lax.fori_loop(0, batches + 1, step, 0)

    lane = lax.broadcasted_iota(jnp.int32, (16, 128), 1)
    for c in range(rows // 16):
        l = l_s[c * 16:c * 16 + 16]
        o = acc[c * 16:c * 16 + 16] / l
        lse = m_s[c * 16:c * 16 + 16] + jnp.log2(l)
        o_ref[:heads, c * 16:c * 16 + 16, :] = jnp.swapaxes(o, 0, 1)
        lse = jnp.swapaxes(lse, 0, 1)
        out = jnp.zeros((16, 128), F32)
        for h in range(heads):
            out = jnp.where(lane == h, lse[h], out)
        o_ref[heads, c * 16:c * 16 + 16, :] = out


def _suffix(lens, q, kn, vn, k, v, scale):
    _, heads, rows, d = q.shape
    slots = k.shape[1]
    per = slots // SLOTS
    wide = SLOTS * heads
    k = k.reshape(rows * per, wide, d)
    v = v.reshape(rows * per, wide, d)
    return pl.pallas_call(
        functools.partial(_suffix_kernel, scale),
        in_specs=[pl.BlockSpec(memory_space=pltpu.SMEM)] + [pl.BlockSpec(memory_space=pl.ANY)] * 5,
        out_specs=pl.BlockSpec(memory_space=VM),
        out_shape=jax.ShapeDtypeStruct((heads + 1, rows, d), F32),
        scratch_shapes=[
            VM((3, heads, rows, d), BF16),
            pltpu.SemaphoreType.DMA((3,)),
            pltpu.SMEM((rows * per + 4 * BATCH,), jnp.int32),
            VM((rows + 1, heads, d), BF16),
            VM((rows + 1, heads, d), F32),
            VM((rows + 1, heads, 128), F32),
            VM((rows + 1, heads, 128), F32),
            VM((RING, BATCH, wide, d), BF16),
            VM((RING, BATCH, wide, d), BF16),
            VM((2, BATCH, heads, wide), F32),
            pltpu.SemaphoreType.DMA((RING,)),
            pltpu.SemaphoreType.DMA((RING,)),
        ],
        compiler_params=pltpu.CompilerParams(vmem_limit_bytes=LIMIT),
        cost_estimate=_cost(2e10, 4 * k.size),
    )(lens, q, kn, vn, k, v)


def solution(mesh):
    row_axes = ('dp', 'ctx')
    def device_step(hidden, w_q, w_k, w_v, w_o, k_prefix, v_prefix, k_suffix, v_suffix, seq_lens):
        scale = LOG2E * k_prefix.shape[2] ** -0.5
        q, kn, vn, kt, vt = _front(hidden, w_q, w_k, w_v, k_prefix, v_prefix)
        suf = _suffix(seq_lens, q, kn, vn, k_suffix, v_suffix, scale)
        return _back(q, kt, vt, suf, hidden, w_o, scale)

    spec_in = (P(row_axes, None), P(None, 'tp'), P(None, 'tp'), P(None, 'tp'), P('tp', None),
               P(row_axes, 'tp', None), P(row_axes, 'tp', None), P(row_axes, None, 'tp', None),
               P(row_axes, None, 'tp', None), P(row_axes))
    return jax.shard_map(device_step, mesh=mesh, in_specs=spec_in, out_specs=P(row_axes, None), check_vma=False)
```

time: 106 us -> 103 us (0.972)
  Pallas kernels: 84 us -> 101 us
  waiting for transfers between devices: 13.3 us -> 0 us
  starting transfers between devices: 5.17 us -> 0 us
  other arithmetic: 3.4 us -> 0 us
  local copies, waits for them, and re-layouts: 0 us -> 2.29 us
    pallas_call x3 -> x2, Pallas kernels: 63.9 us -> 79.1 us  [the longest x1 53.8 us: _back(): pl.pallas_call(functools.partial(_back_kernel, scale), in_specs=[pl.Block...]
    ppermute x4 -> x0, waiting for transfers between devices: 13.3 us -> none  [device_step(): swap = lambda a: lax.ppermute(a, 'tp', tp_swap)]
    ppermute x4 -> x0, starting transfers between devices: 5.17 us -> none  [device_step(): swap = lambda a: lax.ppermute(a, 'tp', tp_swap)]
    unnamed x0 -> x1, local copies, waits for them, and re-layouts: none -> 2.29 us
    convert_element_type x2 -> x0, other arithmetic: 2.19 us -> none  [device_step(): mine = [(a + b.astype(F32)).astype(BF16) for a, b in zip(kept, sent)]]
    pallas_call x1, Pallas kernels: 20 us -> 21.7 us  [_suffix(): pl.pallas_call(functools.partial(_suffix_kernel, scale), in_specs=[pl.Blo...]
    select_n x1 -> x0, other arithmetic: 1.21 us -> none  [device_step(): jnp.where(me == 0, jnp.concatenate([mine, other], axis=1), jnp.concatenat...]
  transfers between devices with their start and end apart: 4 -> 0, of which waited for: 4 -> 0; matrix products, arithmetic and copies ran while one was open for 2% -> 0% of each run, Pallas kernels for 5% -> 0%
where the time goes in v4:
time: 103 us
  Pallas kernels  101 us (98%)
  local copies, waits for them, and re-layouts  2.29 us (2%)
    pallas_call x1, Pallas kernels, _back(): pl.pallas_call(functools.partial(_back_kernel, scale), in_specs=[pl.Block...  53.8 us
    pallas_call x1, Pallas kernels, _front(): pl.pallas_call(_front_kernel, in_specs=[pl.BlockSpec(memory_space=pl.ANY)...  25.3 us
    pallas_call x1, Pallas kernels, _suffix(): pl.pallas_call(functools.partial(_suffix_kernel, scale), in_specs=[pl.Blo...  21.7 us
    unnamed x1, local copies, waits for them, and re-layouts  2.29 us

profile of v4, /device:TPU:0, one launch (start us, length us, event | category | flops | bytes accessed | tf_op | source)
XLA Modules:
  0.0 103.1 jit_solution(18353120874461825749)
XLA Ops:
  0.0 25.3 %shard_map.100 = (bf16[4,16,128,128]{3,2,1,0:T(8,128)(2,1)}, bf16[16,128,128]{2,1,0:T(8,128)(2,1)}, bf16[16,128,128]{2,1,0:T(8,128)(2,1)}, bf16[16,1024,128]{2,1,0:T(8,128)(2,1)}, bf16[16,1024,128]{2,1,0:T(8,128)(2,1)}) custom-call(bf16[128,4096]{1,0:T(8,128)(2,1)} %x_hbm.3, bf16[4096,2048]{1,0:T(8,128)(2,1)} %wq_hbm.1, bf16[4096,2048]{1,0:T(8,128)(2,1)} %wk_hbm.1, ...), custom_call_target="tpu_custom_call" | custom-call | flops 20000000000 | bytes 50331648 | tf_op jit(solution)/shard_map/pallas_call | solution.py:187
  25.3 21.7 %shard_map.101.suf_hbm = f32[17,128,128]{2,1,0:T(8,128)} custom-call(s32[128]{0:T(128)} %lens.1, bf16[4,16,128,128]{3,2,1,0:T(8,128)(2,1)} %get-tuple-element.10.q_hbm, bf16[16,128,128]{2,1,0:T(8,128)(2,1)} %get-tuple-element.13.kn_hbm, bf16[16,128,128]{2,1,0:T(8,128)(2,1)} %get-tuple-element.14.vn_hbm, bf16[512,256,128]{2,1,0:T(8,128)(2,1)} %bitcast.2, ...), custom_call_target="tpu_custom_call" | custom-call | flops 20000000000 | bytes 67108864 | tf_op jit(solution)/shard_map/pallas_call | solution.py:519
  47.1 53.8 %shard_map.102 = bf16[128,4096]{1,0:T(8,128)(2,1)} custom-call(bf16[4,16,128,128]{3,2,1,0:T(8,128)(2,1)} %get-tuple-element.10.q_hbm, bf16[16,1024,128]{2,1,0:T(8,128)(2,1)} %get-tuple-element.11.kt_hbm, bf16[16,1024,128]{2,1,0:T(8,128)(2,1)} %get-tuple-element.12.vt_hbm, f32[17,128,128]{2,1,0:T(8,128)} %shard_map.101.suf_hbm, bf16[128,4096]{1,0:T(8,128)(2,1)} %x_hbm.3, ...), custom_call_target="tpu_custom_call" | custom-call | flops 49999998976 | bytes 16777216 | tf_op jit(solution)/shard_map/pallas_call | solution.py:381
  100.9 2.3 %copy.12 = bf16[128,4096]{1,0:T(8,128)(2,1)} copy(bf16[128,4096]{1,0:T(8,128)(2,1)} %shard_map.102) | data formatting | bytes 2097152

commit v5 on v4

--- a/solution.py
+++ b/solution.py
@@ -201,7 +201,7 @@
 
 
 def _back_kernel(scale, q_hbm, kt_hbm, vt_hbm, suf_hbm, x_hbm, w_hbm, y_ref,
-                 qs, kt, vt, suf, x_ref, wo, ds, dr, ns, nr, fo, mo, xs, xr, xl, xlr, att, keep, ps, pr,
+                 qs, kt, vt, suf, x_ref, wo, ds, dr, ns, nr, fo, mo, xs, xr, xl, xlr, att, keep, ps, pr, sb, mb,
                  qsem, ksem, wsem, d_s, d_r, n_s, n_r, x_s, x_r, p_s, p_r, y_s, y_r):
     heads, n_pos, d = kt.shape
     rows = x_ref.shape[0]
@@ -256,17 +256,31 @@
         at = (pl.ds(a * rh, rh), pl.ds(pl.multiple_of(tp * half + j * wide, wide), wide))
         return _remote(y_ref.at[at], y_ref.at[at], y_s.at[a, j], y_r.at[a, j], tp=1 - tp)
 
-    def attend(a, h, q0, q1, dst0, dst1):
+    def scores(a, h, q0, q1, slot):
         at = slice(a * rh, (a + 1) * rh)
         q = jnp.concatenate([qs[q0, h, at], qs[q1, h, at]], axis=0)
         s = _dot(q, kt[h], NT)
-        m = jnp.max(s, axis=1, keepdims=True) * scale
-        e = jnp.exp2(s * scale - m)
-        l = jnp.sum(e, axis=1, keepdims=True)
-        o = _dot(e.astype(BF16), vt[h]) / l
-        lse = jnp.broadcast_to(m + jnp.log2(l), (rows, d))
+        sb[slot] = s
+        mb[slot] = jnp.broadcast_to(jnp.max(s, axis=1, keepdims=True) * scale, (rows, d))
+
+    def weigh(h, slot, dst0, dst1):
+        m = mb[slot]
+        es, l = [], None
+        for k in range(0, n_pos, d):
+            e = jnp.exp2(sb[slot, :, k:k + d] * scale - m)
+            l = e if l is None else l + e
+            es.append(e.astype(BF16))
+        l = jnp.sum(l, axis=1, keepdims=True)
+        o = _dot(jnp.concatenate(es, axis=1), vt[h]) / l
+        lse = m + jnp.log2(l)
         dst0[h, 0], dst0[h, 1] = o[:rh], lse[:rh]
         dst1[h, 0], dst1[h, 1] = o[rh:], lse[rh:]
+
+    def attend(a, i, q0, q1, dst0, dst1):
+        for u in range(group):
+            h = i * group + u
+            scores(a, jnp.minimum(h + 1, heads - 1), q0, q1, (u + 1) % 2)
+            weigh(h, u % 2, dst0, dst1)
 
     def merge_far(a, i):
         d_copy(a, i).wait_recv()
@@ -289,16 +303,17 @@
 
     xl[...] = jnp.zeros_like(xl)
     q_cp.wait()
+    for cp in kv_cp[0]:
+        cp.wait()
     for a in range(2):
         def far_step(i, c):
             if a == 0:
-                for k in range(steps):
+                for k in range(steps - 1):
                     @pl.when(i == k)
                     def _():
-                        for cp in kv_cp[k]:
+                        for cp in kv_cp[k + 1]:
                             cp.wait()
-            for u in range(group):
-                attend(a, i * group + u, 3, 2, ds.at[a], fo)
+            attend(a, i, 3, 2, ds.at[a], fo)
             if a == 0:
                 @pl.when(i == 0)
                 def _():
@@ -309,11 +324,11 @@
             def _():
                 merge_far(a, i - 1)
             return c
+        scores(a, 0, 3, 2, 0)
         lax.fori_loop(0, steps, far_step, 0)
 
         def near_step(i, c):
-            for u in range(group):
-                attend(a, i * group + u, 1, 0, ns.at[a], mo)
+            attend(a, i, 1, 0, ns.at[a], mo)
             n_copy(a, i).start()
 
             @pl.when(i == 0)
@@ -323,6 +338,7 @@
                 if a == 1:
                     add_peer(0)
             return c
+        scores(a, 0, 1, 0, 0)
         lax.fori_loop(0, steps, near_step, 0)
 
         if a == 0:
@@ -389,6 +405,7 @@
         + [VM((2, heads, 2, rh, d), F32)] * 4 + [VM((heads, 2, rh, d), F32)] * 2
         + [VM((2, heads, rh, d), BF16)] * 2 + [VM((2, rh, d), F32)] * 2
         + [VM((rh, depth), BF16), VM((2, blocks, rh, wide), F32)] + [VM((2, blocks, rh, wide), BF16)] * 2
+        + [VM((2, rows, n), F32), VM((2, rows, d), F32)]
         + [dma((3,)), dma((2, steps)), dma((4,))]
         + [dma((2, steps))] * 4 + [dma((2, steps + 1))] * 2 + [dma((2, blocks))] * 4,
         compiler_params=pltpu.CompilerParams(vmem_limit_bytes=62 * 2**20, collective_id=1, has_side_effects=True),

time: 103 us -> 98.2 us (0.953)
  Pallas kernels: 101 us -> 95.1 us
    pallas_call x1, Pallas kernels: 53.8 us -> 49.7 us  [_back(): pl.pallas_call(functools.partial(_back_kernel, scale), in_specs=[pl.Block...]
    pallas_call x1, Pallas kernels: 21.7 us -> 20 us  [_suffix(): pl.pallas_call(functools.partial(_suffix_kernel, scale), in_specs=[pl.Blo...]
where the time goes in v5:
time: 98.2 us; the launch traced here: 97.4 us
  Pallas kernels  95.1 us (97%)
  local copies, waits for them, and re-layouts  2.29 us (2%)
    pallas_call x1, Pallas kernels, _back(): pl.pallas_call(functools.partial(_back_kernel, scale), in_specs=[pl.Block...  49.7 us
    pallas_call x1, Pallas kernels, _front(): pl.pallas_call(_front_kernel, in_specs=[pl.BlockSpec(memory_space=pl.ANY)...  25.3 us
    pallas_call x1, Pallas kernels, _suffix(): pl.pallas_call(functools.partial(_suffix_kernel, scale), in_specs=[pl.Blo...  20 us
    unnamed x1, local copies, waits for them, and re-layouts  2.29 us

profile of v5, /device:TPU:0, one launch (start us, length us, event | category | flops | bytes accessed | tf_op | source)
XLA Modules:
  0.0 97.4 jit_solution(5737290674208401058)
XLA Ops:
  0.0 25.3 %shard_map.100 = (bf16[4,16,128,128]{3,2,1,0:T(8,128)(2,1)}, bf16[16,128,128]{2,1,0:T(8,128)(2,1)}, bf16[16,128,128]{2,1,0:T(8,128)(2,1)}, bf16[16,1024,128]{2,1,0:T(8,128)(2,1)}, bf16[16,1024,128]{2,1,0:T(8,128)(2,1)}) custom-call(bf16[128,4096]{1,0:T(8,128)(2,1)} %x_hbm.3, bf16[4096,2048]{1,0:T(8,128)(2,1)} %wq_hbm.1, bf16[4096,2048]{1,0:T(8,128)(2,1)} %wk_hbm.1, ...), custom_call_target="tpu_custom_call" | custom-call | flops 20000000000 | bytes 50331648 | tf_op jit(solution)/shard_map/pallas_call | solution.py:187
  25.3 20.0 %shard_map.101.suf_hbm = f32[17,128,128]{2,1,0:T(8,128)} custom-call(s32[128]{0:T(128)} %lens.1, bf16[4,16,128,128]{3,2,1,0:T(8,128)(2,1)} %get-tuple-element.10.q_hbm, bf16[16,128,128]{2,1,0:T(8,128)(2,1)} %get-tuple-element.13.kn_hbm, bf16[16,128,128]{2,1,0:T(8,128)(2,1)} %get-tuple-element.14.vn_hbm, bf16[512,256,128]{2,1,0:T(8,128)(2,1)} %bitcast.2, ...), custom_call_target="tpu_custom_call" | custom-call | flops 20000000000 | bytes 67108864 | tf_op jit(solution)/shard_map/pallas_call | solution.py:536
  45.4 49.7 %shard_map.102 = bf16[128,4096]{1,0:T(8,128)(2,1)} custom-call(bf16[4,16,128,128]{3,2,1,0:T(8,128)(2,1)} %get-tuple-element.10.q_hbm, bf16[16,1024,128]{2,1,0:T(8,128)(2,1)} %get-tuple-element.11.kt_hbm, bf16[16,1024,128]{2,1,0:T(8,128)(2,1)} %get-tuple-element.12.vt_hbm, f32[17,128,128]{2,1,0:T(8,128)} %shard_map.101.suf_hbm, bf16[128,4096]{1,0:T(8,128)(2,1)} %x_hbm.3, ...), custom_call_target="tpu_custom_call" | custom-call | flops 49999998976 | bytes 16777216 | tf_op jit(solution)/shard_map/pallas_call | solution.py:397
  95.1 2.3 %copy.12 = bf16[128,4096]{1,0:T(8,128)(2,1)} copy(bf16[128,4096]{1,0:T(8,128)(2,1)} %shard_map.102) | data formatting | bytes 2097152

commit v6 on v5

--- a/solution.py
+++ b/solution.py
@@ -85,62 +85,18 @@
                                         device_id=to, device_id_type=MESH)
 
 
-def _front_kernel(x_hbm, wq_hbm, wk_hbm, wv_hbm, kp_hbm, vp_hbm, q_hbm, kn_hbm, vn_hbm, kt_hbm, vt_hbm,
-                  x_ref, bufs, acc, raw, kt, vt, qs, kvn,
-                  xsem, sem, psem, osem, tsem, q_s, q_r):
-    heads, n_pos, d = kt.shape
-    ring, chunk, _ = bufs.shape
+def _front_kernel(x_hbm, wq_hbm, wk_hbm, wv_hbm, q_hbm, kn_hbm, vn_hbm,
+                  x_ref, bufs, acc, qs, kvn, xsem, sem, osem, q_s, q_r):
+    _, heads, _, d = qs.shape
     near, far = _peers()
-    n = x_hbm.shape[1] // chunk
-    pos = n_pos // (2 * n)
-    stages = 4
-    span = n_pos // stages
-
     cp = pltpu.make_async_copy(x_hbm, x_ref, xsem)
     cp.start()
-
-    hh = heads // 2
-    half = [pl.ds(j * hh, hh) for j in range(2)]
     q_near = _remote(qs.at[0], qs.at[1], q_s.at[0], q_r.at[0], ctx=near)
-    q_far = [_remote(qs.at[0, at], qs.at[2, at], q_s.at[1 + j], q_r.at[1 + j], ctx=far) for j, at in enumerate(half)]
-    q_diag = [_remote(qs.at[2, at], qs.at[3, at], q_s.at[3 + j], q_r.at[3 + j], ctx=near) for j, at in enumerate(half)]
+    q_far = _remote(qs.at[0], qs.at[2], q_s.at[1], q_r.at[1], ctx=far)
     outs = [pltpu.make_async_copy(qs.at[0], q_hbm.at[0], osem.at[0]),
             pltpu.make_async_copy(kvn.at[0], kn_hbm, osem.at[1]),
             pltpu.make_async_copy(kvn.at[1], vn_hbm, osem.at[2])]
-
-    def pieces(g):
-        at = pl.ds((g - n) * pos, pos)
-        slot = lax.rem(g, ring)
-        return [pltpu.make_async_copy(src.at[at], raw.at[slot, j], psem.at[slot, j])
-                for j, src in enumerate((kp_hbm, vp_hbm))]
-
-    def stores(t):
-        at = pl.ds(pl.multiple_of(t * span, span), span)
-        return [pltpu.make_async_copy(src.at[:, at], dst.at[:, at], tsem.at[j, t])
-                for j, (src, dst) in enumerate(((kt, kt_hbm), (vt, vt_hbm)))]
-
-    def extra_start(g):
-        @pl.when((g >= n) & (g < 3 * n))
-        def _():
-            for c in pieces(g):
-                c.start()
-
-    def extra_body(i, g):
-        if i == 0:
-            return
-        slot = lax.rem(g, ring)
-        for c in pieces(g):
-            c.wait()
-        for j, dst in enumerate((kt, vt)):
-            for u in range(pos // 16):
-                at = pl.multiple_of((g - n) * pos + u * 16, 16)
-                dst[:, pl.ds(at, 16), :] = jnp.swapaxes(raw[slot, j, u * 16:u * 16 + 16], 0, 1)
-        done = (g - n + 1) * pos
-
-        @pl.when(lax.rem(done, span) == 0)
-        def _():
-            for c in stores(done // span - 1):
-                c.start()
+    rest = [pltpu.make_async_copy(qs.at[j], q_hbm.at[j], osem.at[2 + j]) for j in (1, 2)]
 
     def emit(i):
         dst = qs.at[0] if i == 0 else kvn.at[i - 1]
@@ -148,61 +104,48 @@
             dst[h] = acc[:, h * d:(h + 1) * d].astype(BF16)
         if i == 0:
             pl.semaphore_wait(barrier, 2)
-            for c in (q_far[0], q_far[1], q_near):
-                c.start()
+            q_far.start()
+            q_near.start()
         outs[i].start()
 
-    prime, run = _stream(x_ref, [wq_hbm, wk_hbm, wv_hbm], bufs, sem, acc, emit, extra_start, extra_body)
+    prime, run = _stream(x_ref, [wq_hbm, wk_hbm, wv_hbm], bufs, sem, acc, emit)
     prime()
     barrier = pltpu.get_barrier_semaphore()
     for to in (near, far):
         pl.semaphore_signal(barrier, inc=1, device_id={'ctx': to}, device_id_type=MESH)
     cp.wait()
     run()
-
-    for j in range(2):
-        q_far[j].wait_recv()
-        q_diag[j].start()
-    q_near.wait_recv()
-    for c in q_diag:
+    for c, r in zip((q_near, q_far), rest):
         c.wait_recv()
-    rest = pltpu.make_async_copy(qs.at[pl.ds(1, 3)], q_hbm.at[pl.ds(1, 3)], xsem)
-    rest.start()
-    for c in outs + [rest]:
+        r.start()
+    for c in outs + rest:
         c.wait()
-    for t in range(stages):
-        for c in stores(t):
-            c.wait()
-    for c in [q_near] + q_far + q_diag:
-        c.wait_send()
-
-
-def _front(x, wq, wk, wv, kp, vp):
+    q_near.wait_send()
+    q_far.wait_send()
+
+
+def _front(x, wq, wk, wv, d):
     rows, depth = x.shape
     cols = wq.shape[1]
-    n, heads, d = kp.shape
-    pos = n // (2 * depth // CHUNK)
     dma = pltpu.SemaphoreType.DMA
-    blk = (heads, rows, d)
+    blk = (cols // d, rows, d)
     return pl.pallas_call(
         _front_kernel,
-        in_specs=[pl.BlockSpec(memory_space=pl.ANY)] * 6,
-        out_specs=[pl.BlockSpec(memory_space=pl.ANY)] * 5,
-        out_shape=[jax.ShapeDtypeStruct((4,) + blk, BF16)] + [jax.ShapeDtypeStruct(blk, BF16)] * 2
-        + [jax.ShapeDtypeStruct((heads, n, d), BF16)] * 2,
+        in_specs=[pl.BlockSpec(memory_space=pl.ANY)] * 4,
+        out_specs=[pl.BlockSpec(memory_space=pl.ANY)] * 3,
+        out_shape=[jax.ShapeDtypeStruct((3,) + blk, BF16)] + [jax.ShapeDtypeStruct(blk, BF16)] * 2,
         scratch_shapes=[
             VM((rows, depth), BF16), VM((RINGW, CHUNK, cols), BF16), VM((rows, cols), F32),
-            VM((RINGW, 2, pos, heads, d), BF16), VM((heads, n, d), BF16), VM((heads, n, d), BF16),
-            VM((4,) + blk, BF16), VM((2,) + blk, BF16),
-            dma, dma((RINGW,)), dma((RINGW, 2)), dma((3,)), dma((2, 4)), dma((5,)), dma((5,))],
+            VM((3,) + blk, BF16), VM((2,) + blk, BF16),
+            dma, dma((RINGW,)), dma((5,)), dma((2,)), dma((2,))],
         compiler_params=pltpu.CompilerParams(vmem_limit_bytes=LIMIT, collective_id=0, has_side_effects=True),
         cost_estimate=_cost(2e10, 6 * depth * cols),
-    )(x, wq, wk, wv, kp, vp)
-
-
-def _back_kernel(scale, q_hbm, kt_hbm, vt_hbm, suf_hbm, x_hbm, w_hbm, y_ref,
-                 qs, kt, vt, suf, x_ref, wo, ds, dr, ns, nr, fo, mo, xs, xr, xl, xlr, att, keep, ps, pr, sb, mb,
-                 qsem, ksem, wsem, d_s, d_r, n_s, n_r, x_s, x_r, p_s, p_r, y_s, y_r):
+    )(x, wq, wk, wv)
+
+
+def _back_kernel(scale, q_hbm, kp_hbm, vp_hbm, suf_hbm, x_hbm, w_hbm, y_hbm,
+                 y_ref, raw, qs, kt, vt, suf, x_ref, wo, ds, dr, ns, nr, fo, mo, xs, xr, xl, xlr, att, keep, ps, pr, sb, mb,
+                 qsem, ksem, wsem, osem, q_s, q_r, d_s, d_r, n_s, n_r, x_s, x_r, p_s, p_r, y_s, y_r):
     heads, n_pos, d = kt.shape
     rows = x_ref.shape[0]
     rh = rows // 2
@@ -218,17 +161,43 @@
     barrier = pltpu.get_barrier_semaphore()
     for to in ({'ctx': near}, {'ctx': far}, {'tp': 1 - tp}):
         pl.semaphore_signal(barrier, inc=1, device_id=to, device_id_type=MESH)
-    q_cp = pltpu.make_async_copy(q_hbm, qs, qsem.at[0])
-    q_cp.start()
-    kv_cp = [[pltpu.make_async_copy(src.at[pl.ds(i * group, group)], dst.at[pl.ds(i * group, group)], ksem.at[j, i])
-              for j, (src, dst) in enumerate(((kt_hbm, kt), (vt_hbm, vt)))] for i in range(steps)]
-    for cs in kv_cp:
-        for c in cs:
+    ring, _, pos = raw.shape[:3]
+    q_cp = [pltpu.make_async_copy(q_hbm.at[j], qs.at[j], qsem.at[2 + j]) for j in range(3)]
+    q_cp[2].start()
+
+    def piece(g):
+        slot = lax.rem(g, ring)
+        return [pltpu.make_async_copy(src.at[pl.ds(g * pos, pos)], raw.at[slot, j], ksem.at[slot, j])
+                for j, src in enumerate((kp_hbm, vp_hbm))]
+    for g in range(ring):
+        for c in piece(g):
             c.start()
-    suf_cp = pltpu.make_async_copy(suf_hbm, suf, qsem.at[1])
-    x_cp = pltpu.make_async_copy(x_hbm, x_ref, qsem.at[2])
+    q_cp[0].start()
+    q_cp[1].start()
+    suf_cp = pltpu.make_async_copy(suf_hbm, suf, qsem.at[0])
+    x_cp = pltpu.make_async_copy(x_hbm, x_ref, qsem.at[1])
     wr = w_hbm.shape[0] // 4
     w_cp = [pltpu.make_async_copy(w_hbm.at[pl.ds(i * wr, wr)], wo.at[pl.ds(i * wr, wr)], wsem.at[i]) for i in range(4)]
+    q_diag = _remote(qs.at[2], qs.at[3], q_s.at[0], q_r.at[0], ctx=near)
+    q_cp[2].wait()
+    pl.semaphore_wait(barrier, 3)
+    q_diag.start()
+
+    def relayout(g, c):
+        slot = lax.rem(g, ring)
+        for cp in piece(g):
+            cp.wait()
+        for j, dst in enumerate((kt, vt)):
+            for u in range(pos // 16):
+                to = pl.multiple_of(g * pos + u * 16, 16)
+                dst[:, pl.ds(to, 16), :] = jnp.swapaxes(raw[slot, j, u * 16:u * 16 + 16], 0, 1)
+
+        @pl.when(g + ring < n_pos // pos)
+        def _():
+            for cp in piece(g + ring):
+                cp.start()
+        return c
+    lax.fori_loop(0, n_pos // pos, relayout, 0)
     for c in [suf_cp, x_cp] + w_cp:
         c.start()
 
@@ -279,8 +248,8 @@
     def attend(a, i, q0, q1, dst0, dst1):
         for u in range(group):
             h = i * group + u
-            scores(a, jnp.minimum(h + 1, heads - 1), q0, q1, (u + 1) % 2)
-            weigh(h, u % 2, dst0, dst1)
+            scores(a, jnp.minimum(h + 1, heads - 1), q0, q1, (u + 1) % 4)
+            weigh(h, u % 4, dst0, dst1)
 
     def merge_far(a, i):
         d_copy(a, i).wait_recv()
@@ -302,22 +271,12 @@
             y_copy(a, j).start()
 
     xl[...] = jnp.zeros_like(xl)
-    q_cp.wait()
-    for cp in kv_cp[0]:
-        cp.wait()
+    q_cp[0].wait()
+    q_cp[1].wait()
+    q_diag.wait_recv()
     for a in range(2):
         def far_step(i, c):
-            if a == 0:
-                for k in range(steps - 1):
-                    @pl.when(i == k)
-                    def _():
-                        for cp in kv_cp[k + 1]:
-                            cp.wait()
             attend(a, i, 3, 2, ds.at[a], fo)
-            if a == 0:
-                @pl.when(i == 0)
-                def _():
-                    pl.semaphore_wait(barrier, 3)
             d_copy(a, i).start()
 
             @pl.when(i > 0)
@@ -375,9 +334,14 @@
         lax.fori_loop(0, blocks, keep_block, 0)
 
     add_peer(1)
+    outs = [pltpu.make_async_copy(y_ref.at[pl.ds(a * rh, rh)], y_hbm.at[pl.ds(a * rh, rh)], osem.at[a]) for a in range(2)]
     for a in range(2):
         for j in range(blocks):
             y_copy(a, j).wait_recv()
+        outs[a].start()
+    q_diag.wait_send()
+    for a in range(2):
+        for j in range(blocks):
             y_copy(a, j).wait_send()
             p_copy(a, j).wait_send()
         for i in range(steps):
@@ -385,11 +349,12 @@
             n_copy(a, i).wait_send()
             x_copy(a, i).wait_send()
         l_copy(a).wait_send()
-
-
-def _back(q, kt, vt, suf, x, w_o, scale):
+        outs[a].wait()
+
+
+def _back(q, kp, vp, suf, x, w_o, scale):
     _, heads, rows, d = q.shape
-    n = kt.shape[1]
+    n = kp.shape[0]
     depth, cols = w_o.shape
     dma = pltpu.SemaphoreType.DMA
     rh, wide, steps = rows // 2, 512, 4
@@ -397,20 +362,21 @@
     return pl.pallas_call(
         functools.partial(_back_kernel, scale),
         in_specs=[pl.BlockSpec(memory_space=pl.ANY)] * 6,
-        out_specs=pl.BlockSpec(memory_space=VM),
+        out_specs=pl.BlockSpec(memory_space=pl.ANY),
         out_shape=jax.ShapeDtypeStruct((rows, cols), BF16),
         scratch_shapes=[
-            VM(q.shape, BF16), VM(kt.shape, BF16), VM(vt.shape, BF16), VM(suf.shape, F32), VM((rows, cols), BF16),
+            VM((rows, cols), BF16), VM((4, 2, 128, heads, d), BF16),
+            VM((4, heads, rows, d), BF16), VM((heads, n, d), BF16), VM((heads, n, d), BF16), VM(suf.shape, F32), VM((rows, cols), BF16),
             VM(w_o.shape, BF16)]
         + [VM((2, heads, 2, rh, d), F32)] * 4 + [VM((heads, 2, rh, d), F32)] * 2
         + [VM((2, heads, rh, d), BF16)] * 2 + [VM((2, rh, d), F32)] * 2
         + [VM((rh, depth), BF16), VM((2, blocks, rh, wide), F32)] + [VM((2, blocks, rh, wide), BF16)] * 2
-        + [VM((2, rows, n), F32), VM((2, rows, d), F32)]
-        + [dma((3,)), dma((2, steps)), dma((4,))]
+        + [VM((4, rows, n), F32), VM((4, rows, d), F32)]
+        + [dma((5,)), dma((4, 2)), dma((4,)), dma((2,)), dma((1,)), dma((1,))]
         + [dma((2, steps))] * 4 + [dma((2, steps + 1))] * 2 + [dma((2, blocks))] * 4,
         compiler_params=pltpu.CompilerParams(vmem_limit_bytes=62 * 2**20, collective_id=1, has_side_effects=True),
         cost_estimate=_cost(5e10, 2 * depth * cols),
-    )(q, kt, vt, suf, x, w_o)
+    )(q, kp, vp, suf, x, w_o)
 
 
 def _suffix_kernel(scale, lens, q_hbm, kn_hbm, vn_hbm, k_hbm, v_hbm, o_ref,
@@ -431,7 +397,7 @@
         for j in range(per):
             items[BATCH + t + j] = b * per + j
         return t + (lens[b] + SLOTS - 1) // SLOTS
-    total = lax.fori_loop(0, rows, listing, 0)
+    total = lax.fori_loop(0, rows, listing, 0, unroll=4)
     for g in range(2 * BATCH):
         items[BATCH + total + g] = dummy
     batches = (total + BATCH - 1) // BATCH
@@ -561,9 +527,9 @@
     row_axes = ('dp', 'ctx')
     def device_step(hidden, w_q, w_k, w_v, w_o, k_prefix, v_prefix, k_suffix, v_suffix, seq_lens):
         scale = LOG2E * k_prefix.shape[2] ** -0.5
-        q, kn, vn, kt, vt = _front(hidden, w_q, w_k, w_v, k_prefix, v_prefix)
+        q, kn, vn = _front(hidden, w_q, w_k, w_v, k_prefix.shape[2])
         suf = _suffix(seq_lens, q, kn, vn, k_suffix, v_suffix, scale)
-        return _back(q, kt, vt, suf, hidden, w_o, scale)
+        return _back(q, k_prefix, v_prefix, suf, hidden, w_o, scale)
 
     spec_in = (P(row_axes, None), P(None, 'tp'), P(None, 'tp'), P(None, 'tp'), P('tp', None),
                P(row_axes, 'tp', None), P(row_axes, 'tp', None), P(row_axes, None, 'tp', None),

time: 98.2 us -> 94.2 us (0.959)
  Pallas kernels: 95.1 us -> 91.8 us
    pallas_call x1, Pallas kernels: 25.3 us -> 23.1 us  [_front(): pl.pallas_call(_front_kernel, in_specs=[pl.BlockSpec(memory_space=pl.ANY)...]
    pallas_call x1, Pallas kernels: 49.7 us -> 48.2 us  [_back(): pl.pallas_call(functools.partial(_back_kernel, scale), in_specs=[pl.Block...]
where the time goes in v6:
time: 94.2 us; the launch traced here: 94.1 us
  Pallas kernels  91.8 us (97%)
  local copies, waits for them, and re-layouts  2.29 us (2%)
    pallas_call x1, Pallas kernels, _back(): pl.pallas_call(functools.partial(_back_kernel, scale), in_specs=[pl.Block...  48.2 us
    pallas_call x1, Pallas kernels, _front(): pl.pallas_call(_front_kernel, in_specs=[pl.BlockSpec(memory_space=pl.ANY)...  23.1 us
    pallas_call x1, Pallas kernels, _suffix(): pl.pallas_call(functools.partial(_suffix_kernel, scale), in_specs=[pl.Blo...  20.6 us
    unnamed x1, local copies, waits for them, and re-layouts  2.29 us

profile of v6, /device:TPU:0, one launch (start us, length us, event | category | flops | bytes accessed | tf_op | source)
XLA Modules:
  0.0 94.1 jit_solution(14418656567761560302)
XLA Ops:
  0.0 23.1 %shard_map.100 = (bf16[3,16,128,128]{3,2,1,0:T(8,128)(2,1)}, bf16[16,128,128]{2,1,0:T(8,128)(2,1)}, bf16[16,128,128]{2,1,0:T(8,128)(2,1)}) custom-call(bf16[128,4096]{1,0:T(8,128)(2,1)} %x_hbm.3, bf16[4096,2048]{1,0:T(8,128)(2,1)} %wq_hbm.1, bf16[4096,2048]{1,0:T(8,128)(2,1)} %wk_hbm.1, bf16[4096,2048]{1,0:T(8,128)(2,1)} %wv_hbm.1), custom_call_target="tpu_custom_call" | custom-call | flops 20000000000 | bytes 50331648 | tf_op jit(solution)/shard_map/pallas_call | solution.py:132
  23.1 20.6 %shard_map.101.suf_hbm = f32[17,128,128]{2,1,0:T(8,128)} custom-call(s32[128]{0:T(128)} %lens.1, bf16[3,16,128,128]{3,2,1,0:T(8,128)(2,1)} %get-tuple-element.8.q_hbm, bf16[16,128,128]{2,1,0:T(8,128)(2,1)} %get-tuple-element.9.kn_hbm, bf16[16,128,128]{2,1,0:T(8,128)(2,1)} %get-tuple-element.10.vn_hbm, bf16[512,256,128]{2,1,0:T(8,128)(2,1)} %bitcast.2, ...), custom_call_target="tpu_custom_call" | custom-call | flops 20000000000 | bytes 67108864 | tf_op jit(solution)/shard_map/pallas_call | solution.py:502
  43.7 48.2 %shard_map.102 = bf16[128,4096]{1,0:T(8,128)(2,1)} custom-call(bf16[3,16,128,128]{3,2,1,0:T(8,128)(2,1)} %get-tuple-element.8.q_hbm, bf16[1024,16,128]{2,1,0:T(8,128)(2,1)} %kp_hbm.1, bf16[1024,16,128]{2,1,0:T(8,128)(2,1)} %vp_hbm.1, f32[17,128,128]{2,1,0:T(8,128)} %shard_map.101.suf_hbm, bf16[128,4096]{1,0:T(8,128)(2,1)} %x_hbm.3, bf16[2048,4096]{1,0:T(8,128)(2,1)} %w_hbm.1), custom_call_target="tpu_custom_call" | custom-call | flops 49999998976 | bytes 16777216 | tf_op jit(solution)/shard_map/pallas_call | solution.py:362
  91.9 2.3 %copy.12 = bf16[128,4096]{1,0:T(8,128)(2,1)} copy(bf16[128,4096]{1,0:T(8,128)(2,1)} %shard_map.102) | data formatting | bytes 2097152

commit v7 on v6

--- a/solution.py
+++ b/solution.py
@@ -15,7 +15,7 @@
 SLOTS = 16
 RING = 5
 CHUNK = 512
-RINGW = 5
+RINGW = 6
 LIMIT = 56 * 2**20
 
 
@@ -34,7 +34,7 @@
 
 
 def _stream(x_ref, ws, bufs, sem, acc, emit, extra_start=None, extra_body=None):
-    ring, chunk, cols = bufs.shape
+    ring, chunk, _ = bufs.shape
     n = ws[0].shape[0] // chunk
     total = n * len(ws)
     part = 512
@@ -45,7 +45,7 @@
             @pl.when((g >= i * n) & (g < (i + 1) * n))
             def _():
                 at = pl.multiple_of((g - i * n) * chunk, chunk)
-                pltpu.make_async_copy(w.at[pl.ds(at, chunk)], bufs.at[slot], sem.at[slot]).start()
+                pltpu.make_async_copy(w.at[pl.ds(at, chunk)], bufs.at[slot, :, :w.shape[1]], sem.at[slot]).start()
         if extra_start is not None:
             extra_start(g)
 
@@ -57,12 +57,13 @@
 
     def run():
         for i, w in enumerate(ws):
+            cols = w.shape[1]
             acc[...] = jnp.zeros_like(acc)
 
             def body(c, carry):
                 g = i * n + c
                 slot = lax.rem(g, ring)
-                pltpu.make_async_copy(w.at[pl.ds(0, chunk)], bufs.at[slot], sem.at[slot]).wait()
+                pltpu.make_async_copy(w.at[pl.ds(0, chunk)], bufs.at[slot, :, :cols], sem.at[slot]).wait()
                 x = x_ref[:, pl.ds(pl.multiple_of(c * chunk, chunk), chunk)]
                 for j in range(0, cols, part):
                     acc[:, j:j + part] += _dot(x, bufs[slot, :, j:j + part])
@@ -91,37 +92,45 @@
     near, far = _peers()
     cp = pltpu.make_async_copy(x_hbm, x_ref, xsem)
     cp.start()
-    q_near = _remote(qs.at[0], qs.at[1], q_s.at[0], q_r.at[0], ctx=near)
-    q_far = _remote(qs.at[0], qs.at[2], q_s.at[1], q_r.at[1], ctx=far)
+    hh = heads // 2
+    half = [pl.ds(j * hh, hh) for j in range(2)]
+    q_near = [_remote(qs.at[0, at], qs.at[1, at], q_s.at[0, j], q_r.at[0, j], ctx=near) for j, at in enumerate(half)]
+    q_far = [_remote(qs.at[0, at], qs.at[2, at], q_s.at[1, j], q_r.at[1, j], ctx=far) for j, at in enumerate(half)]
     outs = [pltpu.make_async_copy(qs.at[0], q_hbm.at[0], osem.at[0]),
             pltpu.make_async_copy(kvn.at[0], kn_hbm, osem.at[1]),
             pltpu.make_async_copy(kvn.at[1], vn_hbm, osem.at[2])]
     rest = [pltpu.make_async_copy(qs.at[j], q_hbm.at[j], osem.at[2 + j]) for j in (1, 2)]
 
     def emit(i):
-        dst = qs.at[0] if i == 0 else kvn.at[i - 1]
-        for h in range(heads):
-            dst[h] = acc[:, h * d:(h + 1) * d].astype(BF16)
-        if i == 0:
-            pl.semaphore_wait(barrier, 2)
-            q_far.start()
-            q_near.start()
-        outs[i].start()
-
-    prime, run = _stream(x_ref, [wq_hbm, wk_hbm, wv_hbm], bufs, sem, acc, emit)
+        if i < 2:
+            for h in range(hh):
+                qs[0, i * hh + h] = acc[:, h * d:(h + 1) * d].astype(BF16)
+            if i == 0:
+                pl.semaphore_wait(barrier, 2)
+            q_far[i].start()
+            q_near[i].start()
+        else:
+            for h in range(heads):
+                kvn[i - 2, h] = acc[:, h * d:(h + 1) * d].astype(BF16)
+        if i > 0:
+            outs[i - 1].start()
+
+    wq_half = [wq_hbm.at[:, pl.ds(j * hh * d, hh * d)] for j in range(2)]
+    prime, run = _stream(x_ref, wq_half + [wk_hbm, wv_hbm], bufs, sem, acc, emit)
     prime()
     barrier = pltpu.get_barrier_semaphore()
     for to in (near, far):
         pl.semaphore_signal(barrier, inc=1, device_id={'ctx': to}, device_id_type=MESH)
     cp.wait()
     run()
-    for c, r in zip((q_near, q_far), rest):
-        c.wait_recv()
+    for cs, r in zip((q_near, q_far), rest):
+        for c in cs:
+            c.wait_recv()
         r.start()
     for c in outs + rest:
         c.wait()
-    q_near.wait_send()
-    q_far.wait_send()
+    for c in q_near + q_far:
+        c.wait_send()
 
 
 def _front(x, wq, wk, wv, d):
@@ -137,20 +146,19 @@
         scratch_shapes=[
             VM((rows, depth), BF16), VM((RINGW, CHUNK, cols), BF16), VM((rows, cols), F32),
             VM((3,) + blk, BF16), VM((2,) + blk, BF16),
-            dma, dma((RINGW,)), dma((5,)), dma((2,)), dma((2,))],
+            dma, dma((RINGW,)), dma((5,)), dma((2, 2)), dma((2, 2))],
         compiler_params=pltpu.CompilerParams(vmem_limit_bytes=LIMIT, collective_id=0, has_side_effects=True),
         cost_estimate=_cost(2e10, 6 * depth * cols),
     )(x, wq, wk, wv)
 
 
-def _back_kernel(scale, q_hbm, kp_hbm, vp_hbm, suf_hbm, x_hbm, w_hbm, y_hbm,
-                 y_ref, raw, qs, kt, vt, suf, x_ref, wo, ds, dr, ns, nr, fo, mo, xs, xr, xl, xlr, att, keep, ps, pr, sb, mb,
+def _back_kernel(scale, q_hbm, kp_hbm, vp_hbm, suf_hbm, x_hbm, w_hbm, mine_hbm, other_hbm,
+                 mine, other, raw, qs, kt, vt, suf, x_ref, wo, ds, dr, ns, nr, fo, mo, xs, xr, xl, xlr, att, keep, ps, pr, sb, mb,
                  qsem, ksem, wsem, osem, q_s, q_r, d_s, d_r, n_s, n_r, x_s, x_r, p_s, p_r, y_s, y_r):
     heads, n_pos, d = kt.shape
     rows = x_ref.shape[0]
     rh = rows // 2
-    cols = x_ref.shape[1]
-    half = cols // 2
+    half = x_ref.shape[1] // 2
     near, far = _peers()
     tp = lax.axis_index('tp')
     steps = 4
@@ -222,8 +230,8 @@
         return _remote(ps.at[a, j], pr.at[a, j], p_s.at[a, j], p_r.at[a, j], tp=1 - tp)
 
     def y_copy(a, j):
-        at = (pl.ds(a * rh, rh), pl.ds(pl.multiple_of(tp * half + j * wide, wide), wide))
-        return _remote(y_ref.at[at], y_ref.at[at], y_s.at[a, j], y_r.at[a, j], tp=1 - tp)
+        at = (pl.ds(a * rh, rh), pl.ds(j * wide, wide))
+        return _remote(mine.at[at], other.at[at], y_s.at[a, j], y_r.at[a, j], tp=1 - tp)
 
     def scores(a, h, q0, q1, slot):
         at = slice(a * rh, (a + 1) * rh)
@@ -267,7 +275,7 @@
         for j in range(blocks):
             p_copy(a, j).wait_recv()
             y = (keep[a, j] + pr[a, j].astype(F32)).astype(BF16)
-            y_ref[a * rh:(a + 1) * rh, pl.ds(pl.multiple_of(tp * half + j * wide, wide), wide)] = y
+            mine[a * rh:(a + 1) * rh, j * wide:(j + 1) * wide] = y
             y_copy(a, j).start()
 
     xl[...] = jnp.zeros_like(xl)
@@ -334,11 +342,14 @@
         lax.fori_loop(0, blocks, keep_block, 0)
 
     add_peer(1)
-    outs = [pltpu.make_async_copy(y_ref.at[pl.ds(a * rh, rh)], y_hbm.at[pl.ds(a * rh, rh)], osem.at[a]) for a in range(2)]
+    outs = [pltpu.make_async_copy(mine, mine_hbm, osem.at[2])]
+    outs[0].start()
     for a in range(2):
         for j in range(blocks):
             y_copy(a, j).wait_recv()
-        outs[a].start()
+        at = pl.ds(a * rh, rh)
+        outs.append(pltpu.make_async_copy(other.at[at], other_hbm.at[at], osem.at[a]))
+        outs[-1].start()
     q_diag.wait_send()
     for a in range(2):
         for j in range(blocks):
@@ -349,7 +360,8 @@
             n_copy(a, i).wait_send()
             x_copy(a, i).wait_send()
         l_copy(a).wait_send()
-        outs[a].wait()
+    for c in outs:
+        c.wait()
 
 
 def _back(q, kp, vp, suf, x, w_o, scale):
@@ -362,17 +374,17 @@
     return pl.pallas_call(
         functools.partial(_back_kernel, scale),
         in_specs=[pl.BlockSpec(memory_space=pl.ANY)] * 6,
-        out_specs=pl.BlockSpec(memory_space=pl.ANY),
-        out_shape=jax.ShapeDtypeStruct((rows, cols), BF16),
+        out_specs=[pl.BlockSpec(memory_space=pl.ANY)] * 2,
+        out_shape=[jax.ShapeDtypeStruct((rows, cols // 2), BF16)] * 2,
         scratch_shapes=[
-            VM((rows, cols), BF16), VM((4, 2, 128, heads, d), BF16),
+            VM((rows, cols // 2), BF16), VM((rows, cols // 2), BF16), VM((4, 2, 128, heads, d), BF16),
             VM((4, heads, rows, d), BF16), VM((heads, n, d), BF16), VM((heads, n, d), BF16), VM(suf.shape, F32), VM((rows, cols), BF16),
             VM(w_o.shape, BF16)]
         + [VM((2, heads, 2, rh, d), F32)] * 4 + [VM((heads, 2, rh, d), F32)] * 2
         + [VM((2, heads, rh, d), BF16)] * 2 + [VM((2, rh, d), F32)] * 2
         + [VM((rh, depth), BF16), VM((2, blocks, rh, wide), F32)] + [VM((2, blocks, rh, wide), BF16)] * 2
         + [VM((4, rows, n), F32), VM((4, rows, d), F32)]
-        + [dma((5,)), dma((4, 2)), dma((4,)), dma((2,)), dma((1,)), dma((1,))]
+        + [dma((5,)), dma((4, 2)), dma((4,)), dma((3,)), dma((1,)), dma((1,))]
         + [dma((2, steps))] * 4 + [dma((2, steps + 1))] * 2 + [dma((2, blocks))] * 4,
         compiler_params=pltpu.CompilerParams(vmem_limit_bytes=62 * 2**20, collective_id=1, has_side_effects=True),
         cost_estimate=_cost(5e10, 2 * depth * cols),
@@ -387,6 +399,7 @@
     for c in news:
         c.start()
     per = k_hbm.shape[0] // rows
+    shift = per.bit_length() - 1
     wide = SLOTS * heads
     dummy = rows * per
 
@@ -443,8 +456,8 @@
 
         for g in range(BATCH):
             it = items[BATCH + i * BATCH + g]
-            b = it // per
-            left = lens[jnp.minimum(b, rows - 1)] - lax.rem(it, per) * SLOTS
+            b = lax.shift_right_logical(it, shift)
+            left = lens[jnp.minimum(b, rows - 1)] - (it & (per - 1)) * SLOTS
             s = _dot(qb[b], kbuf[slot, g], NT) * scale
             sbuf[par, g] = jnp.where(slot_of < left, s, -jnp.inf)
 
@@ -462,7 +475,7 @@
             parts[g][2] = o[:heads, :d]
             parts[g + 1][2] = o[heads:, d:]
         for g in range(BATCH):
-            b = items[i * BATCH + g] // per
+            b = lax.shift_right_logical(items[i * BATCH + g], shift)
             m, l, o = parts[g]
             m_old = m_s[b]
             m_new = jnp.maximum(m_old, m)
@@ -529,7 +542,9 @@
         scale = LOG2E * k_prefix.shape[2] ** -0.5
         q, kn, vn = _front(hidden, w_q, w_k, w_v, k_prefix.shape[2])
         suf = _suffix(seq_lens, q, kn, vn, k_suffix, v_suffix, scale)
-        return _back(q, k_prefix, v_prefix, suf, hidden, w_o, scale)
+        mine, other = _back(q, k_prefix, v_prefix, suf, hidden, w_o, scale)
+        return jnp.where(lax.axis_index('tp') == 0, jnp.concatenate([mine, other], axis=1),
+                         jnp.concatenate([other, mine], axis=1))
 
     spec_in = (P(row_axes, None), P(None, 'tp'), P(None, 'tp'), P(None, 'tp'), P('tp', None),
                P(row_axes, 'tp', None), P(row_axes, 'tp', None), P(row_axes, None, 'tp', None),

time: 94.2 us -> 91.1 us (0.967)
  Pallas kernels: 91.8 us -> 87.7 us
  other arithmetic: 0 us -> 2.74 us
  local copies, waits for them, and re-layouts: 2.29 us -> 0 us
    select_n x0 -> x1, other arithmetic: none -> 2.74 us  [device_step(): jnp.where(lax.axis_index('tp') == 0, jnp.concatenate([mine, other], axis=...]
    pallas_call x1, Pallas kernels: 23.1 us -> 20.5 us  [_front(): pl.pallas_call(_front_kernel, in_specs=[pl.BlockSpec(memory_space=pl.ANY)...]
    unnamed x1 -> x0, local copies, waits for them, and re-layouts: 2.29 us -> none
    pallas_call x1, Pallas kernels: 20.6 us -> 18.7 us  [_suffix(): pl.pallas_call(functools.partial(_suffix_kernel, scale), in_specs=[pl.Blo...]
where the time goes in v7:
time: 91.1 us; the launch traced here: 90.5 us
  Pallas kernels  87.7 us (96%)
  other arithmetic  2.74 us (3%)
    pallas_call x1, Pallas kernels, _back(): pl.pallas_call(functools.partial(_back_kernel, scale), in_specs=[pl.Block...  48.5 us
    pallas_call x1, Pallas kernels, _front(): pl.pallas_call(_front_kernel, in_specs=[pl.BlockSpec(memory_space=pl.ANY)...  20.5 us
    pallas_call x1, Pallas kernels, _suffix(): pl.pallas_call(functools.partial(_suffix_kernel, scale), in_specs=[pl.Blo...  18.7 us
    select_n x1, other arithmetic, device_step(): jnp.where(lax.axis_index('tp') == 0, jnp.concatenate([mine, other], axis=...  2.74 us

profile of v7, /device:TPU:0, one launch (start us, length us, event | category | flops | bytes accessed | tf_op | source)
XLA Modules:
  0.0 90.5 jit_solution(3087610209100594983)
XLA Ops:
  0.0 20.5 %shard_map.100 = (bf16[3,16,128,128]{3,2,1,0:T(8,128)(2,1)}, bf16[16,128,128]{2,1,0:T(8,128)(2,1)}, bf16[16,128,128]{2,1,0:T(8,128)(2,1)}) custom-call(bf16[128,4096]{1,0:T(8,128)(2,1)} %x_hbm.3, bf16[4096,2048]{1,0:T(8,128)(2,1)} %wq_hbm.1, bf16[4096,2048]{1,0:T(8,128)(2,1)} %wk_hbm.1, bf16[4096,2048]{1,0:T(8,128)(2,1)} %wv_hbm.1), custom_call_target="tpu_custom_call" | custom-call | flops 20000000000 | bytes 50331648 | tf_op jit(solution)/shard_map/pallas_call | solution.py:141
  20.5 18.7 %shard_map.101.suf_hbm = f32[17,128,128]{2,1,0:T(8,128)} custom-call(s32[128]{0:T(128)} %lens.1, bf16[3,16,128,128]{3,2,1,0:T(8,128)(2,1)} %get-tuple-element.10.q_hbm, bf16[16,128,128]{2,1,0:T(8,128)(2,1)} %get-tuple-element.11.kn_hbm, bf16[16,128,128]{2,1,0:T(8,128)(2,1)} %get-tuple-element.12.vn_hbm, bf16[512,256,128]{2,1,0:T(8,128)(2,1)} %bitcast.2, ...), custom_call_target="tpu_custom_call" | custom-call | flops 20000000000 | bytes 67108864 | tf_op jit(solution)/shard_map/pallas_call | solution.py:515
  39.2 48.5 %shard_map.102 = (bf16[128,2048]{1,0:T(8,128)(2,1)}, bf16[128,2048]{1,0:T(8,128)(2,1)}) custom-call(bf16[3,16,128,128]{3,2,1,0:T(8,128)(2,1)} %get-tuple-element.10.q_hbm, bf16[1024,16,128]{2,1,0:T(8,128)(2,1)} %kp_hbm.1, bf16[1024,16,128]{2,1,0:T(8,128)(2,1)} %vp_hbm.1, f32[17,128,128]{2,1,0:T(8,128)} %shard_map.101.suf_hbm, bf16[128,4096]{1,0:T(8,128)(2,1)} %x_hbm.3, ...), custom_call_target="tpu_custom_call" | custom-call | flops 49999998976 | bytes 16777216 | tf_op jit(solution)/shard_map/pallas_call | solution.py:374
  87.7 2.7 %maximum_select_fusion = bf16[128,4096]{1,0:T(8,128)(2,1)} fusion(bf16[128,2048]{1,0:T(8,128)(2,1)} %get-tuple-element.14, bf16[128,2048]{1,0:T(8,128)(2,1)} %get-tuple-element.13, pred[]{:T(512)S(6)} %eq.3), kind=kLoop, calls=%fused_computation | loop fusion | flops 4718592 | bytes 2097153 | tf_op jit(solution)/shard_map/jit(_where)/select_n | solution.py:546

commit v8 on v7

--- a/solution.py
+++ b/solution.py
@@ -152,8 +152,8 @@
     )(x, wq, wk, wv)
 
 
-def _back_kernel(scale, q_hbm, kp_hbm, vp_hbm, suf_hbm, x_hbm, w_hbm, mine_hbm, other_hbm,
-                 mine, other, raw, qs, kt, vt, suf, x_ref, wo, ds, dr, ns, nr, fo, mo, xs, xr, xl, xlr, att, keep, ps, pr, sb, mb,
+def _back_kernel(scale, q_hbm, kp_hbm, vp_hbm, suf_hbm, x_hbm, w_hbm, y_hbm,
+                 y_ref, raw, qs, kt, vt, suf, x_ref, wo, ds, dr, ns, nr, fo, mo, xs, xr, xl, xlr, att, keep, ps, pr, sb, mb,
                  qsem, ksem, wsem, osem, q_s, q_r, d_s, d_r, n_s, n_r, x_s, x_r, p_s, p_r, y_s, y_r):
     heads, n_pos, d = kt.shape
     rows = x_ref.shape[0]
@@ -187,9 +187,6 @@
     wr = w_hbm.shape[0] // 4
     w_cp = [pltpu.make_async_copy(w_hbm.at[pl.ds(i * wr, wr)], wo.at[pl.ds(i * wr, wr)], wsem.at[i]) for i in range(4)]
     q_diag = _remote(qs.at[2], qs.at[3], q_s.at[0], q_r.at[0], ctx=near)
-    q_cp[2].wait()
-    pl.semaphore_wait(barrier, 3)
-    q_diag.start()
 
     def relayout(g, c):
         slot = lax.rem(g, ring)
@@ -205,7 +202,11 @@
             for cp in piece(g + ring):
                 cp.start()
         return c
-    lax.fori_loop(0, n_pos // pos, relayout, 0)
+    lax.fori_loop(0, ring, relayout, 0)
+    q_cp[2].wait()
+    pl.semaphore_wait(barrier, 3)
+    q_diag.start()
+    lax.fori_loop(ring, n_pos // pos, relayout, 0)
     for c in [suf_cp, x_cp] + w_cp:
         c.start()
 
@@ -230,8 +231,8 @@
         return _remote(ps.at[a, j], pr.at[a, j], p_s.at[a, j], p_r.at[a, j], tp=1 - tp)
 
     def y_copy(a, j):
-        at = (pl.ds(a * rh, rh), pl.ds(j * wide, wide))
-        return _remote(mine.at[at], other.at[at], y_s.at[a, j], y_r.at[a, j], tp=1 - tp)
+        at = (pl.ds(a * rh, rh), pl.ds(pl.multiple_of(tp * half + j * wide, wide), wide))
+        return _remote(y_ref.at[at], y_ref.at[at], y_s.at[a, j], y_r.at[a, j], tp=1 - tp)
 
     def scores(a, h, q0, q1, slot):
         at = slice(a * rh, (a + 1) * rh)
@@ -275,7 +276,7 @@
         for j in range(blocks):
             p_copy(a, j).wait_recv()
             y = (keep[a, j] + pr[a, j].astype(F32)).astype(BF16)
-            mine[a * rh:(a + 1) * rh, j * wide:(j + 1) * wide] = y
+            y_ref[a * rh:(a + 1) * rh, pl.ds(pl.multiple_of(tp * half + j * wide, wide), wide)] = y
             y_copy(a, j).start()
 
     xl[...] = jnp.zeros_like(xl)
@@ -342,13 +343,12 @@
         lax.fori_loop(0, blocks, keep_block, 0)
 
     add_peer(1)
-    outs = [pltpu.make_async_copy(mine, mine_hbm, osem.at[2])]
-    outs[0].start()
+    outs = []
     for a in range(2):
         for j in range(blocks):
             y_copy(a, j).wait_recv()
         at = pl.ds(a * rh, rh)
-        outs.append(pltpu.make_async_copy(other.at[at], other_hbm.at[at], osem.at[a]))
+        outs.append(pltpu.make_async_copy(y_ref.at[at], y_hbm.at[at], osem.at[a]))
         outs[-1].start()
     q_diag.wait_send()
     for a in range(2):
@@ -374,25 +374,25 @@
     return pl.pallas_call(
         functools.partial(_back_kernel, scale),
         in_specs=[pl.BlockSpec(memory_space=pl.ANY)] * 6,
-        out_specs=[pl.BlockSpec(memory_space=pl.ANY)] * 2,
-        out_shape=[jax.ShapeDtypeStruct((rows, cols // 2), BF16)] * 2,
+        out_specs=pl.BlockSpec(memory_space=pl.ANY),
+        out_shape=jax.ShapeDtypeStruct((rows, cols), BF16),
         scratch_shapes=[
-            VM((rows, cols // 2), BF16), VM((rows, cols // 2), BF16), VM((4, 2, 128, heads, d), BF16),
+            VM((rows, cols), BF16), VM((4, 2, 128, heads, d), BF16),
             VM((4, heads, rows, d), BF16), VM((heads, n, d), BF16), VM((heads, n, d), BF16), VM(suf.shape, F32), VM((rows, cols), BF16),
             VM(w_o.shape, BF16)]
         + [VM((2, heads, 2, rh, d), F32)] * 4 + [VM((heads, 2, rh, d), F32)] * 2
         + [VM((2, heads, rh, d), BF16)] * 2 + [VM((2, rh, d), F32)] * 2
         + [VM((rh, depth), BF16), VM((2, blocks, rh, wide), F32)] + [VM((2, blocks, rh, wide), BF16)] * 2
         + [VM((4, rows, n), F32), VM((4, rows, d), F32)]
-        + [dma((5,)), dma((4, 2)), dma((4,)), dma((3,)), dma((1,)), dma((1,))]
+        + [dma((5,)), dma((4, 2)), dma((4,)), dma((2,)), dma((1,)), dma((1,))]
         + [dma((2, steps))] * 4 + [dma((2, steps + 1))] * 2 + [dma((2, blocks))] * 4,
         compiler_params=pltpu.CompilerParams(vmem_limit_bytes=62 * 2**20, collective_id=1, has_side_effects=True),
         cost_estimate=_cost(5e10, 2 * depth * cols),
     )(q, kp, vp, suf, x, w_o)
 
 
-def _suffix_kernel(scale, lens, q_hbm, kn_hbm, vn_hbm, k_hbm, v_hbm, o_ref,
-                   new, newsem, items, qb, acc, m_s, l_s, kbuf, vbuf, sbuf, ksem, vsem):
+def _suffix_kernel(scale, lens, q_hbm, kn_hbm, vn_hbm, k_hbm, v_hbm, o_hbm,
+                   o_ref, osem, new, newsem, items, qb, acc, m_s, l_s, kbuf, vbuf, sbuf, ksem, vsem):
     _, heads, rows, d = new.shape
     news = [pltpu.make_async_copy(src, new.at[j], newsem.at[j])
             for j, src in enumerate((q_hbm.at[0], kn_hbm, vn_hbm))]
@@ -410,11 +410,6 @@
         for j in range(per):
             items[BATCH + t + j] = b * per + j
         return t + (lens[b] + SLOTS - 1) // SLOTS
-    total = lax.fori_loop(0, rows, listing, 0, unroll=4)
-    for g in range(2 * BATCH):
-        items[BATCH + total + g] = dummy
-    batches = (total + BATCH - 1) // BATCH
-
     def fetch(i):
         slot = lax.rem(i, RING)
         for g in range(BATCH):
@@ -425,7 +420,14 @@
     def prime(i, c):
         fetch(i)
         return c
-    lax.fori_loop(0, jnp.minimum(batches, RING - 1), prime, 0)
+    some = lax.fori_loop(0, rows // 4, listing, 0, unroll=4)
+    early = jnp.minimum(some // BATCH, RING - 1)
+    lax.fori_loop(0, early, prime, 0)
+    total = lax.fori_loop(rows // 4, rows, listing, some, unroll=4)
+    for g in range(2 * BATCH):
+        items[BATCH + total + g] = dummy
+    batches = (total + BATCH - 1) // BATCH
+    lax.fori_loop(early, jnp.minimum(batches, RING - 1), prime, 0)
 
     for c in news:
         c.wait()
@@ -492,6 +494,10 @@
 
     lax.fori_loop(0, batches + 1, step, 0)
 
+    def leave(c):
+        at = pl.ds(c * 16, 16)
+        return pltpu.make_async_copy(o_ref.at[:, at], o_hbm.at[:, at], osem.at[c])
+
     lane = lax.broadcasted_iota(jnp.int32, (16, 128), 1)
     for c in range(rows // 16):
         l = l_s[c * 16:c * 16 + 16]
@@ -503,6 +509,9 @@
         for h in range(heads):
             out = jnp.where(lane == h, lse[h], out)
         o_ref[heads, c * 16:c * 16 + 16, :] = out
+        leave(c).start()
+    for c in range(rows // 16):
+        leave(c).wait()
 
 
 def _suffix(lens, q, kn, vn, k, v, scale):
@@ -515,9 +524,11 @@
     return pl.pallas_call(
         functools.partial(_suffix_kernel, scale),
         in_specs=[pl.BlockSpec(memory_space=pltpu.SMEM)] + [pl.BlockSpec(memory_space=pl.ANY)] * 5,
-        out_specs=pl.BlockSpec(memory_space=VM),
+        out_specs=pl.BlockSpec(memory_space=pl.ANY),
         out_shape=jax.ShapeDtypeStruct((heads + 1, rows, d), F32),
         scratch_shapes=[
+            VM((heads + 1, rows, d), F32),
+            pltpu.SemaphoreType.DMA((rows // 16,)),
             VM((3, heads, rows, d), BF16),
             pltpu.SemaphoreType.DMA((3,)),
             pltpu.SMEM((rows * per + 4 * BATCH,), jnp.int32),
@@ -542,9 +553,7 @@
         scale = LOG2E * k_prefix.shape[2] ** -0.5
         q, kn, vn = _front(hidden, w_q, w_k, w_v, k_prefix.shape[2])
         suf = _suffix(seq_lens, q, kn, vn, k_suffix, v_suffix, scale)
-        mine, other = _back(q, k_prefix, v_prefix, suf, hidden, w_o, scale)
-        return jnp.where(lax.axis_index('tp') == 0, jnp.concatenate([mine, other], axis=1),
-                         jnp.concatenate([other, mine], axis=1))
+        return _back(q, k_prefix, v_prefix, suf, hidden, w_o, scale)
 
     spec_in = (P(row_axes, None), P(None, 'tp'), P(None, 'tp'), P(None, 'tp'), P('tp', None),
                P(row_axes, 'tp', None), P(row_axes, 'tp', None), P(row_axes, None, 'tp', None),

time: 91.1 us -> 90.7 us (level)
  other arithmetic: 2.74 us -> 0 us
  local copies, waits for them, and re-layouts: 0 us -> 2.29 us
    select_n x1 -> x0, other arithmetic: 2.74 us -> none  [device_step(): jnp.where(lax.axis_index('tp') == 0, jnp.concatenate([mine, other], axis=...]
    unnamed x0 -> x1, local copies, waits for them, and re-layouts: none -> 2.29 us
    pallas_call x1, Pallas kernels: 18.7 us -> 19.8 us  [_suffix(): pl.pallas_call(functools.partial(_suffix_kernel, scale), in_specs=[pl.Blo...]
where the time goes in v8:
time: 90.7 us; the launch traced here: 90.9 us
  Pallas kernels  88.5 us (98%)
  local copies, waits for them, and re-layouts  2.29 us (3%)
    pallas_call x1, Pallas kernels, _back(): pl.pallas_call(functools.partial(_back_kernel, scale), in_specs=[pl.Block...  48.2 us
    pallas_call x1, Pallas kernels, _front(): pl.pallas_call(_front_kernel, in_specs=[pl.BlockSpec(memory_space=pl.ANY)...  20.6 us
    pallas_call x1, Pallas kernels, _suffix(): pl.pallas_call(functools.partial(_suffix_kernel, scale), in_specs=[pl.Blo...  19.8 us
    unnamed x1, local copies, waits for them, and re-layouts  2.29 us

profile of v8, /device:TPU:0, one launch (start us, length us, event | category | flops | bytes accessed | tf_op | source)
XLA Modules:
  0.0 90.9 jit_solution(14060905981778604374)
XLA Ops:
  0.0 20.6 %shard_map.100 = (bf16[3,16,128,128]{3,2,1,0:T(8,128)(2,1)}, bf16[16,128,128]{2,1,0:T(8,128)(2,1)}, bf16[16,128,128]{2,1,0:T(8,128)(2,1)}) custom-call(bf16[128,4096]{1,0:T(8,128)(2,1)} %x_hbm.3, bf16[4096,2048]{1,0:T(8,128)(2,1)} %wq_hbm.1, bf16[4096,2048]{1,0:T(8,128)(2,1)} %wk_hbm.1, bf16[4096,2048]{1,0:T(8,128)(2,1)} %wv_hbm.1), custom_call_target="tpu_custom_call" | custom-call | flops 20000000000 | bytes 50331648 | tf_op jit(solution)/shard_map/pallas_call | solution.py:141
  20.6 19.8 %shard_map.101.suf_hbm = f32[17,128,128]{2,1,0:T(8,128)} custom-call(s32[128]{0:T(128)} %lens.1, bf16[3,16,128,128]{3,2,1,0:T(8,128)(2,1)} %get-tuple-element.8.q_hbm, bf16[16,128,128]{2,1,0:T(8,128)(2,1)} %get-tuple-element.9.kn_hbm, bf16[16,128,128]{2,1,0:T(8,128)(2,1)} %get-tuple-element.10.vn_hbm, bf16[512,256,128]{2,1,0:T(8,128)(2,1)} %bitcast.2, ...), custom_call_target="tpu_custom_call" | custom-call | flops 20000000000 | bytes 67108864 | tf_op jit(solution)/shard_map/pallas_call | solution.py:524
  40.3 48.2 %shard_map.102 = bf16[128,4096]{1,0:T(8,128)(2,1)} custom-call(bf16[3,16,128,128]{3,2,1,0:T(8,128)(2,1)} %get-tuple-element.8.q_hbm, bf16[1024,16,128]{2,1,0:T(8,128)(2,1)} %kp_hbm.1, bf16[1024,16,128]{2,1,0:T(8,128)(2,1)} %vp_hbm.1, f32[17,128,128]{2,1,0:T(8,128)} %shard_map.101.suf_hbm, bf16[128,4096]{1,0:T(8,128)(2,1)} %x_hbm.3, bf16[2048,4096]{1,0:T(8,128)(2,1)} %w_hbm.1), custom_call_target="tpu_custom_call" | custom-call | flops 49999998976 | bytes 16777216 | tf_op jit(solution)/shard_map/pallas_call | solution.py:374
  88.6 2.3 %copy.12 = bf16[128,4096]{1,0:T(8,128)(2,1)} copy(bf16[128,4096]{1,0:T(8,128)(2,1)} %shard_map.102) | data formatting | bytes 2097152

commit v9 on v8

--- a/solution.py
+++ b/solution.py
@@ -235,7 +235,7 @@
         return _remote(y_ref.at[at], y_ref.at[at], y_s.at[a, j], y_r.at[a, j], tp=1 - tp)
 
     def scores(a, h, q0, q1, slot):
-        at = slice(a * rh, (a + 1) * rh)
+        at = pl.ds(pl.multiple_of(a * rh, rh), rh)
         q = jnp.concatenate([qs[q0, h, at], qs[q1, h, at]], axis=0)
         s = _dot(q, kt[h], NT)
         sb[slot] = s
@@ -254,10 +254,15 @@
         dst0[h, 0], dst0[h, 1] = o[:rh], lse[:rh]
         dst1[h, 0], dst1[h, 1] = o[rh:], lse[rh:]
 
-    def attend(a, i, q0, q1, dst0, dst1):
+    def attend(i, this, after, dst0, dst1):
+        over = (i + 1) // steps
         for u in range(group):
             h = i * group + u
-            scores(a, jnp.minimum(h + 1, heads - 1), q0, q1, (u + 1) % 4)
+            if u < group - 1:
+                scores(this[0], h + 1, this[1], this[2], (u + 1) % 4)
+            else:
+                to = [t + over * (n - t) for t, n in zip(this, after)]
+                scores(to[0], lax.rem(h + 1, heads), to[1], to[2], (u + 1) % 4)
             weigh(h, u % 4, dst0, dst1)
 
     def merge_far(a, i):
@@ -272,8 +277,8 @@
             xl[a] = jnp.where(lane == h, m + jnp.log2(t), xl[a])
         x_copy(a, i).start()
 
-    def add_peer(a):
-        for j in range(blocks):
+    def add_peer(a, js):
+        for j in js:
             p_copy(a, j).wait_recv()
             y = (keep[a, j] + pr[a, j].astype(F32)).astype(BF16)
             y_ref[a * rh:(a + 1) * rh, pl.ds(pl.multiple_of(tp * half + j * wide, wide), wide)] = y
@@ -285,28 +290,36 @@
     q_diag.wait_recv()
     for a in range(2):
         def far_step(i, c):
-            attend(a, i, 3, 2, ds.at[a], fo)
+            attend(i, (a, 3, 2), (a, 1, 0), ds.at[a], fo)
             d_copy(a, i).start()
+            if a == 1:
+                for j in range(2):
+                    @pl.when(i == 2 + j)
+                    def _():
+                        add_peer(0, [j])
 
             @pl.when(i > 0)
             def _():
                 merge_far(a, i - 1)
             return c
-        scores(a, 0, 3, 2, 0)
+        if a == 0:
+            scores(a, 0, 3, 2, 0)
         lax.fori_loop(0, steps, far_step, 0)
 
         def near_step(i, c):
-            attend(a, i, 1, 0, ns.at[a], mo)
+            attend(i, (a, 1, 0), (1, 3, 2), ns.at[a], mo)
             n_copy(a, i).start()
 
             @pl.when(i == 0)
             def _():
                 merge_far(a, steps - 1)
                 l_copy(a).start()
-                if a == 1:
-                    add_peer(0)
+            if a == 1:
+                for j in range(2):
+                    @pl.when(i == j)
+                    def _():
+                        add_peer(0, range(2 + j, blocks, 2))
             return c
-        scores(a, 0, 1, 0, 0)
         lax.fori_loop(0, steps, near_step, 0)
 
         if a == 0:
@@ -342,7 +355,7 @@
             return c
         lax.fori_loop(0, blocks, keep_block, 0)
 
-    add_peer(1)
+    add_peer(1, range(blocks))
     outs = []
     for a in range(2):
         for j in range(blocks):

time: 90.7 us -> 90.4 us (level)
  no operation moved by 1% of the time
where the time goes in v9:
time: 90.4 us; the launch traced here: 90.2 us
  Pallas kernels  87.9 us (97%)
  local copies, waits for them, and re-layouts  2.29 us (3%)
    pallas_call x1, Pallas kernels, _back(): pl.pallas_call(functools.partial(_back_kernel, scale), in_specs=[pl.Block...  47.6 us
    pallas_call x1, Pallas kernels, _front(): pl.pallas_call(_front_kernel, in_specs=[pl.BlockSpec(memory_space=pl.ANY)...  20.5 us
    pallas_call x1, Pallas kernels, _suffix(): pl.pallas_call(functools.partial(_suffix_kernel, scale), in_specs=[pl.Blo...  19.8 us
    unnamed x1, local copies, waits for them, and re-layouts  2.29 us

profile of v9, /device:TPU:0, one launch (start us, length us, event | category | flops | bytes accessed | tf_op | source)
XLA Modules:
  0.0 90.2 jit_solution(5016470129102259419)
XLA Ops:
  0.0 20.5 %shard_map.100 = (bf16[3,16,128,128]{3,2,1,0:T(8,128)(2,1)}, bf16[16,128,128]{2,1,0:T(8,128)(2,1)}, bf16[16,128,128]{2,1,0:T(8,128)(2,1)}) custom-call(bf16[128,4096]{1,0:T(8,128)(2,1)} %x_hbm.3, bf16[4096,2048]{1,0:T(8,128)(2,1)} %wq_hbm.1, bf16[4096,2048]{1,0:T(8,128)(2,1)} %wk_hbm.1, bf16[4096,2048]{1,0:T(8,128)(2,1)} %wv_hbm.1), custom_call_target="tpu_custom_call" | custom-call | flops 20000000000 | bytes 50331648 | tf_op jit(solution)/shard_map/pallas_call | solution.py:141
  20.6 19.8 %shard_map.101.suf_hbm = f32[17,128,128]{2,1,0:T(8,128)} custom-call(s32[128]{0:T(128)} %lens.1, bf16[3,16,128,128]{3,2,1,0:T(8,128)(2,1)} %get-tuple-element.8.q_hbm, bf16[16,128,128]{2,1,0:T(8,128)(2,1)} %get-tuple-element.9.kn_hbm, bf16[16,128,128]{2,1,0:T(8,128)(2,1)} %get-tuple-element.10.vn_hbm, bf16[512,256,128]{2,1,0:T(8,128)(2,1)} %bitcast.2, ...), custom_call_target="tpu_custom_call" | custom-call | flops 20000000000 | bytes 67108864 | tf_op jit(solution)/shard_map/pallas_call | solution.py:537
  40.4 47.6 %shard_map.102 = bf16[128,4096]{1,0:T(8,128)(2,1)} custom-call(bf16[3,16,128,128]{3,2,1,0:T(8,128)(2,1)} %get-tuple-element.8.q_hbm, bf16[1024,16,128]{2,1,0:T(8,128)(2,1)} %kp_hbm.1, bf16[1024,16,128]{2,1,0:T(8,128)(2,1)} %vp_hbm.1, f32[17,128,128]{2,1,0:T(8,128)} %shard_map.101.suf_hbm, bf16[128,4096]{1,0:T(8,128)(2,1)} %x_hbm.3, bf16[2048,4096]{1,0:T(8,128)(2,1)} %w_hbm.1), custom_call_target="tpu_custom_call" | custom-call | flops 49999998976 | bytes 16777216 | tf_op jit(solution)/shard_map/pallas_call | solution.py:387
  88.0 2.3 %copy.12 = bf16[128,4096]{1,0:T(8,128)(2,1)} copy(bf16[128,4096]{1,0:T(8,128)(2,1)} %shard_map.102) | data formatting | bytes 2097152

commit v10 on v9

--- a/solution.py
+++ b/solution.py
@@ -13,7 +13,7 @@
 LOG2E = 1.4426950408889634
 BATCH = 16
 SLOTS = 16
-RING = 5
+RING = 6
 CHUNK = 512
 RINGW = 6
 LIMIT = 56 * 2**20
@@ -355,9 +355,10 @@
             return c
         lax.fori_loop(0, blocks, keep_block, 0)
 
-    add_peer(1, range(blocks))
     outs = []
     for a in range(2):
+        if a == 1:
+            add_peer(1, range(blocks))
         for j in range(blocks):
             y_copy(a, j).wait_recv()
         at = pl.ds(a * rh, rh)

time: 90.4 us -> 89.6 us (level)
    pallas_call x1, Pallas kernels: 19.8 us -> 18.8 us  [_suffix(): pl.pallas_call(functools.partial(_suffix_kernel, scale), in_specs=[pl.Blo...]
where the time goes in v10:
time: 89.6 us; the launch traced here: 89.3 us
  Pallas kernels  87 us (97%)
  local copies, waits for them, and re-layouts  2.29 us (3%)
    pallas_call x1, Pallas kernels, _back(): pl.pallas_call(functools.partial(_back_kernel, scale), in_specs=[pl.Block...  47.6 us
    pallas_call x1, Pallas kernels, _front(): pl.pallas_call(_front_kernel, in_specs=[pl.BlockSpec(memory_space=pl.ANY)...  20.5 us
    pallas_call x1, Pallas kernels, _suffix(): pl.pallas_call(functools.partial(_suffix_kernel, scale), in_specs=[pl.Blo...  18.8 us
    unnamed x1, local copies, waits for them, and re-layouts  2.29 us

profile of v10, /device:TPU:0, one launch (start us, length us, event | category | flops | bytes accessed | tf_op | source)
XLA Modules:
  0.0 89.3 jit_solution(17290114809004106879)
XLA Ops:
  0.0 20.5 %shard_map.100 = (bf16[3,16,128,128]{3,2,1,0:T(8,128)(2,1)}, bf16[16,128,128]{2,1,0:T(8,128)(2,1)}, bf16[16,128,128]{2,1,0:T(8,128)(2,1)}) custom-call(bf16[128,4096]{1,0:T(8,128)(2,1)} %x_hbm.3, bf16[4096,2048]{1,0:T(8,128)(2,1)} %wq_hbm.1, bf16[4096,2048]{1,0:T(8,128)(2,1)} %wk_hbm.1, bf16[4096,2048]{1,0:T(8,128)(2,1)} %wv_hbm.1), custom_call_target="tpu_custom_call" | custom-call | flops 20000000000 | bytes 50331648 | tf_op jit(solution)/shard_map/pallas_call | solution.py:141
  20.6 18.8 %shard_map.101.suf_hbm = f32[17,128,128]{2,1,0:T(8,128)} custom-call(s32[128]{0:T(128)} %lens.1, bf16[3,16,128,128]{3,2,1,0:T(8,128)(2,1)} %get-tuple-element.8.q_hbm, bf16[16,128,128]{2,1,0:T(8,128)(2,1)} %get-tuple-element.9.kn_hbm, bf16[16,128,128]{2,1,0:T(8,128)(2,1)} %get-tuple-element.10.vn_hbm, bf16[512,256,128]{2,1,0:T(8,128)(2,1)} %bitcast.2, ...), custom_call_target="tpu_custom_call" | custom-call | flops 20000000000 | bytes 67108864 | tf_op jit(solution)/shard_map/pallas_call | solution.py:538
  39.4 47.6 %shard_map.102 = bf16[128,4096]{1,0:T(8,128)(2,1)} custom-call(bf16[3,16,128,128]{3,2,1,0:T(8,128)(2,1)} %get-tuple-element.8.q_hbm, bf16[1024,16,128]{2,1,0:T(8,128)(2,1)} %kp_hbm.1, bf16[1024,16,128]{2,1,0:T(8,128)(2,1)} %vp_hbm.1, f32[17,128,128]{2,1,0:T(8,128)} %shard_map.101.suf_hbm, bf16[128,4096]{1,0:T(8,128)(2,1)} %x_hbm.3, bf16[2048,4096]{1,0:T(8,128)(2,1)} %w_hbm.1), custom_call_target="tpu_custom_call" | custom-call | flops 49999998976 | bytes 16777216 | tf_op jit(solution)/shard_map/pallas_call | solution.py:388
  87.0 2.3 %copy.12 = bf16[128,4096]{1,0:T(8,128)(2,1)} copy(bf16[128,4096]{1,0:T(8,128)(2,1)} %shard_map.102) | data formatting | bytes 2097152
